TPU v7x, 32 devices: a whole 2x2x4 slice. The times are simulated.
32 devices in a mesh: pole: 2 (over y), prow: 4 (over z), pcol: 4 (over x, core).
Axes of the slice: x: 2, y: 2, z: 4, core: 2. Of those that a mesh axis runs over, the one named last changes fastest.
Arguments:
- ainv_anc: bfloat16 [2, 4096, 2048], P(None, ('pole', 'prow'), 'pcol'), parts along dimension 1, may hold values from -6 to 6
- panel: bfloat16 [2, 8, 1024, 256], P(None, 'pole', ('pcol', 'prow')), parts along dimension 1, may hold values from -6 to 6
- u_inv: bfloat16 [2, 8, 256, 256], P(None, 'pole'), parts along dimension 1, may hold values from -0.01171875 to 0.01171875
- k_inv: float32 [2, 8, 256, 256], P(None, ('pole', 'pcol')), parts along dimension 1, may hold values from -6 to 6
- structure: int32 [4, 4], replicated, may hold values from -1 to 7, as said below
Outputs:
- sel_inv: float32 [2, 4096, 1024], P(None, ('pole', 'prow'), 'pcol'), parts along dimension 1
- diag_inv: float32 [2, 8, 256, 256], P(None, ('pole', 'pcol')), parts along dimension 1
There are 2 independent parts, one for each index of `pole`. A program takes and returns all parts, laid end to end along the dimension named above; an argument that names none is the same for every part. Nothing has to cross between parts.
Inputs may be any that keep to these rules, and one draw needn't show every extreme that they name: `structure`: slots g * 1 to (g + 1) * 1 - 1 of row k hold distinct blocks of g * 2 to (g + 1) * 2 - 1 in rising order, followed by -1 for empty slots; each such group of each row holds at least one block, and for every g some row fills all 1 slots of group g.
All inputs are finite; a program needn't handle non-finite values.
Results may differ from a plain program's by a relative error of at most 0.005.
Values may be sent and summed in bfloat16 or wider, within the bound.
No kernel may reach another device: no remote copies, remote signals or barrier semaphores. Data moves between devices by JAX's collectives and lax.ppermute only.
A program may use at most 128 MiB of HBM per device.

v0:
```python
import jax
import jax.numpy as jnp
from jax import lax
from jax.sharding import PartitionSpec as P


def complex_quad(z_part, s_part):
    highest = lax.Precision.HIGHEST

    def single(left, right):
        return jnp.einsum("kra,rkb->kab", left, right, precision=highest)

    real = single(z_part[0], s_part[0]) - single(z_part[1], s_part[1])
    imag = single(z_part[0], s_part[1]) + single(z_part[1], s_part[0])
    return jnp.stack([real, imag])


def local(ainv_anc, panel, u_inv, k_inv, structure):
    block_width = u_inv.shape[-1]
    total_k = u_inv.shape[1]
    own_k = k_inv.shape[1]
    n_cols = lax.axis_size("pcol")
    row_here = lax.axis_index("prow")
    col_here = lax.axis_index("pcol")
    row_blocks = ainv_anc.shape[1] // block_width
    group_blocks = ainv_anc.shape[2] // block_width
    group_slots = structure.shape[1] // n_cols
    rows_all = row_blocks * block_width
    col_struct = lax.dynamic_slice_in_dim(structure, col_here * group_slots, group_slots, 1)
    slot_live = col_struct >= 0
    slot_pos = col_struct - col_here * group_blocks
    first_block = row_here * row_blocks
    target = first_block + jnp.arange(row_blocks, dtype=jnp.int32)
    rows_in = lax.all_gather(panel, "prow", axis=2, tiled=True)

    def single(left, right):
        return jnp.einsum("knb,kbc->knc", left, right, preferred_element_type=jnp.float32)

    real = single(rows_in[0], u_inv[0]) - single(rows_in[1], u_inv[1])
    imag = single(rows_in[0], u_inv[1]) + single(rows_in[1], u_inv[0])
    placed = jnp.stack([real, imag]).astype(jnp.bfloat16)
    placed = placed.reshape(2, total_k, group_slots, block_width, block_width)
    placed = jnp.where(slot_live[None, :, :, None, None], placed, jnp.zeros((), jnp.bfloat16))
    block_ids = jnp.arange(group_blocks, dtype=jnp.int32)
    pick_table = (slot_pos[:, :, None] == block_ids[None, None, :]).astype(jnp.bfloat16)
    ainv_blocks = ainv_anc.reshape(2, rows_all, group_blocks, block_width)

    def one_node(items):
        table_k, rows_k = items
        picked = jnp.einsum(
            "sg,cigw->cisw", table_k, ainv_blocks, preferred_element_type=jnp.float32
        )
        picked = picked.astype(jnp.bfloat16).reshape(2, rows_all, group_slots * block_width)
        right = rows_k.reshape(2, group_slots * block_width, block_width)
        real = jnp.dot(picked[0], right[0], preferred_element_type=jnp.float32) - jnp.dot(
            picked[1], right[1], preferred_element_type=jnp.float32
        )
        imag = jnp.dot(picked[0], right[1], preferred_element_type=jnp.float32) + jnp.dot(
            picked[1], right[0], preferred_element_type=jnp.float32
        )
        return jnp.stack([real, imag])

    per_node = lax.map(one_node, (pick_table, jnp.moveaxis(placed, 1, 0)))
    partial_value = jnp.transpose(per_node, (1, 2, 0, 3))
    row_table = (col_struct[:, None, :] == target[None, :, None]).astype(jnp.bfloat16)
    z_rows = jnp.einsum("kts,ckswb->cktwb", row_table, placed, preferred_element_type=jnp.float32)
    z_rows = z_rows.astype(jnp.bfloat16).reshape(2, total_k, rows_all, block_width)
    summed = lax.psum_scatter(
        partial_value.reshape(2, rows_all, total_k * block_width),
        "pcol",
        scatter_dimension=2,
        tiled=True,
    )
    own_struct = lax.dynamic_slice_in_dim(structure, col_here * own_k, own_k, 0)
    member = jnp.any(own_struct[:, :, None] == target[None, None, :], axis=1)
    selected = -summed.reshape(2, row_blocks, block_width, own_k, block_width)
    selected = jnp.where(member.T[None, :, None, :, None], selected, 0.0)
    sel_inv = selected.reshape(2, rows_all, own_k * block_width)
    received = lax.all_to_all(z_rows, "pcol", split_axis=1, concat_axis=1, tiled=True)
    z_own = (
        received.astype(jnp.float32).reshape(2, n_cols, own_k, rows_all, block_width).sum(axis=1)
    )
    quad_term = complex_quad(z_own, selected.reshape(2, rows_all, own_k, block_width))
    total_sum = lax.psum(quad_term, "prow")
    diag_inv = k_inv - total_sum
    return (sel_inv, diag_inv)


def solution(mesh):
    placed = (
        P(None, ("pole", "prow"), "pcol"),
        P(None, "pole", ("pcol", "prow"), None),
        P(None, "pole", None, None),
        P(None, ("pole", "pcol"), None, None),
        P(),
    )
    return jax.shard_map(
        local,
        mesh=mesh,
        in_specs=placed,
        out_specs=(P(None, ("pole", "prow"), "pcol"), P(None, ("pole", "pcol"), None, None)),
        check_vma=False,
    )
```

profile of v0, /device:TPU:0, one launch (start us, length us, event | category | flops | bytes accessed | tf_op | source)
XLA Modules:
  0.0 170.8 jit_solution(10218093751577018464)
XLA Ops:
  7.2 0.7 all-gather.2.cloned.1.call-update
  8.0 1.3 reshape.276
  9.3 0.9 compare_reduce_fusion
  10.2 0.9 dynamic-slice_reduce_fusion
  11.2 29.1 %all-gather.2.cloned.1.call-done = bf16[2,4,256,256]{3,2,1,0:T(8,128)(2,1)} async-done(((bf16[2,4,64,256]{3,2,1,0:T(8,128)(2,1)}), bf16[2,4,256,256]{3,2,1,0:T(8,128)(2,1)}) %all-gather.2.cloned.1.call-update) | async-done | bytes 1048592 | tf_op jit(solution)/shard_map/all_gather | solution.py:34
  40.3 1.6 fusion.13
  41.9 1.3 fusion.17
  43.3 0.3 fusion.9
  43.6 0.3 fusion.8
  44.1 13.4 %while.10 = (s32[]{:T(128)}, f32[4,2,512,256]{3,2,1,0:T(8,128)}, bf16[4,1,2]{2,1,0:T(2,128)(2,1)S(1)}, bf16[2,512,2,256]{3,2,1,0:T(2,128)(2,1)S(1)}, bf16[4,2,1,256,256]{4,3,0,2,1:T(8,128)(2,1)S(1)}, /*index=5*/s32[]{:T(128)}) while((s32[]{:T(128)}, f32[4,2,512,256]{3,2,1,0:T(8,128)}, bf16[4,1,2]{2,1,0:T(2,128)(2,1)S(1)}, ...), condition=%wide.region_2.3_spmd, body=%wide.region_1.2_spmd.sunk | while | flops 270008320 | bytes 9962073 | solution.py:63
  44.1 1.2 fusion.42
  45.4 0.2 fusion.45
  45.7 0.2 fusion.46
  45.9 0.2 fusion.43
  46.1 0.2 fusion.44
  46.4 1.0 fusion.47
  47.4 1.2 fusion.42
  49.0 0.2 fusion.46
  49.2 0.2 fusion.43
  49.5 0.2 fusion.44
  49.7 1.1 fusion.47
  50.8 1.2 fusion.42
  52.1 0.2 fusion.45
  52.4 0.2 fusion.46
  52.6 0.2 fusion.43
  52.8 0.2 fusion.44
  53.1 1.1 fusion.47
  54.2 1.2 fusion.42
  55.5 0.2 fusion.45
  55.7 0.2 fusion.46
  56.2 0.2 fusion.44
  56.4 1.0 fusion.47
  57.5 4.8 %copy.21 = f32[4,2,64,8,256]{4,3,0,2,1:T(8,128)} copy(f32[4,2,64,8,256]{4,3,2,1,0:T(8,128)} %bitcast.135) | data formatting | bytes 8388608 | tf_op jit(solution)/shard_map/reshape | solution.py:69
  62.5 0.5 multiply_convert_fusion
  63.0 1.5 copy.17
  64.5 3.8 %all-to-all-start = ((bf16[2,4,512,256]{3,2,0,1:T(8,128)(2,1)}), bf16[2,4,512,256]{3,2,0,1:T(8,128)(2,1)S(1)}, u32[]{:S(2)}, u32[]{:S(2)}) async-start(bf16[2,4,512,256]{3,2,0,1:T(8,128)(2,1)} %copy.17), calls=%async_computation.1 | async-start | bytes 4194304 | tf_op jit(solution)/shard_map/all_to_all | solution.py:79
  68.3 0.7 dynamic-slice_bitcast_fusion.1
  69.2 36.9 %all-to-all-done = bf16[2,4,512,256]{3,2,0,1:T(8,128)(2,1)S(1)} async-done(((bf16[2,4,512,256]{3,2,0,1:T(8,128)(2,1)}), bf16[2,4,512,256]{3,2,0,1:T(8,128)(2,1)S(1)}, u32[]{:S(2)}, u32[]{:S(2)}) %all-to-all-start) | async-done | bytes 2097184 | tf_op jit(solution)/shard_map/all_to_all | solution.py:79
  106.1 0.3 convert_reduce_fusion
  106.4 11.5 %reduce-scatter.2.cloned.1.call-done = f32[2,512,256]{2,1,0:T(8,128)} async-done(((f32[2,512,1024]{2,1,0:T(8,128)}), f32[2,512,256]{2,1,0:T(8,128)}) %reduce-scatter.2.cloned.1.call-update) | async-done | bytes 1048592 | tf_op jit(solution)/shard_map/reduce_scatter | solution.py:68
  117.9 2.3 %fusion.26 = (f32[2,512,256]{2,1,0:T(8,128)S(1)}, f32[2,512,256]{2,1,0:T(8,128)}) fusion(f32[2,512,256]{2,1,0:T(8,128)} %reduce-scatter.2.cloned.1.call-done, pred[512]{0:T(512)(128)(4,1)S(1)} %broadcast_in_dim.53), kind=kLoop, calls=%fused_computation.59 | loop fusion | flops 524288 | bytes 3146240 | tf_op jit(solution)/shard_map/neg | solution.py:76
  120.5 1.0 fusion.19
  121.5 1.0 fusion.20
  122.5 1.0 fusion.10
  123.5 1.0 fusion.11
  124.5 0.8 pad_maximum_fusion
  125.4 37.0 %all-reduce.2.cloned.1.call-done = f32[2,1,256,256]{3,2,1,0:T(8,128)} async-done(((f32[2,1,256,256]{3,2,1,0:T(8,128)}), f32[2,1,256,256]{3,2,1,0:T(8,128)}) %all-reduce.2.cloned.1.call-update) | async-done | bytes 524304 | tf_op jit(solution)/shard_map/psum | solution.py:84
  162.4 1.9 %sub.26 = f32[2,1,256,256]{3,2,1,0:T(8,128)} subtract(f32[2,1,256,256]{3,2,1,0:T(8,128)S(1)} %copy-done.2, f32[2,1,256,256]{3,2,1,0:T(8,128)} %all-reduce.2.cloned.1.call-done) | non-fusion elementwise | flops 131072 | bytes 1572864 | tf_op jit(solution)/shard_map/sub | solution.py:85
  (32 shorter events, 2.0 us)
Async XLA Ops:
  7.2 34.7 %copy-start = (bf16[2,4,256,256]{3,2,1,0:T(8,128)(2,1)S(1)}, bf16[2,4,256,256]{3,2,1,0:T(8,128)(2,1)}, u32[]{:S(2)}) copy-start(bf16[2,4,256,256]{3,2,1,0:T(8,128)(2,1)} %param.9) | copy-start | bytes 3145732
  7.2 33.1 %all-gather.2.cloned.1.call-start = ((), (), s32[]{:S(2)}) async-start(), calls=%async_computation.2 | async-start | bytes 1310720 | tf_op jit(solution)/shard_map/all_gather | solution.py:34
  7.9 110.0 %reduce-scatter.2.cloned.1.call-start = ((), (), s32[]{:S(2)}) async-start(), calls=%async_computation.3 | async-start | bytes 5242880 | tf_op jit(solution)/shard_map/reduce_scatter | solution.py:68
  40.3 3.0 %copy-start.1 = (bf16[2,4,256,256]{3,2,1,0:T(8,128)(2,1)S(1)}, bf16[2,4,256,256]{3,2,1,0:T(8,128)(2,1)}, u32[]{:S(2)}) copy-start(bf16[2,4,256,256]{3,2,1,0:T(8,128)(2,1)} %all-gather.2.cloned.1.call-done) | copy-start | bytes 3145732
  64.5 41.6 %all-to-all-start = ((bf16[2,4,512,256]{3,2,0,1:T(8,128)(2,1)}), bf16[2,4,512,256]{3,2,0,1:T(8,128)(2,1)S(1)}, u32[]{:S(2)}, u32[]{:S(2)}) async-start(bf16[2,4,512,256]{3,2,0,1:T(8,128)(2,1)} %copy.17), calls=%async_computation.1 | async-start | bytes 4194304 | tf_op jit(solution)/shard_map/all_to_all | solution.py:79
  68.2 94.1 %all-reduce.2.cloned.1.call-start = ((), (), s32[]{:S(2)}) async-start(), calls=%async_computation.4 | async-start | bytes 1048576 | tf_op jit(solution)/shard_map/psum | solution.py:84
  120.4 41.9 %copy-start.2 = (f32[2,1,256,256]{3,2,1,0:T(8,128)S(1)}, f32[2,1,256,256]{3,2,1,0:T(8,128)}, u32[]{:S(2)}) copy-start(f32[2,1,256,256]{3,2,1,0:T(8,128)} %param.10) | copy-start | bytes 1572868
Sparse Core Ops, SparseCore 0:
  9.6 30.6 all-gather.1
  62.4 55.4 reduce-scatter.1
  125.5 36.8 all-reduce.1
where the time goes:
time: 171 us
  waiting for transfers between devices  115 us (67%)
  matrix products  16.1 us (9%)
  between operations  13.9 us (8%)
  other arithmetic  12.6 us (7%)
  local copies, waits for them, and re-layouts  8.88 us (5%)
  starting transfers between devices  3.88 us (2%)
    psum x1, waiting for transfers between devices, local(): total_sum = lax.psum(quad_term, 'prow')  37 us
    all_to_all x1, waiting for transfers between devices, local(): lax.all_to_all(z_rows, 'pcol', split_axis=1, concat_axis=1, tiled=True)  36.9 us
    all_gather x1, waiting for transfers between devices, local(): rows_in = lax.all_gather(panel, 'prow', axis=2, tiled=True)  29.1 us
    reduce_scatter x1, waiting for transfers between devices, local(): lax.psum_scatter(partial_value.reshape(2, rows_all, total_k * block_width...  11.5 us
    dot_general x4, matrix products, one_node(): jnp.einsum('sg,cigw->cisw', table_k, ainv_blocks, preferred_element_type=...  4.94 us
    reshape x1, local copies, waits for them, and re-layouts, local(): partial_value.reshape(2, rows_all, total_k * block_width)  4.76 us
    dynamic_update_slice x4, other arithmetic, local(): per_node = lax.map(one_node, (pick_table, jnp.moveaxis(placed, 1, 0)))  4.27 us
    dot_general x4, matrix products, single(): return jnp.einsum('kra,rkb->kab', left, right, precision=highest)  4.02 us
  transfers between devices with their start and end apart: 4, of which 4 were waited for; matrix products, arithmetic and copies ran while one was open for 4% of the time, Pallas kernels for 0%

commit v1 on v0

v1 whole, which is shorter than its diff:
```python
import jax
import jax.numpy as jnp
from jax import lax
from jax.experimental import pallas as pl
from jax.experimental.pallas import tpu as pltpu
from jax.sharding import PartitionSpec as P

BF16 = jnp.bfloat16
F32 = jnp.float32
ANY = pl.BlockSpec(memory_space=pl.ANY)
VMEM = pl.BlockSpec(memory_space=pltpu.VMEM)
SMEM = pl.BlockSpec(memory_space=pltpu.SMEM)


def swap(x, axis, d):
    n = lax.axis_size(axis)
    return lax.ppermute(x, axis, [(i, i ^ d) for i in range(n)])


def run_copies(copies):
    for copy in copies:
        copy.start()
    for copy in copies:
        copy.wait()


def pick_panel(panel, own_k):
    n_cols = lax.axis_size("pcol")
    planes, _, rows, width = panel.shape

    def kernel(panel_ref, *refs):
        outs, sems = refs[:n_cols], refs[n_cols]
        col = lax.axis_index("pcol")
        run_copies(
            [
                pltpu.make_async_copy(
                    panel_ref.at[:, pl.ds((col ^ d) * own_k, own_k)], outs[d], sems.at[d]
                )
                for d in range(n_cols)
            ]
        )

    return pl.pallas_call(
        kernel,
        name="pick_panel",
        in_specs=[ANY],
        out_specs=[ANY] * n_cols,
        out_shape=[jax.ShapeDtypeStruct((planes, own_k, rows, width), panel.dtype)] * n_cols,
        scratch_shapes=[pltpu.SemaphoreType.DMA((n_cols,))],
    )(panel)


class Rows:
    def __init__(self, row_blocks, group_blocks, group_slots):
        self.row_blocks, self.group_blocks, self.group_slots = row_blocks, group_blocks, group_slots
        nested = row_blocks % group_blocks == 0 or group_blocks % row_blocks == 0
        slots = max(row_blocks // group_blocks, 1) * group_slots
        self.by_slot = nested and slots < row_blocks
        self.count = slots if self.by_slot else row_blocks

    def entry(self, struct_ref, node, row, index):
        base = row * self.row_blocks
        if self.by_slot:
            slot = (base // self.group_blocks) * self.group_slots + index
            block = struct_ref[node, slot] - base
            live = jnp.logical_and(block >= 0, block < self.row_blocks)
            return jnp.where(live, block, 0), live, slot // self.group_slots, slot % self.group_slots
        target = base + index
        group = target // self.group_blocks
        found, live = jnp.int32(0), jnp.int32(0)
        for s in range(self.group_slots):
            hit = struct_ref[node, group * self.group_slots + s] == target
            found = jnp.where(hit, s, found)
            live = jnp.where(hit, 1, live)
        return jnp.int32(index), live > 0, group, found


def pick_ainv(ainv, u_inv, structure, own_k, rows):
    n_cols = lax.axis_size("pcol")
    width = u_inv.shape[-1]
    slots = rows.group_slots

    def kernel(struct_ref, ainv_ref, u_ref, *refs):
        outs, u_out, sems, u_sem = refs[:n_cols], refs[n_cols], refs[n_cols + 1], refs[n_cols + 2]
        col, row = lax.axis_index("pcol"), lax.axis_index("prow")
        copies = [pltpu.make_async_copy(u_ref.at[:, pl.ds(col * own_k, own_k)], u_out, u_sem)]
        for d in range(n_cols):
            for kk in range(own_k):
                node = (col ^ d) * own_k + kk
                for i in range(rows.count):
                    block, _, _, _ = rows.entry(struct_ref, node, row, i)
                    for s in range(slots):
                        j = struct_ref[node, col * slots + s] - col * rows.group_blocks
                        j = jnp.maximum(j, 0)
                        copies.append(
                            pltpu.make_async_copy(
                                ainv_ref.at[:, pl.ds(block * width, width), pl.ds(j * width, width)],
                                outs[d].at[:, kk, pl.ds(i * width, width), pl.ds(s * width, width)],
                                sems.at[d, kk, i, s],
                            )
                        )
        run_copies(copies)

    shape = jax.ShapeDtypeStruct((2, own_k, rows.count * width, slots * width), ainv.dtype)
    out = pl.pallas_call(
        kernel,
        name="pick_ainv",
        in_specs=[SMEM, ANY, ANY],
        out_specs=[ANY] * (n_cols + 1),
        out_shape=[shape] * n_cols + [jax.ShapeDtypeStruct((2, own_k, width, width), u_inv.dtype)],
        scratch_shapes=[
            pltpu.SemaphoreType.DMA((n_cols, own_k, rows.count, slots)),
            pltpu.SemaphoreType.DMA,
        ],
    )(structure, ainv, u_inv)
    return out[:n_cols], out[n_cols]


def dot(left, right):
    return jnp.dot(left, right, preferred_element_type=F32)


def tdot(left, right):
    return lax.dot_general(left, right, (((0,), (0,)), ((), ())), preferred_element_type=F32)


def solve(structure, own, rest, ainv, u_own, rows):
    n_rows, n_cols = lax.axis_size("prow"), lax.axis_size("pcol")
    _, own_k, part, width = own[0].shape
    slots = rows.group_slots
    sub = min(part, width)
    band = width // n_rows

    def kernel(struct_ref, u_ref, *refs):
        own_refs, refs = refs[:n_rows], refs[n_rows:]
        rest_refs, refs = refs[:n_rows], refs[n_rows:]
        ainv_refs, refs = refs[:n_cols], refs[n_cols:]
        sel_ref, q_refs, (scaled, quad) = refs[0], refs[1 : 1 + n_rows], refs[1 + n_rows :]
        col, row = lax.axis_index("pcol"), lax.axis_index("prow")
        if rows.by_slot:
            sel_ref[...] = jnp.zeros_like(sel_ref)
        for kk in range(own_k):
            node = col * own_k + kk
            u_real, u_imag = u_ref[0, kk], u_ref[1, kk]
            for dz in range(n_rows):
                first = (row ^ dz) * part
                for real, imag, dxs in (
                    (own_refs[dz][0, kk], own_refs[dz][1, kk], (0,)),
                    (
                        rest_refs[dz][:, 0, kk].reshape((n_cols - 1) * part, width),
                        rest_refs[dz][:, 1, kk].reshape((n_cols - 1) * part, width),
                        tuple(range(1, n_cols)),
                    ),
                ):
                    s_real = dot(real, u_real) - dot(imag, u_imag)
                    s_imag = dot(real, u_imag) + dot(imag, u_real)
                    for n, dx in enumerate(dxs):
                        for o in range(0, part, sub):
                            slot = (first + o) // width
                            live = struct_ref[node, (col ^ dx) * slots + slot] >= 0
                            at = pl.ds(pl.multiple_of(first + o, sub), sub)
                            for plane, value in ((0, s_real), (1, s_imag)):
                                piece = value[n * part + o : n * part + o + sub]
                                scaled[plane, kk, dx, at, :] = jnp.where(live, piece, 0.0).astype(BF16)
            q_real = jnp.zeros((width, width), F32)
            q_imag = jnp.zeros((width, width), F32)
            for i in range(rows.count):
                block, live, group, slot = rows.entry(struct_ref, node, row, i)
                here = slice(i * width, (i + 1) * width)
                acc_real = jnp.zeros((width, width), F32)
                acc_imag = jnp.zeros((width, width), F32)
                for dx in range(n_cols):
                    a_real, a_imag = ainv_refs[dx][0, kk, here, :], ainv_refs[dx][1, kk, here, :]
                    s_real, s_imag = scaled[0, kk, dx], scaled[1, kk, dx]
                    acc_real += dot(a_real, s_real) - dot(a_imag, s_imag)
                    acc_imag += dot(a_real, s_imag) + dot(a_imag, s_real)
                sel_real = jnp.where(live, -acc_real, 0.0)
                sel_imag = jnp.where(live, -acc_imag, 0.0)

                def put(block=block, sel_real=sel_real, sel_imag=sel_imag, kk=kk):
                    at = pl.ds(pl.multiple_of(block * width, width), width)
                    sel_ref[0, at, kk * width : (kk + 1) * width] = sel_real
                    sel_ref[1, at, kk * width : (kk + 1) * width] = sel_imag

                if rows.by_slot:
                    pl.when(live)(put)
                else:
                    put()
                at = pl.ds(pl.multiple_of(slot * width, width), width)
                left_real, left_imag = scaled[0, kk, group ^ col, at, :], scaled[1, kk, group ^ col, at, :]
                hi_real, hi_imag = sel_real.astype(BF16), sel_imag.astype(BF16)
                lo_real = (sel_real - hi_real.astype(F32)).astype(BF16)
                lo_imag = (sel_imag - hi_imag.astype(F32)).astype(BF16)
                right = jnp.concatenate([hi_real, hi_imag, lo_real, lo_imag], axis=1)
                by_real, by_imag = tdot(left_real, right), tdot(left_imag, right)
                by_real = by_real[:, : 2 * width] + by_real[:, 2 * width :]
                by_imag = by_imag[:, : 2 * width] + by_imag[:, 2 * width :]
                q_real += by_real[:, :width] - by_imag[:, width:]
                q_imag += by_real[:, width:] + by_imag[:, :width]
            quad[0], quad[1] = q_real, q_imag
            for dz in range(n_rows):
                at = pl.ds(pl.multiple_of((row ^ dz) * band, band), band)
                for plane in range(2):
                    q_refs[dz][plane, kk] = quad[plane, at, :].astype(q_refs[dz].dtype)

    chunk = (2, own_k, band, width)
    out = pl.pallas_call(
        kernel,
        name="solve",
        in_specs=[SMEM] + [VMEM] * (1 + 2 * n_rows + n_cols),
        out_specs=[VMEM] * (1 + n_rows),
        out_shape=[
            jax.ShapeDtypeStruct((2, rows.row_blocks * width, own_k * width), F32),
            jax.ShapeDtypeStruct(chunk, F32),
        ]
        + [jax.ShapeDtypeStruct(chunk, BF16)] * (n_rows - 1),
        scratch_shapes=[
            pltpu.VMEM((2, own_k, n_cols, slots * width, width), BF16),
            pltpu.VMEM((2, width, width), F32),
        ],
    )(structure, u_own, *own, *rest, *ainv)
    return out[0], out[1:]


def finish_band(k_inv, terms):
    def kernel(k_ref, *refs):
        *term_refs, out_ref = refs
        row = lax.axis_index("prow")
        band = out_ref.shape[2]
        total = term_refs[0][...]
        for ref in term_refs[1:]:
            total += ref[...].astype(F32)
        at = pl.ds(pl.multiple_of(row * band, band), band)
        out_ref[...] = (k_ref[:, :, at, :] - total).astype(BF16)

    return pl.pallas_call(
        kernel,
        name="finish_band",
        in_specs=[VMEM] * (1 + len(terms)),
        out_specs=VMEM,
        out_shape=jax.ShapeDtypeStruct(terms[0].shape, BF16),
    )(k_inv, *terms)


def join_bands(bands, shape):
    def kernel(*refs):
        *band_refs, out_ref = refs
        row = lax.axis_index("prow")
        band = band_refs[0].shape[2]
        for d, ref in enumerate(band_refs):
            at = pl.ds(pl.multiple_of((row ^ d) * band, band), band)
            out_ref[:, :, at, :] = ref[...].astype(F32)

    return pl.pallas_call(
        kernel,
        name="join_bands",
        in_specs=[VMEM] * len(bands),
        out_specs=VMEM,
        out_shape=jax.ShapeDtypeStruct(shape, F32),
    )(*bands)


def gather_rows(x):
    n = lax.axis_size("prow")
    held = {0: x}
    d = n // 2
    while d:
        held.update({at ^ d: swap(value, "prow", d) for at, value in list(held.items())})
        d //= 2
    return [held[d] for d in range(n)]


def local(ainv_anc, panel, u_inv, k_inv, structure):
    width = u_inv.shape[-1]
    own_k = k_inv.shape[1]
    n_rows, n_cols = lax.axis_size("prow"), lax.axis_size("pcol")
    rows = Rows(ainv_anc.shape[1] // width, ainv_anc.shape[2] // width, structure.shape[1] // n_cols)
    parts = pick_panel(panel, own_k)
    own = gather_rows(parts[0])
    got = [swap(parts[d], "pcol", d) for d in range(1, n_cols)]
    rest = gather_rows(jnp.stack(got))
    blocks, u_own = pick_ainv(ainv_anc, u_inv, structure, own_k, rows)
    ainv = [blocks[0]] + [swap(blocks[d], "pcol", d) for d in range(1, n_cols)]
    sel_inv, terms = solve(structure, own, rest, ainv, u_own, rows)
    terms = [terms[0]] + [swap(terms[d], "prow", d) for d in range(1, n_rows)]
    mine = finish_band(k_inv, terms)
    bands = [mine] + [swap(mine, "prow", d) for d in range(1, n_rows)]
    return sel_inv, join_bands(bands, k_inv.shape)


def solution(mesh):
    placed = (
        P(None, ("pole", "prow"), "pcol"),
        P(None, "pole", ("pcol", "prow"), None),
        P(None, "pole", None, None),
        P(None, ("pole", "pcol"), None, None),
        P(),
    )
    return jax.shard_map(
        local,
        mesh=mesh,
        in_specs=placed,
        out_specs=(P(None, ("pole", "prow"), "pcol"), P(None, ("pole", "pcol"), None, None)),
        check_vma=False,
    )
```

time: 171 us -> 108 us (0.63)
  waiting for transfers between devices: 115 us -> 24 us
  Pallas kernels: 0 us -> 59.1 us
  starting transfers between devices: 3.88 us -> 21.1 us
  matrix products: 16.1 us -> 0 us
  between operations: 13.9 us -> 0.77 us
  other arithmetic: 12.6 us -> 0.02 us
  local copies, waits for them, and re-layouts: 8.88 us -> 2.52 us
    pallas_call x0 -> x5, Pallas kernels: none -> 59.1 us  [the longest x1 41.6 us: pick_ainv(): pl.pallas_call(kernel, name='pick_ainv', in_specs=[SMEM, ANY, ANY], out_s...]
    psum x1 -> x0, waiting for transfers between devices: 37 us -> none  [local(): total_sum = lax.psum(quad_term, 'prow')]
    all_to_all x1 -> x0, waiting for transfers between devices: 36.9 us -> none  [local(): lax.all_to_all(z_rows, 'pcol', split_axis=1, concat_axis=1, tiled=True)]
    all_gather x1 -> x0, waiting for transfers between devices: 29.1 us -> none  [local(): rows_in = lax.all_gather(panel, 'prow', axis=2, tiled=True)]
    ppermute x0 -> x18, waiting for transfers between devices: none -> 24 us  [swap(): return lax.ppermute(x, axis, [(i, i ^ d) for i in range(n)])]
    ppermute x0 -> x18, starting transfers between devices: none -> 21.1 us  [swap(): return lax.ppermute(x, axis, [(i, i ^ d) for i in range(n)])]
    dot_general x28 -> x0, matrix products: 16.1 us -> none  [the longest x4 4.94 us: one_node(): jnp.einsum('sg,cigw->cisw', table_k, ainv_blocks, preferred_element_type=...]
    reduce_scatter x1 -> x0, waiting for transfers between devices: 11.5 us -> none  [local(): lax.psum_scatter(partial_value.reshape(2, rows_all, total_k * block_width...]
  transfers between devices with their start and end apart: 4 -> 18, of which waited for: 4 -> 10; matrix products, arithmetic and copies ran while one was open for 4% -> 0% of each run, Pallas kernels for 0% -> 39%
where the time goes in v1:
time: 108 us
  Pallas kernels  59.1 us (55%)
  waiting for transfers between devices  24 us (22%)
  starting transfers between devices  21.1 us (20%)
  local copies, waits for them, and re-layouts  2.52 us (2%)
    pallas_call x1, Pallas kernels, pick_ainv(): pl.pallas_call(kernel, name='pick_ainv', in_specs=[SMEM, ANY, ANY], out_s...  41.6 us
    ppermute x18, waiting for transfers between devices, swap(): return lax.ppermute(x, axis, [(i, i ^ d) for i in range(n)])  24 us
    ppermute x18, starting transfers between devices, swap(): return lax.ppermute(x, axis, [(i, i ^ d) for i in range(n)])  21.1 us
    pallas_call x1, Pallas kernels, pick_panel(): pl.pallas_call(kernel, name='pick_panel', in_specs=[ANY], out_specs=[ANY]...  9.08 us
    pallas_call x1, Pallas kernels, solve(): pl.pallas_call(kernel, name='solve', in_specs=[SMEM] + [VMEM] * (1 + 2 *...  4.91 us
    unnamed x34, local copies, waits for them, and re-layouts  2.52 us
  transfers between devices with their start and end apart: 18, of which 10 were waited for; matrix products, arithmetic and copies ran while one was open for 0% of the time, Pallas kernels for 39%

profile of v1, /device:TPU:0, one launch (start us, length us, event | category | flops | bytes accessed | tf_op | source)
XLA Modules:
  0.0 107.5 jit_solution(2564040228043913520)
XLA Ops:
  0.6 9.1 %pick_panel.1 = (bf16[2,1,64,256]{3,2,1,0:T(8,128)(2,1)}, bf16[2,1,64,256]{3,2,1,0:T(8,128)(2,1)}, bf16[2,1,64,256]{3,2,1,0:T(8,128)(2,1)}, bf16[2,1,64,256]{3,2,1,0:T(8,128)(2,1)}) custom-call(bf16[2,4,64,256]{3,2,1,0:T(8,128)(2,1)} %panel_ref.1), custom_call_target="tpu_custom_call" | custom-call | tf_op jit(solution)/shard_map/pick_panel/pallas_call | solution.py:43
  9.7 3.0 %collective-permute-start.4 = (bf16[2,1,64,256]{3,2,0,1:T(8,128)(2,1)}, bf16[2,1,64,256]{3,2,0,1:T(8,128)(2,1)S(1)}, u32[]{:S(2)}, u32[]{:S(2)}) collective-permute-start(bf16[2,1,64,256]{3,2,0,1:T(8,128)(2,1)} %bitcast.11), channel_id=1, source_target_pairs={{0,2},{1,3},{2,0},{3,1},{4,6},{5,7},{6,4},{7,5},{8,10},{9,11},{10,... | collective-permute-start | bytes 196616 | tf_op jit(solution)/shard_map/ppermute | solution.py:17
  12.8 0.0 collective-permute-start.3
  12.8 0.2 collective-permute-start.5
  12.9 2.4 %collective-permute-done.4 = bf16[2,1,64,256]{3,2,0,1:T(8,128)(2,1)S(1)} collective-permute-done((bf16[2,1,64,256]{3,2,0,1:T(8,128)(2,1)}, bf16[2,1,64,256]{3,2,0,1:T(8,128)(2,1)S(1)}, u32[]{:S(2)}, u32[]{:S(2)}) %collective-permute-start.4) | collective-permute-done | bytes 65568 | tf_op jit(solution)/shard_map/ppermute | solution.py:17
  15.4 0.0 collective-permute-done.3
  15.4 1.3 %collective-permute-done.5 = bf16[2,1,64,256]{3,2,0,1:T(8,128)(2,1)S(1)} collective-permute-done((bf16[2,1,64,256]{3,2,0,1:T(8,128)(2,1)}, bf16[2,1,64,256]{3,2,0,1:T(8,128)(2,1)S(1)}, u32[]{:S(2)}, u32[]{:S(2)}) %collective-permute-start.5) | collective-permute-done | bytes 65568 | tf_op jit(solution)/shard_map/ppermute | solution.py:17
  16.7 0.0 copy-start
  16.7 2.7 %collective-permute-start.7 = (bf16[3,2,1,64,256]{4,3,2,1,0:T(8,128)(2,1)S(1)}, bf16[3,2,1,64,256]{4,3,2,1,0:T(8,128)(2,1)S(1)}, u32[]{:S(2)}, u32[]{:S(2)}) collective-permute-start(bf16[3,2,1,64,256]{4,3,2,1,0:T(8,128)(2,1)S(1)} %pad_maximum_fusion.refs_4_), channel_id=1, source_target_pairs={{0,8},{4,12},{8,0},{12,4},{1,9},{5,13},{9,1},{13,5},{2,10},{6,14},... | collective-permute-start | bytes 589832 | tf_op jit(solution)/shard_map/ppermute | solution.py:17
  19.4 0.0 copy-done.10
  19.4 0.7 collective-permute-start.1
  20.1 1.6 %collective-permute-start = (bf16[2,1,64,256]{3,2,1,0:T(8,128)(2,1)S(1)}, bf16[2,1,64,256]{3,2,1,0:T(8,128)(2,1)S(1)}, u32[]{:S(2)}, u32[]{:S(2)}) collective-permute-start(bf16[2,1,64,256]{3,2,1,0:T(8,128)(2,1)S(1)} %copy-done.10), channel_id=1, source_target_pairs={{0,4},{4,0},{8,12},{12,8},{1,5},{5,1},{9,13},{13,9},{2,6},{6,2},{1... | collective-permute-start | bytes 196616 | tf_op jit(solution)/shard_map/ppermute | solution.py:17
  21.7 41.6 %pick_ainv.1 = (bf16[2,1,256,256]{3,2,1,0:T(8,128)(2,1)}, bf16[2,1,256,256]{3,2,1,0:T(8,128)(2,1)}, bf16[2,1,256,256]{3,2,1,0:T(8,128)(2,1)}, bf16[2,1,256,256]{3,2,1,0:T(8,128)(2,1)}, bf16[2,1,256,256]{3,2,1,0:T(8,128)(2,1)}) custom-call(s32[4,4]{1,0:T(4,128)} %struct_ref.3, bf16[2,512,512]{2,1,0:T(8,128)(2,1)} %ainv_ref.1, bf16[2,4,256,256]{3,2,1,0:T(8,128)(2,1)} %u_ref.1), custom_call_target="tpu_custom_call" | custom-call | tf_op jit(solution)/shard_map/pick_ainv/pallas_call | solution.py:105
  63.2 0.1 collective-permute-start.9
  63.3 0.0 collective-permute-done.1.refs_2_
  63.3 0.5 collective-permute-start.2
  63.9 1.2 %collective-permute-start.10 = (bf16[2,1,256,256]{3,2,1,0:T(8,128)(2,1)}, bf16[2,1,256,256]{3,2,1,0:T(8,128)(2,1)S(1)}, u32[]{:S(2)}, u32[]{:S(2)}) collective-permute-start(bf16[2,1,256,256]{3,2,1,0:T(8,128)(2,1)} %get-tuple-element.23), channel_id=1, source_target_pairs={{0,2},{1,3},{2,0},{3,1},{4,6},{5,7},{6,4},{7,5},{8,10},{9,11},{10,... | collective-permute-start | bytes 786440 | tf_op jit(solution)/shard_map/ppermute | solution.py:17
  65.1 0.0 collective-permute-done.refs_1_
  65.1 0.3 collective-permute-start.11
  65.4 2.5 %collective-permute-done.2.refs_3_ = bf16[2,1,64,256]{3,2,1,0:T(8,128)(2,1)S(1)} collective-permute-done((bf16[2,1,64,256]{3,2,1,0:T(8,128)(2,1)S(1)}, bf16[2,1,64,256]{3,2,1,0:T(8,128)(2,1)S(1)}, u32[]{:S(2)}, u32[]{:S(2)}) %collective-permute-start.2) | collective-permute-done | bytes 65568 | tf_op jit(solution)/shard_map/ppermute | solution.py:17
  67.8 0.5 collective-permute-start.6
  68.3 0.0 collective-permute-done.7.refs_6_
  68.3 1.6 %collective-permute-start.8 = (bf16[3,2,1,64,256]{4,3,2,1,0:T(8,128)(2,1)S(1)}, bf16[3,2,1,64,256]{4,3,2,1,0:T(8,128)(2,1)S(1)}, u32[]{:S(2)}, u32[]{:S(2)}) collective-permute-start(bf16[3,2,1,64,256]{4,3,2,1,0:T(8,128)(2,1)S(1)} %collective-permute-done.7.refs_6_), channel_id=1, source_target_pairs={{0,4},{4,0},{8,12},{12,8},{1,5},{5,1},{9,13},{13,9},{2,6},{6,2},{1... | collective-permute-start | bytes 589832 | tf_op jit(solution)/shard_map/ppermute | solution.py:17
  69.9 5.7 %collective-permute-done.6.refs_5_ = bf16[3,2,1,64,256]{4,3,2,1,0:T(8,128)(2,1)S(1)} collective-permute-done((bf16[3,2,1,64,256]{4,3,2,1,0:T(8,128)(2,1)S(1)}, bf16[3,2,1,64,256]{4,3,2,1,0:T(8,128)(2,1)S(1)}, u32[]{:S(2)}, u32[]{:S(2)}) %collective-permute-start.6) | collective-permute-done | bytes 196640 | tf_op jit(solution)/shard_map/ppermute | solution.py:17
  75.6 0.0 collective-permute-done.9.refs_9_
  75.6 0.0 collective-permute-done.10.refs_10_
  75.6 1.6 %collective-permute-done.11.refs_11_ = bf16[2,1,256,256]{3,2,1,0:T(8,128)(2,1)S(1)} collective-permute-done((bf16[2,1,256,256]{3,2,1,0:T(8,128)(2,1)}, bf16[2,1,256,256]{3,2,1,0:T(8,128)(2,1)S(1)}, u32[]{:S(2)}, u32[]{:S(2)}) %collective-permute-start.11) | collective-permute-done | bytes 262176 | tf_op jit(solution)/shard_map/ppermute | solution.py:17
  77.2 1.2 %collective-permute-done.8.refs_7_ = bf16[3,2,1,64,256]{4,3,2,1,0:T(8,128)(2,1)S(1)} collective-permute-done((bf16[3,2,1,64,256]{4,3,2,1,0:T(8,128)(2,1)S(1)}, bf16[3,2,1,64,256]{4,3,2,1,0:T(8,128)(2,1)S(1)}, u32[]{:S(2)}, u32[]{:S(2)}) %collective-permute-start.8) | collective-permute-done | bytes 196640 | tf_op jit(solution)/shard_map/ppermute | solution.py:17
  78.5 0.6 copy-done.6
  79.1 4.9 %solve.1 = (f32[2,512,256]{2,1,0:T(8,128)}, f32[2,1,64,256]{3,2,1,0:T(8,128)}, bf16[2,1,64,256]{3,2,1,0:T(8,128)(2,1)}, bf16[2,1,64,256]{3,2,1,0:T(8,128)(2,1)}, bf16[2,1,64,256]{3,2,1,0:T(8,128)(2,1)}) custom-call(s32[4,4]{1,0:T(4,128)} %struct_ref.3, bf16[2,1,256,256]{3,2,1,0:T(8,128)(2,1)} %get-tuple-element.16.u_ref, ...), custom_call_target="tpu_custom_call" | custom-call | tf_op jit(solution)/shard_map/solve/pallas_call | solution.py:207
  84.0 0.5 collective-permute-start.12
  84.4 2.2 %collective-permute-start.13 = (bf16[2,1,64,256]{3,2,1,0:T(8,128)(2,1)}, bf16[2,1,64,256]{3,2,1,0:T(8,128)(2,1)S(1)}, u32[]{:S(2)}, u32[]{:S(2)}) collective-permute-start(bf16[2,1,64,256]{3,2,1,0:T(8,128)(2,1)} %get-tuple-element.28), channel_id=1, source_target_pairs={{0,8},{4,12},{8,0},{12,4},{1,9},{5,13},{9,1},{13,5},{2,10},{6,14},... | collective-permute-start | bytes 196616 | tf_op jit(solution)/shard_map/ppermute | solution.py:17
  86.6 1.7 %collective-permute-start.14 = (bf16[2,1,64,256]{3,2,1,0:T(8,128)(2,1)}, bf16[2,1,64,256]{3,2,1,0:T(8,128)(2,1)S(1)}, u32[]{:S(2)}, u32[]{:S(2)}) collective-permute-start(bf16[2,1,64,256]{3,2,1,0:T(8,128)(2,1)} %get-tuple-element.29), channel_id=1, source_target_pairs={{0,12},{4,8},{8,4},{12,0},{1,13},{5,9},{9,5},{13,1},{2,14},{6,10},... | collective-permute-start | bytes 196616 | tf_op jit(solution)/shard_map/ppermute | solution.py:17
  88.4 0.1 collective-permute-done.12.refs_1_
  88.5 4.8 %collective-permute-done.13.refs_2_ = bf16[2,1,64,256]{3,2,1,0:T(8,128)(2,1)S(1)} collective-permute-done((bf16[2,1,64,256]{3,2,1,0:T(8,128)(2,1)}, bf16[2,1,64,256]{3,2,1,0:T(8,128)(2,1)S(1)}, u32[]{:S(2)}, u32[]{:S(2)}) %collective-permute-start.13) | collective-permute-done | bytes 65568 | tf_op jit(solution)/shard_map/ppermute | solution.py:17
  93.3 0.0 collective-permute-done.14.refs_3_
  93.3 0.6 copy-done.8
  93.9 0.0 copy-done.9
  93.9 1.8 %finish_band.1.refs_0_ = bf16[2,1,64,256]{3,2,1,0:T(8,128)(2,1)} custom-call(f32[2,1,256,256]{3,2,1,0:T(8,128)} %k_ref.1, f32[2,1,64,256]{3,2,1,0:T(8,128)} %get-tuple-element.26.refs_0_, bf16[2,1,64,256]{3,2,1,0:T(8,128)(2,1)} %copy-done.7, bf16[2,1,64,256]{3,2,1,0:T(8,128)(2,1)} %copy-done.8, bf16[2,1,64,256]{3,2,1,0:T(8,128)(2,1)} %copy-done.9), custom_call_target="tpu_custom_call" | custom-call | tf_op jit(solution)/shard_map/finish_band/pallas_call | solution.py:236
  95.7 2.6 %collective-permute-start.17 = (bf16[2,1,64,256]{3,2,1,0:T(8,128)(2,1)}, bf16[2,1,64,256]{3,2,1,0:T(8,128)(2,1)S(1)}, u32[]{:S(2)}, u32[]{:S(2)}) collective-permute-start(bf16[2,1,64,256]{3,2,1,0:T(8,128)(2,1)} %finish_band.1.refs_0_), channel_id=1, source_target_pairs={{0,12},{4,8},{8,4},{12,0},{1,13},{5,9},{9,5},{13,1},{2,14},{6,10},... | collective-permute-start | bytes 196616 | tf_op jit(solution)/shard_map/ppermute | solution.py:17
  98.3 0.3 collective-permute-start.16
  98.6 1.5 %collective-permute-start.15 = (bf16[2,1,64,256]{3,2,1,0:T(8,128)(2,1)}, bf16[2,1,64,256]{3,2,1,0:T(8,128)(2,1)S(1)}, u32[]{:S(2)}, u32[]{:S(2)}) collective-permute-start(bf16[2,1,64,256]{3,2,1,0:T(8,128)(2,1)} %finish_band.1.refs_0_), channel_id=1, source_target_pairs={{0,4},{4,0},{8,12},{12,8},{1,5},{5,1},{9,13},{13,9},{2,6},{6,2},{1... | collective-permute-start | bytes 196616 | tf_op jit(solution)/shard_map/ppermute | solution.py:17
  100.1 2.5 %collective-permute-done.17.refs_3_ = bf16[2,1,64,256]{3,2,1,0:T(8,128)(2,1)S(1)} collective-permute-done((bf16[2,1,64,256]{3,2,1,0:T(8,128)(2,1)}, bf16[2,1,64,256]{3,2,1,0:T(8,128)(2,1)S(1)}, u32[]{:S(2)}, u32[]{:S(2)}) %collective-permute-start.17) | collective-permute-done | bytes 65568 | tf_op jit(solution)/shard_map/ppermute | solution.py:17
  102.6 1.9 %collective-permute-done.16.refs_2_ = bf16[2,1,64,256]{3,2,1,0:T(8,128)(2,1)S(1)} collective-permute-done((bf16[2,1,64,256]{3,2,1,0:T(8,128)(2,1)}, bf16[2,1,64,256]{3,2,1,0:T(8,128)(2,1)S(1)}, u32[]{:S(2)}, u32[]{:S(2)}) %collective-permute-start.16) | collective-permute-done | bytes 65568 | tf_op jit(solution)/shard_map/ppermute | solution.py:17
  104.5 0.0 collective-permute-done.15.refs_1_
  104.5 0.6 copy-done.15
  105.1 0.6 copy-done.16
  105.8 1.8 %join_bands.1 = f32[2,1,256,256]{3,2,1,0:T(8,128)} custom-call(bf16[2,1,64,256]{3,2,1,0:T(8,128)(2,1)} %finish_band.1.refs_0_, bf16[2,1,64,256]{3,2,1,0:T(8,128)(2,1)} %copy-done.16, bf16[2,1,64,256]{3,2,1,0:T(8,128)(2,1)} %copy-done.15, bf16[2,1,64,256]{3,2,1,0:T(8,128)(2,1)} %copy-done.14), custom_call_target="tpu_custom_call" | custom-call | tf_op jit(solution)/shard_map/join_bands/pallas_call | solution.py:254
  (28 shorter events, 0.1 us)
Async XLA Ops:
  9.7 5.7 %collective-permute-start.4 = (bf16[2,1,64,256]{3,2,0,1:T(8,128)(2,1)}, bf16[2,1,64,256]{3,2,0,1:T(8,128)(2,1)S(1)}, u32[]{:S(2)}, u32[]{:S(2)}) collective-permute-start(bf16[2,1,64,256]{3,2,0,1:T(8,128)(2,1)} %bitcast.11), channel_id=1, source_target_pairs={{0,2},{1,3},{2,0},{3,1},{4,6},{5,7},{6,4},{7,5},{8,10},{9,11},{10,... | collective-permute-start | bytes 196616 | tf_op jit(solution)/shard_map/ppermute | solution.py:17
  12.8 2.6 %collective-permute-start.3 = (bf16[2,1,64,256]{3,2,0,1:T(8,128)(2,1)}, bf16[2,1,64,256]{3,2,0,1:T(8,128)(2,1)S(1)}, u32[]{:S(2)}, u32[]{:S(2)}) collective-permute-start(bf16[2,1,64,256]{3,2,0,1:T(8,128)(2,1)} %bitcast.10), channel_id=1, source_target_pairs={{0,1},{1,0},{2,3},{3,2},{4,5},{5,4},{6,7},{7,6},{8,9},{9,8},{10,11... | collective-permute-start | bytes 196616 | tf_op jit(solution)/shard_map/ppermute | solution.py:17
  12.8 3.9 %collective-permute-start.5 = (bf16[2,1,64,256]{3,2,0,1:T(8,128)(2,1)}, bf16[2,1,64,256]{3,2,0,1:T(8,128)(2,1)S(1)}, u32[]{:S(2)}, u32[]{:S(2)}) collective-permute-start(bf16[2,1,64,256]{3,2,0,1:T(8,128)(2,1)} %bitcast.9), channel_id=1, source_target_pairs={{0,3},{1,2},{2,1},{3,0},{4,7},{5,6},{6,5},{7,4},{8,11},{9,10},{10,... | collective-permute-start | bytes 196616 | tf_op jit(solution)/shard_map/ppermute | solution.py:17
  16.7 2.7 %copy-start.10 = (bf16[2,1,64,256]{3,2,1,0:T(8,128)(2,1)S(1)}, bf16[2,1,64,256]{3,2,1,0:T(8,128)(2,1)}, u32[]{:S(2)}) copy-start(bf16[2,1,64,256]{3,2,1,0:T(8,128)(2,1)} %get-tuple-element.17.refs_0_) | copy-start | bytes 196612
  16.7 51.1 %copy-start = (bf16[3,2,1,64,256]{4,3,2,1,0:T(8,128)(2,1)}, bf16[3,2,1,64,256]{4,3,2,1,0:T(8,128)(2,1)S(1)}, u32[]{:S(2)}) copy-start(bf16[3,2,1,64,256]{4,3,2,1,0:T(8,128)(2,1)S(1)} %pad_maximum_fusion.refs_4_) | copy-start | bytes 589828
  16.7 51.6 %collective-permute-start.7 = (bf16[3,2,1,64,256]{4,3,2,1,0:T(8,128)(2,1)S(1)}, bf16[3,2,1,64,256]{4,3,2,1,0:T(8,128)(2,1)S(1)}, u32[]{:S(2)}, u32[]{:S(2)}) collective-permute-start(bf16[3,2,1,64,256]{4,3,2,1,0:T(8,128)(2,1)S(1)} %pad_maximum_fusion.refs_4_), channel_id=1, source_target_pairs={{0,8},{4,12},{8,0},{12,4},{1,9},{5,13},{9,1},{13,5},{2,10},{6,14},... | collective-permute-start | bytes 589832 | tf_op jit(solution)/shard_map/ppermute | solution.py:17
  19.4 44.0 %collective-permute-start.1 = (bf16[2,1,64,256]{3,2,1,0:T(8,128)(2,1)S(1)}, bf16[2,1,64,256]{3,2,1,0:T(8,128)(2,1)S(1)}, u32[]{:S(2)}, u32[]{:S(2)}) collective-permute-start(bf16[2,1,64,256]{3,2,1,0:T(8,128)(2,1)S(1)} %copy-done.10), channel_id=1, source_target_pairs={{0,8},{4,12},{8,0},{12,4},{1,9},{5,13},{9,1},{13,5},{2,10},{6,14},... | collective-permute-start | bytes 196616 | tf_op jit(solution)/shard_map/ppermute | solution.py:17
  20.1 45.0 %collective-permute-start = (bf16[2,1,64,256]{3,2,1,0:T(8,128)(2,1)S(1)}, bf16[2,1,64,256]{3,2,1,0:T(8,128)(2,1)S(1)}, u32[]{:S(2)}, u32[]{:S(2)}) collective-permute-start(bf16[2,1,64,256]{3,2,1,0:T(8,128)(2,1)S(1)} %copy-done.10), channel_id=1, source_target_pairs={{0,4},{4,0},{8,12},{12,8},{1,5},{5,1},{9,13},{13,9},{2,6},{6,2},{1... | collective-permute-start | bytes 196616 | tf_op jit(solution)/shard_map/ppermute | solution.py:17
  63.2 12.4 %collective-permute-start.9 = (bf16[2,1,256,256]{3,2,1,0:T(8,128)(2,1)}, bf16[2,1,256,256]{3,2,1,0:T(8,128)(2,1)S(1)}, u32[]{:S(2)}, u32[]{:S(2)}) collective-permute-start(bf16[2,1,256,256]{3,2,1,0:T(8,128)(2,1)} %get-tuple-element.22), channel_id=1, source_target_pairs={{0,1},{1,0},{2,3},{3,2},{4,5},{5,4},{6,7},{7,6},{8,9},{9,8},{10,11... | collective-permute-start | bytes 786440 | tf_op jit(solution)/shard_map/ppermute | solution.py:17
  63.3 15.1 %copy-start.11 = (bf16[2,1,64,256]{3,2,1,0:T(8,128)(2,1)}, bf16[2,1,64,256]{3,2,1,0:T(8,128)(2,1)S(1)}, u32[]{:S(2)}) copy-start(bf16[2,1,64,256]{3,2,1,0:T(8,128)(2,1)S(1)} %collective-permute-done.1.refs_2_) | copy-start | bytes 196612
  63.3 4.5 %collective-permute-start.2 = (bf16[2,1,64,256]{3,2,1,0:T(8,128)(2,1)S(1)}, bf16[2,1,64,256]{3,2,1,0:T(8,128)(2,1)S(1)}, u32[]{:S(2)}, u32[]{:S(2)}) collective-permute-start(bf16[2,1,64,256]{3,2,1,0:T(8,128)(2,1)S(1)} %collective-permute-done.1.refs_2_), channel_id=1, source_target_pairs={{0,4},{4,0},{8,12},{12,8},{1,5},{5,1},{9,13},{13,9},{2,6},{6,2},{1... | collective-permute-start | bytes 196616 | tf_op jit(solution)/shard_map/ppermute | solution.py:17
  63.9 11.8 %collective-permute-start.10 = (bf16[2,1,256,256]{3,2,1,0:T(8,128)(2,1)}, bf16[2,1,256,256]{3,2,1,0:T(8,128)(2,1)S(1)}, u32[]{:S(2)}, u32[]{:S(2)}) collective-permute-start(bf16[2,1,256,256]{3,2,1,0:T(8,128)(2,1)} %get-tuple-element.23), channel_id=1, source_target_pairs={{0,2},{1,3},{2,0},{3,1},{4,6},{5,7},{6,4},{7,5},{8,10},{9,11},{10,... | collective-permute-start | bytes 786440 | tf_op jit(solution)/shard_map/ppermute | solution.py:17
  65.1 13.3 %copy-start.12 = (bf16[2,1,64,256]{3,2,1,0:T(8,128)(2,1)}, bf16[2,1,64,256]{3,2,1,0:T(8,128)(2,1)S(1)}, u32[]{:S(2)}) copy-start(bf16[2,1,64,256]{3,2,1,0:T(8,128)(2,1)S(1)} %collective-permute-done.refs_1_) | copy-start | bytes 196612
  65.1 12.1 %collective-permute-start.11 = (bf16[2,1,256,256]{3,2,1,0:T(8,128)(2,1)}, bf16[2,1,256,256]{3,2,1,0:T(8,128)(2,1)S(1)}, u32[]{:S(2)}, u32[]{:S(2)}) collective-permute-start(bf16[2,1,256,256]{3,2,1,0:T(8,128)(2,1)} %get-tuple-element.24), channel_id=1, source_target_pairs={{0,3},{1,2},{2,1},{3,0},{4,7},{5,6},{6,5},{7,4},{8,11},{9,10},{10,... | collective-permute-start | bytes 786440 | tf_op jit(solution)/shard_map/ppermute | solution.py:17
  67.8 10.6 %copy-start.13 = (bf16[2,1,64,256]{3,2,1,0:T(8,128)(2,1)}, bf16[2,1,64,256]{3,2,1,0:T(8,128)(2,1)S(1)}, u32[]{:S(2)}) copy-start(bf16[2,1,64,256]{3,2,1,0:T(8,128)(2,1)S(1)} %collective-permute-done.2.refs_3_) | copy-start | bytes 196612
  67.8 7.8 %collective-permute-start.6 = (bf16[3,2,1,64,256]{4,3,2,1,0:T(8,128)(2,1)S(1)}, bf16[3,2,1,64,256]{4,3,2,1,0:T(8,128)(2,1)S(1)}, u32[]{:S(2)}, u32[]{:S(2)}) collective-permute-start(bf16[3,2,1,64,256]{4,3,2,1,0:T(8,128)(2,1)S(1)} %pad_maximum_fusion.refs_4_), channel_id=1, source_target_pairs={{0,4},{4,0},{8,12},{12,8},{1,5},{5,1},{9,13},{13,9},{2,6},{6,2},{1... | collective-permute-start | bytes 589832 | tf_op jit(solution)/shard_map/ppermute | solution.py:17
  68.3 10.1 %copy-start.4 = (bf16[3,2,1,64,256]{4,3,2,1,0:T(8,128)(2,1)}, bf16[3,2,1,64,256]{4,3,2,1,0:T(8,128)(2,1)S(1)}, u32[]{:S(2)}) copy-start(bf16[3,2,1,64,256]{4,3,2,1,0:T(8,128)(2,1)S(1)} %collective-permute-done.7.refs_6_) | copy-start | bytes 589828
  68.3 10.1 %collective-permute-start.8 = (bf16[3,2,1,64,256]{4,3,2,1,0:T(8,128)(2,1)S(1)}, bf16[3,2,1,64,256]{4,3,2,1,0:T(8,128)(2,1)S(1)}, u32[]{:S(2)}, u32[]{:S(2)}) collective-permute-start(bf16[3,2,1,64,256]{4,3,2,1,0:T(8,128)(2,1)S(1)} %collective-permute-done.7.refs_6_), channel_id=1, source_target_pairs={{0,4},{4,0},{8,12},{12,8},{1,5},{5,1},{9,13},{13,9},{2,6},{6,2},{1... | collective-permute-start | bytes 589832 | tf_op jit(solution)/shard_map/ppermute | solution.py:17
  75.6 2.8 %copy-start.5 = (bf16[3,2,1,64,256]{4,3,2,1,0:T(8,128)(2,1)}, bf16[3,2,1,64,256]{4,3,2,1,0:T(8,128)(2,1)S(1)}, u32[]{:S(2)}) copy-start(bf16[3,2,1,64,256]{4,3,2,1,0:T(8,128)(2,1)S(1)} %collective-permute-done.6.refs_5_) | copy-start | bytes 589828
  75.6 2.8 %copy-start.1 = (bf16[2,1,256,256]{3,2,1,0:T(8,128)(2,1)}, bf16[2,1,256,256]{3,2,1,0:T(8,128)(2,1)S(1)}, u32[]{:S(2)}) copy-start(bf16[2,1,256,256]{3,2,1,0:T(8,128)(2,1)S(1)} %collective-permute-done.9.refs_9_) | copy-start | bytes 786436
  75.6 2.8 %copy-start.2 = (bf16[2,1,256,256]{3,2,1,0:T(8,128)(2,1)}, bf16[2,1,256,256]{3,2,1,0:T(8,128)(2,1)S(1)}, u32[]{:S(2)}) copy-start(bf16[2,1,256,256]{3,2,1,0:T(8,128)(2,1)S(1)} %collective-permute-done.10.refs_10_) | copy-start | bytes 786436
  77.2 1.3 %copy-start.3 = (bf16[2,1,256,256]{3,2,1,0:T(8,128)(2,1)}, bf16[2,1,256,256]{3,2,1,0:T(8,128)(2,1)S(1)}, u32[]{:S(2)}) copy-start(bf16[2,1,256,256]{3,2,1,0:T(8,128)(2,1)S(1)} %collective-permute-done.11.refs_11_) | copy-start | bytes 786436
  78.4 0.7 copy-start.6
  84.0 4.5 %collective-permute-start.12 = (bf16[2,1,64,256]{3,2,1,0:T(8,128)(2,1)}, bf16[2,1,64,256]{3,2,1,0:T(8,128)(2,1)S(1)}, u32[]{:S(2)}, u32[]{:S(2)}) collective-permute-start(bf16[2,1,64,256]{3,2,1,0:T(8,128)(2,1)} %get-tuple-element.27), channel_id=1, source_target_pairs={{0,4},{4,0},{8,12},{12,8},{1,5},{5,1},{9,13},{13,9},{2,6},{6,2},{1... | collective-permute-start | bytes 196616 | tf_op jit(solution)/shard_map/ppermute | solution.py:17
  84.4 8.8 %collective-permute-start.13 = (bf16[2,1,64,256]{3,2,1,0:T(8,128)(2,1)}, bf16[2,1,64,256]{3,2,1,0:T(8,128)(2,1)S(1)}, u32[]{:S(2)}, u32[]{:S(2)}) collective-permute-start(bf16[2,1,64,256]{3,2,1,0:T(8,128)(2,1)} %get-tuple-element.28), channel_id=1, source_target_pairs={{0,8},{4,12},{8,0},{12,4},{1,9},{5,13},{9,1},{13,5},{2,10},{6,14},... | collective-permute-start | bytes 196616 | tf_op jit(solution)/shard_map/ppermute | solution.py:17
  86.6 6.6 %collective-permute-start.14 = (bf16[2,1,64,256]{3,2,1,0:T(8,128)(2,1)}, bf16[2,1,64,256]{3,2,1,0:T(8,128)(2,1)S(1)}, u32[]{:S(2)}, u32[]{:S(2)}) collective-permute-start(bf16[2,1,64,256]{3,2,1,0:T(8,128)(2,1)} %get-tuple-element.29), channel_id=1, source_target_pairs={{0,12},{4,8},{8,4},{12,0},{1,13},{5,9},{9,5},{13,1},{2,14},{6,10},... | collective-permute-start | bytes 196616 | tf_op jit(solution)/shard_map/ppermute | solution.py:17
  88.5 4.8 %copy-start.7 = (bf16[2,1,64,256]{3,2,1,0:T(8,128)(2,1)}, bf16[2,1,64,256]{3,2,1,0:T(8,128)(2,1)S(1)}, u32[]{:S(2)}) copy-start(bf16[2,1,64,256]{3,2,1,0:T(8,128)(2,1)S(1)} %collective-permute-done.12.refs_1_) | copy-start | bytes 196612
  93.3 0.6 copy-start.8
  93.3 0.6 copy-start.9
  95.7 6.9 %collective-permute-start.17 = (bf16[2,1,64,256]{3,2,1,0:T(8,128)(2,1)}, bf16[2,1,64,256]{3,2,1,0:T(8,128)(2,1)S(1)}, u32[]{:S(2)}, u32[]{:S(2)}) collective-permute-start(bf16[2,1,64,256]{3,2,1,0:T(8,128)(2,1)} %finish_band.1.refs_0_), channel_id=1, source_target_pairs={{0,12},{4,8},{8,4},{12,0},{1,13},{5,9},{9,5},{13,1},{2,14},{6,10},... | collective-permute-start | bytes 196616 | tf_op jit(solution)/shard_map/ppermute | solution.py:17
  98.3 6.3 %collective-permute-start.16 = (bf16[2,1,64,256]{3,2,1,0:T(8,128)(2,1)}, bf16[2,1,64,256]{3,2,1,0:T(8,128)(2,1)S(1)}, u32[]{:S(2)}, u32[]{:S(2)}) collective-permute-start(bf16[2,1,64,256]{3,2,1,0:T(8,128)(2,1)} %finish_band.1.refs_0_), channel_id=1, source_target_pairs={{0,8},{4,12},{8,0},{12,4},{1,9},{5,13},{9,1},{13,5},{2,10},{6,14},... | collective-permute-start | bytes 196616 | tf_op jit(solution)/shard_map/ppermute | solution.py:17
  98.6 5.9 %collective-permute-start.15 = (bf16[2,1,64,256]{3,2,1,0:T(8,128)(2,1)}, bf16[2,1,64,256]{3,2,1,0:T(8,128)(2,1)S(1)}, u32[]{:S(2)}, u32[]{:S(2)}) collective-permute-start(bf16[2,1,64,256]{3,2,1,0:T(8,128)(2,1)} %finish_band.1.refs_0_), channel_id=1, source_target_pairs={{0,4},{4,0},{8,12},{12,8},{1,5},{5,1},{9,13},{13,9},{2,6},{6,2},{1... | collective-permute-start | bytes 196616 | tf_op jit(solution)/shard_map/ppermute | solution.py:17
  102.6 1.9 %copy-start.14 = (bf16[2,1,64,256]{3,2,1,0:T(8,128)(2,1)}, bf16[2,1,64,256]{3,2,1,0:T(8,128)(2,1)S(1)}, u32[]{:S(2)}) copy-start(bf16[2,1,64,256]{3,2,1,0:T(8,128)(2,1)S(1)} %collective-permute-done.17.refs_3_) | copy-start | bytes 196612
  104.5 0.6 copy-start.15
  105.1 0.6 copy-start.16

commit v2 on v1

--- a/solution.py
+++ b/solution.py
@@ -7,7 +7,9 @@
 
 BF16 = jnp.bfloat16
 F32 = jnp.float32
+FEW = 8
 ANY = pl.BlockSpec(memory_space=pl.ANY)
+HBM = pl.BlockSpec(memory_space=pltpu.HBM)
 VMEM = pl.BlockSpec(memory_space=pltpu.VMEM)
 SMEM = pl.BlockSpec(memory_space=pltpu.SMEM)
 
@@ -15,6 +17,14 @@
 def swap(x, axis, d):
     n = lax.axis_size(axis)
     return lax.ppermute(x, axis, [(i, i ^ d) for i in range(n)])
+
+
+def nbytes(*arrays):
+    return sum(a.size * a.dtype.itemsize for a in arrays)
+
+
+def limits(*arrays):
+    return pltpu.CompilerParams(vmem_limit_bytes=nbytes(*arrays) + (4 << 20))
 
 
 def run_copies(copies):
@@ -40,13 +50,15 @@
             ]
         )
 
+    outs = [jax.ShapeDtypeStruct((planes, own_k, rows, width), panel.dtype)] * n_cols
     return pl.pallas_call(
         kernel,
         name="pick_panel",
-        in_specs=[ANY],
-        out_specs=[ANY] * n_cols,
-        out_shape=[jax.ShapeDtypeStruct((planes, own_k, rows, width), panel.dtype)] * n_cols,
+        in_specs=[HBM],
+        out_specs=[VMEM] * n_cols,
+        out_shape=outs,
         scratch_shapes=[pltpu.SemaphoreType.DMA((n_cols,))],
+        compiler_params=limits(*outs),
     )(panel)
 
 
@@ -102,12 +114,14 @@
         run_copies(copies)
 
     shape = jax.ShapeDtypeStruct((2, own_k, rows.count * width, slots * width), ainv.dtype)
+    outs = [shape] * n_cols + [jax.ShapeDtypeStruct((2, own_k, width, width), u_inv.dtype)]
     out = pl.pallas_call(
         kernel,
         name="pick_ainv",
         in_specs=[SMEM, ANY, ANY],
-        out_specs=[ANY] * (n_cols + 1),
-        out_shape=[shape] * n_cols + [jax.ShapeDtypeStruct((2, own_k, width, width), u_inv.dtype)],
+        out_specs=[VMEM] * (n_cols + 1),
+        out_shape=outs,
+        compiler_params=limits(*outs),
         scratch_shapes=[
             pltpu.SemaphoreType.DMA((n_cols, own_k, rows.count, slots)),
             pltpu.SemaphoreType.DMA,
@@ -126,29 +140,31 @@
 
 def solve(structure, own, rest, ainv, u_own, rows):
     n_rows, n_cols = lax.axis_size("prow"), lax.axis_size("pcol")
-    _, own_k, part, width = own[0].shape
+    _, own_k, part, width = own[0].shape[-4:]
+    few = len(own) == n_rows
     slots = rows.group_slots
     sub = min(part, width)
     band = width // n_rows
 
     def kernel(struct_ref, u_ref, *refs):
-        own_refs, refs = refs[:n_rows], refs[n_rows:]
-        rest_refs, refs = refs[:n_rows], refs[n_rows:]
+        own_refs, refs = refs[: len(own)], refs[len(own) :]
+        rest_refs, refs = refs[: len(rest)], refs[len(rest) :]
         ainv_refs, refs = refs[:n_cols], refs[n_cols:]
-        sel_ref, q_refs, (scaled, quad) = refs[0], refs[1 : 1 + n_rows], refs[1 + n_rows :]
+        sel_ref, *q_refs, scaled, quad = refs
         col, row = lax.axis_index("pcol"), lax.axis_index("prow")
         if rows.by_slot:
             sel_ref[...] = jnp.zeros_like(sel_ref)
         for kk in range(own_k):
             node = col * own_k + kk
             u_real, u_imag = u_ref[0, kk], u_ref[1, kk]
-            for dz in range(n_rows):
-                first = (row ^ dz) * part
+
+            def scale(own_ref, rest_ref, member, node=node, kk=kk, u_real=u_real, u_imag=u_imag):
+                first = member * part
                 for real, imag, dxs in (
-                    (own_refs[dz][0, kk], own_refs[dz][1, kk], (0,)),
+                    (own_ref[0, kk], own_ref[1, kk], (0,)),
                     (
-                        rest_refs[dz][:, 0, kk].reshape((n_cols - 1) * part, width),
-                        rest_refs[dz][:, 1, kk].reshape((n_cols - 1) * part, width),
+                        rest_ref[:, 0, kk].reshape((n_cols - 1) * part, width),
+                        rest_ref[:, 1, kk].reshape((n_cols - 1) * part, width),
                         tuple(range(1, n_cols)),
                     ),
                 ):
@@ -162,6 +178,16 @@
                             for plane, value in ((0, s_real), (1, s_imag)):
                                 piece = value[n * part + o : n * part + o + sub]
                                 scaled[plane, kk, dx, at, :] = jnp.where(live, piece, 0.0).astype(BF16)
+
+            if few:
+                for dz in range(n_rows):
+                    scale(own_refs[dz], rest_refs[dz], row ^ dz)
+            else:
+
+                @pl.loop(0, n_rows)
+                def _(i, scale=scale):
+                    scale(own_refs[0].at[i], rest_refs[0].at[i], i)
+
             q_real = jnp.zeros((width, width), F32)
             q_imag = jnp.zeros((width, width), F32)
             for i in range(rows.count):
@@ -198,26 +224,31 @@
                 q_real += by_real[:, :width] - by_imag[:, width:]
                 q_imag += by_real[:, width:] + by_imag[:, :width]
             quad[0], quad[1] = q_real, q_imag
-            for dz in range(n_rows):
-                at = pl.ds(pl.multiple_of((row ^ dz) * band, band), band)
+            if few:
+                for dz in range(n_rows):
+                    at = pl.ds(pl.multiple_of((row ^ dz) * band, band), band)
+                    for plane in range(2):
+                        q_refs[dz][plane, kk] = quad[plane, at, :].astype(q_refs[dz].dtype)
+            else:
                 for plane in range(2):
-                    q_refs[dz][plane, kk] = quad[plane, at, :].astype(q_refs[dz].dtype)
-
+                    q_refs[0][plane, kk] = quad[plane].astype(BF16)
+
+    sel = jax.ShapeDtypeStruct((2, rows.row_blocks * width, own_k * width), F32)
     chunk = (2, own_k, band, width)
+    if few:
+        terms = [jax.ShapeDtypeStruct(chunk, F32)] + [jax.ShapeDtypeStruct(chunk, BF16)] * (n_rows - 1)
+    else:
+        terms = [jax.ShapeDtypeStruct((2, own_k, width, width), BF16)]
+    scaled = jax.ShapeDtypeStruct((2, own_k, n_cols, slots * width, width), BF16)
+    quad = jax.ShapeDtypeStruct((2, width, width), F32)
     out = pl.pallas_call(
         kernel,
         name="solve",
-        in_specs=[SMEM] + [VMEM] * (1 + 2 * n_rows + n_cols),
-        out_specs=[VMEM] * (1 + n_rows),
-        out_shape=[
-            jax.ShapeDtypeStruct((2, rows.row_blocks * width, own_k * width), F32),
-            jax.ShapeDtypeStruct(chunk, F32),
-        ]
-        + [jax.ShapeDtypeStruct(chunk, BF16)] * (n_rows - 1),
-        scratch_shapes=[
-            pltpu.VMEM((2, own_k, n_cols, slots * width, width), BF16),
-            pltpu.VMEM((2, width, width), F32),
-        ],
+        in_specs=[SMEM] + [VMEM] * (1 + len(own) + len(rest) + n_cols),
+        out_specs=[VMEM] * (1 + len(terms)),
+        out_shape=[sel] + terms,
+        scratch_shapes=[pltpu.VMEM(scaled.shape, scaled.dtype), pltpu.VMEM(quad.shape, quad.dtype)],
+        compiler_params=limits(sel, *terms, scaled, quad, u_own, *own, *rest, *ainv),
     )(structure, u_own, *own, *rest, *ainv)
     return out[0], out[1:]
 
@@ -227,7 +258,7 @@
         *term_refs, out_ref = refs
         row = lax.axis_index("prow")
         band = out_ref.shape[2]
-        total = term_refs[0][...]
+        total = term_refs[0][...].astype(F32)
         for ref in term_refs[1:]:
             total += ref[...].astype(F32)
         at = pl.ds(pl.multiple_of(row * band, band), band)
@@ -239,6 +270,7 @@
         in_specs=[VMEM] * (1 + len(terms)),
         out_specs=VMEM,
         out_shape=jax.ShapeDtypeStruct(terms[0].shape, BF16),
+        compiler_params=limits(k_inv, *terms),
     )(k_inv, *terms)
 
 
@@ -257,11 +289,14 @@
         in_specs=[VMEM] * len(bands),
         out_specs=VMEM,
         out_shape=jax.ShapeDtypeStruct(shape, F32),
+        compiler_params=limits(jax.ShapeDtypeStruct(shape, F32), *bands),
     )(*bands)
 
 
 def gather_rows(x):
     n = lax.axis_size("prow")
+    if n > FEW:
+        return [lax.all_gather(x, "prow")]
     held = {0: x}
     d = n // 2
     while d:
@@ -282,6 +317,10 @@
     blocks, u_own = pick_ainv(ainv_anc, u_inv, structure, own_k, rows)
     ainv = [blocks[0]] + [swap(blocks[d], "pcol", d) for d in range(1, n_cols)]
     sel_inv, terms = solve(structure, own, rest, ainv, u_own, rows)
+    if n_rows > FEW:
+        total = lax.psum_scatter(terms[0], "prow", scatter_dimension=2, tiled=True)
+        mine = finish_band(k_inv, [total])
+        return sel_inv, lax.all_gather(mine, "prow", axis=2, tiled=True).astype(F32)
     terms = [terms[0]] + [swap(terms[d], "prow", d) for d in range(1, n_rows)]
     mine = finish_band(k_inv, terms)
     bands = [mine] + [swap(mine, "prow", d) for d in range(1, n_rows)]

time: 108 us -> 61.5 us (0.57)
  Pallas kernels: 59.1 us -> 5.3 us
  waiting for transfers between devices: 24 us -> 30.8 us
    pallas_call x1, Pallas kernels: 41.6 us -> 0.76 us  [pick_ainv(): pl.pallas_call(kernel, name='pick_ainv', in_specs=[SMEM, ANY, ANY], out_s...]
    pallas_call x2, Pallas kernels: 14 us -> 3.66 us  [the longest x1 3.47 us: solve(): pl.pallas_call(kernel, name='solve', in_specs=[SMEM] + [VMEM] * (1 + len(...]
    ppermute x18, waiting for transfers between devices: 24 us -> 30.8 us  [swap(): return lax.ppermute(x, axis, [(i, i ^ d) for i in range(n)])]
    pallas_call x1, Pallas kernels: 1.81 us -> 0.04 us  [finish_band(): pl.pallas_call(kernel, name='finish_band', in_specs=[VMEM] * (1 + len(ter...]
    unnamed x34 -> x10, local copies, waits for them, and re-layouts: 2.52 us -> 3.4 us
  transfers between devices with their start and end apart: 18 -> 18, of which waited for: 10 -> 11; matrix products, arithmetic and copies ran while one was open for 0% -> 0% of each run, Pallas kernels for 39% -> 1%
where the time goes in v2:
time: 61.5 us; the launch traced here: 61.3 us
  waiting for transfers between devices  30.8 us (50%)
  starting transfers between devices  21.1 us (34%)
  Pallas kernels  5.3 us (9%)
  local copies, waits for them, and re-layouts  3.4 us (6%)
  between operations  0.69 us (1%)
    ppermute x18, waiting for transfers between devices, swap(): return lax.ppermute(x, axis, [(i, i ^ d) for i in range(n)])  30.8 us
    ppermute x18, starting transfers between devices, swap(): return lax.ppermute(x, axis, [(i, i ^ d) for i in range(n)])  21.1 us
    pallas_call x1, Pallas kernels, solve(): pl.pallas_call(kernel, name='solve', in_specs=[SMEM] + [VMEM] * (1 + len(...  3.47 us
    unnamed x10, local copies, waits for them, and re-layouts  3.4 us
  transfers between devices with their start and end apart: 18, of which 11 were waited for; matrix products, arithmetic and copies ran while one was open for 0% of the time, Pallas kernels for 1%

profile of v2, /device:TPU:0, one launch (start us, length us, event | category | flops | bytes accessed | tf_op | source)
XLA Modules:
  0.0 61.3 jit_solution(3457366766009304521)
XLA Ops:
  0.6 0.0 copy-start.3
  0.6 0.9 %copy-done.3 = bf16[2,4,64,256]{3,2,1,0:T(8,128)(2,1)S(1)} copy-done((bf16[2,4,64,256]{3,2,1,0:T(8,128)(2,1)S(1)}, bf16[2,4,64,256]{3,2,1,0:T(8,128)(2,1)}, u32[]{:S(2)}) %copy-start.3) | copy-done | bytes 262168
  1.6 0.2 pick_panel.1
  1.8 3.0 %collective-permute-start.4 = (bf16[2,1,64,256]{3,2,0,1:T(8,128)(2,1)S(1)}, bf16[2,1,64,256]{3,2,0,1:T(8,128)(2,1)S(1)}, u32[]{:S(2)}, u32[]{:S(2)}) collective-permute-start(bf16[2,1,64,256]{3,2,0,1:T(8,128)(2,1)S(1)} %bitcast.8), channel_id=1, source_target_pairs={{0,2},{1,3},{2,0},{3,1},{4,6},{5,7},{6,4},{7,5},{8,10},{9,11},{10,... | collective-permute-start | bytes 196616 | tf_op jit(solution)/shard_map/ppermute | solution.py:19
  4.8 0.0 collective-permute-start.3
  4.8 0.2 collective-permute-start.5
  5.0 2.1 %collective-permute-done.4 = bf16[2,1,64,256]{3,2,0,1:T(8,128)(2,1)S(1)} collective-permute-done((bf16[2,1,64,256]{3,2,0,1:T(8,128)(2,1)S(1)}, bf16[2,1,64,256]{3,2,0,1:T(8,128)(2,1)S(1)}, u32[]{:S(2)}, u32[]{:S(2)}) %collective-permute-start.4) | collective-permute-done | bytes 65568 | tf_op jit(solution)/shard_map/ppermute | solution.py:19
  7.1 0.0 collective-permute-done.3
  7.1 1.4 %collective-permute-done.5 = bf16[2,1,64,256]{3,2,0,1:T(8,128)(2,1)S(1)} collective-permute-done((bf16[2,1,64,256]{3,2,0,1:T(8,128)(2,1)S(1)}, bf16[2,1,64,256]{3,2,0,1:T(8,128)(2,1)S(1)}, u32[]{:S(2)}, u32[]{:S(2)}) %collective-permute-start.5) | collective-permute-done | bytes 65568 | tf_op jit(solution)/shard_map/ppermute | solution.py:19
  8.5 0.0 copy-start.4
  8.5 2.7 %collective-permute-start.7 = (bf16[3,2,1,64,256]{4,3,2,1,0:T(8,128)(2,1)S(1)}, bf16[3,2,1,64,256]{4,3,2,1,0:T(8,128)(2,1)S(1)}, u32[]{:S(2)}, u32[]{:S(2)}) collective-permute-start(bf16[3,2,1,64,256]{4,3,2,1,0:T(8,128)(2,1)S(1)} %pad_maximum_fusion.refs_4_), channel_id=1, source_target_pairs={{0,8},{4,12},{8,0},{12,4},{1,9},{5,13},{9,1},{13,5},{2,10},{6,14},... | collective-permute-start | bytes 589832 | tf_op jit(solution)/shard_map/ppermute | solution.py:19
  11.2 0.3 collective-permute-start.1
  11.5 1.6 %collective-permute-start = (bf16[2,1,64,256]{3,2,1,0:T(8,128)(2,1)S(1)}, bf16[2,1,64,256]{3,2,1,0:T(8,128)(2,1)S(1)}, u32[]{:S(2)}, u32[]{:S(2)}) collective-permute-start(bf16[2,1,64,256]{3,2,1,0:T(8,128)(2,1)S(1)} %get-tuple-element.17.refs_0_), channel_id=1, source_target_pairs={{0,4},{4,0},{8,12},{12,8},{1,5},{5,1},{9,13},{13,9},{2,6},{6,2},{1... | collective-permute-start | bytes 196616 | tf_op jit(solution)/shard_map/ppermute | solution.py:19
  13.1 0.0 copy-done.4
  13.1 0.0 copy-start
  13.1 1.2 %copy-done = bf16[2,512,512]{2,1,0:T(8,128)(2,1)S(1)} copy-done((bf16[2,512,512]{2,1,0:T(8,128)(2,1)S(1)}, bf16[2,512,512]{2,1,0:T(8,128)(2,1)}, u32[]{:S(2)}) %copy-start) | copy-done | bytes 1048600
  14.3 1.2 %copy-done.1 = bf16[2,4,256,256]{3,2,1,0:T(8,128)(2,1)S(1)} copy-done((bf16[2,4,256,256]{3,2,1,0:T(8,128)(2,1)S(1)}, bf16[2,4,256,256]{3,2,1,0:T(8,128)(2,1)}, u32[]{:S(2)}) %copy-start.1) | copy-done | bytes 1048600
  15.6 0.8 %pick_ainv.1 = (bf16[2,1,256,256]{3,2,1,0:T(8,128)(2,1)S(1)}, bf16[2,1,256,256]{3,2,1,0:T(8,128)(2,1)S(1)}, bf16[2,1,256,256]{3,2,1,0:T(8,128)(2,1)S(1)}, bf16[2...) custom-call(s32[4,4]{1,0:T(4,128)S(1)} %copy-done.4, bf16[2,512,512]{2,1,0:T(8,128)(2,1)S(1)} %copy-done, ...), custom_call_target="tpu_custom_call" | custom-call | tf_op jit(solution)/shard_map/pick_ainv/pallas_call | solution.py:118
  16.3 0.1 collective-permute-start.9
  16.4 7.4 %collective-permute-done.1.refs_2_ = bf16[2,1,64,256]{3,2,1,0:T(8,128)(2,1)S(1)} collective-permute-done((bf16[2,1,64,256]{3,2,1,0:T(8,128)(2,1)S(1)}, bf16[2,1,64,256]{3,2,1,0:T(8,128)(2,1)S(1)}, u32[]{:S(2)}, u32[]{:S(2)}) %collective-permute-start.1) | collective-permute-done | bytes 65568 | tf_op jit(solution)/shard_map/ppermute | solution.py:19
  23.9 0.7 %collective-permute-start.2 = (bf16[2,1,64,256]{3,2,1,0:T(8,128)(2,1)S(1)}, bf16[2,1,64,256]{3,2,1,0:T(8,128)(2,1)S(1)}, u32[]{:S(2)}, u32[]{:S(2)}) collective-permute-start(bf16[2,1,64,256]{3,2,1,0:T(8,128)(2,1)S(1)} %collective-permute-done.1.refs_2_), channel_id=1, source_target_pairs={{0,4},{4,0},{8,12},{12,8},{1,5},{5,1},{9,13},{13,9},{2,6},{6,2},{1... | collective-permute-start | bytes 196616 | tf_op jit(solution)/shard_map/ppermute | solution.py:19
  24.5 1.2 %collective-permute-start.10 = (bf16[2,1,256,256]{3,2,1,0:T(8,128)(2,1)S(1)}, bf16[2,1,256,256]{3,2,1,0:T(8,128)(2,1)S(1)}, u32[]{:S(2)}, u32[]{:S(2)}) collective-permute-start(bf16[2,1,256,256]{3,2,1,0:T(8,128)(2,1)S(1)} %get-tuple-element.23), channel_id=1, source_target_pairs={{0,2},{1,3},{2,0},{3,1},{4,6},{5,7},{6,4},{7,5},{8,10},{9,11},{10,... | collective-permute-start | bytes 786440 | tf_op jit(solution)/shard_map/ppermute | solution.py:19
  25.8 0.0 collective-permute-done.refs_1_
  25.8 0.0 collective-permute-start.11
  25.8 2.3 %collective-permute-done.2.refs_3_ = bf16[2,1,64,256]{3,2,1,0:T(8,128)(2,1)S(1)} collective-permute-done((bf16[2,1,64,256]{3,2,1,0:T(8,128)(2,1)S(1)}, bf16[2,1,64,256]{3,2,1,0:T(8,128)(2,1)S(1)}, u32[]{:S(2)}, u32[]{:S(2)}) %collective-permute-start.2) | collective-permute-done | bytes 65568 | tf_op jit(solution)/shard_map/ppermute | solution.py:19
  28.1 0.7 %collective-permute-start.6 = (bf16[3,2,1,64,256]{4,3,2,1,0:T(8,128)(2,1)S(1)}, bf16[3,2,1,64,256]{4,3,2,1,0:T(8,128)(2,1)S(1)}, u32[]{:S(2)}, u32[]{:S(2)}) collective-permute-start(bf16[3,2,1,64,256]{4,3,2,1,0:T(8,128)(2,1)S(1)} %pad_maximum_fusion.refs_4_), channel_id=1, source_target_pairs={{0,4},{4,0},{8,12},{12,8},{1,5},{5,1},{9,13},{13,9},{2,6},{6,2},{1... | collective-permute-start | bytes 589832 | tf_op jit(solution)/shard_map/ppermute | solution.py:19
  28.8 0.0 collective-permute-done.7.refs_6_
  28.8 1.3 %collective-permute-start.8 = (bf16[3,2,1,64,256]{4,3,2,1,0:T(8,128)(2,1)S(1)}, bf16[3,2,1,64,256]{4,3,2,1,0:T(8,128)(2,1)S(1)}, u32[]{:S(2)}, u32[]{:S(2)}) collective-permute-start(bf16[3,2,1,64,256]{4,3,2,1,0:T(8,128)(2,1)S(1)} %collective-permute-done.7.refs_6_), channel_id=1, source_target_pairs={{0,4},{4,0},{8,12},{12,8},{1,5},{5,1},{9,13},{13,9},{2,6},{6,2},{1... | collective-permute-start | bytes 589832 | tf_op jit(solution)/shard_map/ppermute | solution.py:19
  30.1 5.5 %collective-permute-done.6.refs_5_ = bf16[3,2,1,64,256]{4,3,2,1,0:T(8,128)(2,1)S(1)} collective-permute-done((bf16[3,2,1,64,256]{4,3,2,1,0:T(8,128)(2,1)S(1)}, bf16[3,2,1,64,256]{4,3,2,1,0:T(8,128)(2,1)S(1)}, u32[]{:S(2)}, u32[]{:S(2)}) %collective-permute-start.6) | collective-permute-done | bytes 196640 | tf_op jit(solution)/shard_map/ppermute | solution.py:19
  35.6 0.0 collective-permute-done.9.refs_9_
  35.6 0.0 collective-permute-done.10.refs_10_
  35.6 1.3 %collective-permute-done.11.refs_11_ = bf16[2,1,256,256]{3,2,1,0:T(8,128)(2,1)S(1)} collective-permute-done((bf16[2,1,256,256]{3,2,1,0:T(8,128)(2,1)S(1)}, bf16[2,1,256,256]{3,2,1,0:T(8,128)(2,1)S(1)}, u32[]{:S(2)}, u32[]{:S(2)}) %collective-permute-start.11) | collective-permute-done | bytes 262176 | tf_op jit(solution)/shard_map/ppermute | solution.py:19
  36.9 0.8 %collective-permute-done.8.refs_7_ = bf16[3,2,1,64,256]{4,3,2,1,0:T(8,128)(2,1)S(1)} collective-permute-done((bf16[3,2,1,64,256]{4,3,2,1,0:T(8,128)(2,1)S(1)}, bf16[3,2,1,64,256]{4,3,2,1,0:T(8,128)(2,1)S(1)}, u32[]{:S(2)}, u32[]{:S(2)}) %collective-permute-start.8) | collective-permute-done | bytes 196640 | tf_op jit(solution)/shard_map/ppermute | solution.py:19
  37.7 3.5 %solve.1 = (f32[2,512,256]{2,1,0:T(8,128)}, f32[2,1,64,256]{3,2,1,0:T(8,128)S(1)}, bf16[2,1,64,256]{3,2,1,0:T(8,128)(2,1)S(1)}, bf16[2,1,64,256]{3,2,1,0:T(8,128)(2,1)S(1)}, bf16[2,1,64,256]{3,2,1,0:T(8,128)(2,1)S(1)}) custom-call(s32[4,4]{1,0:T(4,128)S(1)} %copy-done.4, bf16[2,1,256,256]{3,2,1,0:T(8,128)(2,1)S(1)} %get-tuple-element.16.u_ref, ...), custom_call_target="tpu_custom_call" | custom-call | tf_op jit(solution)/shard_map/solve/pallas_call | solution.py:244
  41.2 1.3 %collective-permute-start.12 = (bf16[2,1,64,256]{3,2,1,0:T(8,128)(2,1)S(1)}, bf16[2,1,64,256]{3,2,1,0:T(8,128)(2,1)S(1)}, u32[]{:S(2)}, u32[]{:S(2)}) collective-permute-start(bf16[2,1,64,256]{3,2,1,0:T(8,128)(2,1)S(1)} %get-tuple-element.27), channel_id=1, source_target_pairs={{0,4},{4,0},{8,12},{12,8},{1,5},{5,1},{9,13},{13,9},{2,6},{6,2},{1... | collective-permute-start | bytes 196616 | tf_op jit(solution)/shard_map/ppermute | solution.py:19
  42.5 3.1 %collective-permute-start.13 = (bf16[2,1,64,256]{3,2,1,0:T(8,128)(2,1)S(1)}, bf16[2,1,64,256]{3,2,1,0:T(8,128)(2,1)S(1)}, u32[]{:S(2)}, u32[]{:S(2)}) collective-permute-start(bf16[2,1,64,256]{3,2,1,0:T(8,128)(2,1)S(1)} %get-tuple-element.28), channel_id=1, source_target_pairs={{0,8},{4,12},{8,0},{12,4},{1,9},{5,13},{9,1},{13,5},{2,10},{6,14},... | collective-permute-start | bytes 196616 | tf_op jit(solution)/shard_map/ppermute | solution.py:19
  45.6 0.4 collective-permute-start.14
  46.0 0.0 collective-permute-done.12.refs_1_
  46.0 2.1 %collective-permute-done.13.refs_2_ = bf16[2,1,64,256]{3,2,1,0:T(8,128)(2,1)S(1)} collective-permute-done((bf16[2,1,64,256]{3,2,1,0:T(8,128)(2,1)S(1)}, bf16[2,1,64,256]{3,2,1,0:T(8,128)(2,1)S(1)}, u32[]{:S(2)}, u32[]{:S(2)}) %collective-permute-start.13) | collective-permute-done | bytes 65568 | tf_op jit(solution)/shard_map/ppermute | solution.py:19
  48.1 3.7 %collective-permute-done.14.refs_3_ = bf16[2,1,64,256]{3,2,1,0:T(8,128)(2,1)S(1)} collective-permute-done((bf16[2,1,64,256]{3,2,1,0:T(8,128)(2,1)S(1)}, bf16[2,1,64,256]{3,2,1,0:T(8,128)(2,1)S(1)}, u32[]{:S(2)}, u32[]{:S(2)}) %collective-permute-start.14) | collective-permute-done | bytes 65568 | tf_op jit(solution)/shard_map/ppermute | solution.py:19
  51.8 0.0 copy-done.2
  51.8 2.2 %collective-permute-start.17 = (bf16[2,1,64,256]{3,2,1,0:T(8,128)(2,1)S(1)}, bf16[2,1,64,256]{3,2,1,0:T(8,128)(2,1)S(1)}, u32[]{:S(2)}, u32[]{:S(2)}) collective-permute-start(bf16[2,1,64,256]{3,2,1,0:T(8,128)(2,1)S(1)} %finish_band.1.refs_0_), channel_id=1, source_target_pairs={{0,12},{4,8},{8,4},{12,0},{1,13},{5,9},{9,5},{13,1},{2,14},{6,10},... | collective-permute-start | bytes 196616 | tf_op jit(solution)/shard_map/ppermute | solution.py:19
  54.0 0.4 collective-permute-start.16
  54.4 1.9 %collective-permute-start.15 = (bf16[2,1,64,256]{3,2,1,0:T(8,128)(2,1)S(1)}, bf16[2,1,64,256]{3,2,1,0:T(8,128)(2,1)S(1)}, u32[]{:S(2)}, u32[]{:S(2)}) collective-permute-start(bf16[2,1,64,256]{3,2,1,0:T(8,128)(2,1)S(1)} %finish_band.1.refs_0_), channel_id=1, source_target_pairs={{0,4},{4,0},{8,12},{12,8},{1,5},{5,1},{9,13},{13,9},{2,6},{6,2},{1... | collective-permute-start | bytes 196616 | tf_op jit(solution)/shard_map/ppermute | solution.py:19
  56.3 2.3 %collective-permute-done.17.refs_3_ = bf16[2,1,64,256]{3,2,1,0:T(8,128)(2,1)S(1)} collective-permute-done((bf16[2,1,64,256]{3,2,1,0:T(8,128)(2,1)S(1)}, bf16[2,1,64,256]{3,2,1,0:T(8,128)(2,1)S(1)}, u32[]{:S(2)}, u32[]{:S(2)}) %collective-permute-start.17) | collective-permute-done | bytes 65568 | tf_op jit(solution)/shard_map/ppermute | solution.py:19
  58.5 1.9 %collective-permute-done.16.refs_2_ = bf16[2,1,64,256]{3,2,1,0:T(8,128)(2,1)S(1)} collective-permute-done((bf16[2,1,64,256]{3,2,1,0:T(8,128)(2,1)S(1)}, bf16[2,1,64,256]{3,2,1,0:T(8,128)(2,1)S(1)}, u32[]{:S(2)}, u32[]{:S(2)}) %collective-permute-start.16) | collective-permute-done | bytes 65568 | tf_op jit(solution)/shard_map/ppermute | solution.py:19
  60.5 0.0 collective-permute-done.15.refs_1_
  60.5 0.8 %join_bands.1 = f32[2,1,256,256]{3,2,1,0:T(8,128)} custom-call(bf16[2,1,64,256]{3,2,1,0:T(8,128)(2,1)S(1)} %finish_band.1.refs_0_, bf16[2,1,64,256]{3,2,1,0:T(8,128)(2,1)S(1)} %collective-permute-done.15.refs_1_, bf16[2,1,64,256]{3,2,1,0:T(8,128)(2,1)S(1)} %collective-permute-done.16.refs_2_, bf16[2,1,64,256]{3,2,1,0:T(8,128)(2,1)S(1)} %collective-permute-done.17.refs_3_), custom_call_target="tpu_custom_call" | custom-call | tf_op jit(solution)/shard_map/join_bands/pallas_call | solution.py:286
  (4 shorter events, 0.1 us)
Async XLA Ops:
  0.6 1.0 %copy-start.3 = (bf16[2,4,64,256]{3,2,1,0:T(8,128)(2,1)S(1)}, bf16[2,4,64,256]{3,2,1,0:T(8,128)(2,1)}, u32[]{:S(2)}) copy-start(bf16[2,4,64,256]{3,2,1,0:T(8,128)(2,1)} %panel_ref.1) | copy-start | bytes 786436
  1.8 5.3 %collective-permute-start.4 = (bf16[2,1,64,256]{3,2,0,1:T(8,128)(2,1)S(1)}, bf16[2,1,64,256]{3,2,0,1:T(8,128)(2,1)S(1)}, u32[]{:S(2)}, u32[]{:S(2)}) collective-permute-start(bf16[2,1,64,256]{3,2,0,1:T(8,128)(2,1)S(1)} %bitcast.8), channel_id=1, source_target_pairs={{0,2},{1,3},{2,0},{3,1},{4,6},{5,7},{6,4},{7,5},{8,10},{9,11},{10,... | collective-permute-start | bytes 196616 | tf_op jit(solution)/shard_map/ppermute | solution.py:19
  4.8 2.3 %collective-permute-start.3 = (bf16[2,1,64,256]{3,2,0,1:T(8,128)(2,1)S(1)}, bf16[2,1,64,256]{3,2,0,1:T(8,128)(2,1)S(1)}, u32[]{:S(2)}, u32[]{:S(2)}) collective-permute-start(bf16[2,1,64,256]{3,2,0,1:T(8,128)(2,1)S(1)} %bitcast.7), channel_id=1, source_target_pairs={{0,1},{1,0},{2,3},{3,2},{4,5},{5,4},{6,7},{7,6},{8,9},{9,8},{10,11... | collective-permute-start | bytes 196616 | tf_op jit(solution)/shard_map/ppermute | solution.py:19
  4.8 3.7 %collective-permute-start.5 = (bf16[2,1,64,256]{3,2,0,1:T(8,128)(2,1)S(1)}, bf16[2,1,64,256]{3,2,0,1:T(8,128)(2,1)S(1)}, u32[]{:S(2)}, u32[]{:S(2)}) collective-permute-start(bf16[2,1,64,256]{3,2,0,1:T(8,128)(2,1)S(1)} %bitcast.6), channel_id=1, source_target_pairs={{0,3},{1,2},{2,1},{3,0},{4,7},{5,6},{6,5},{7,4},{8,11},{9,10},{10,... | collective-permute-start | bytes 196616 | tf_op jit(solution)/shard_map/ppermute | solution.py:19
  8.5 4.6 %copy-start.4 = (s32[4,4]{1,0:T(4,128)S(1)}, s32[4,4]{1,0:T(4,128)}, u32[]{:S(2)}) copy-start(s32[4,4]{1,0:T(4,128)} %struct_ref.3) | copy-start | bytes 196
  8.5 20.3 %collective-permute-start.7 = (bf16[3,2,1,64,256]{4,3,2,1,0:T(8,128)(2,1)S(1)}, bf16[3,2,1,64,256]{4,3,2,1,0:T(8,128)(2,1)S(1)}, u32[]{:S(2)}, u32[]{:S(2)}) collective-permute-start(bf16[3,2,1,64,256]{4,3,2,1,0:T(8,128)(2,1)S(1)} %pad_maximum_fusion.refs_4_), channel_id=1, source_target_pairs={{0,8},{4,12},{8,0},{12,4},{1,9},{5,13},{9,1},{13,5},{2,10},{6,14},... | collective-permute-start | bytes 589832 | tf_op jit(solution)/shard_map/ppermute | solution.py:19
  11.2 12.7 %collective-permute-start.1 = (bf16[2,1,64,256]{3,2,1,0:T(8,128)(2,1)S(1)}, bf16[2,1,64,256]{3,2,1,0:T(8,128)(2,1)S(1)}, u32[]{:S(2)}, u32[]{:S(2)}) collective-permute-start(bf16[2,1,64,256]{3,2,1,0:T(8,128)(2,1)S(1)} %get-tuple-element.17.refs_0_), channel_id=1, source_target_pairs={{0,8},{4,12},{8,0},{12,4},{1,9},{5,13},{9,1},{13,5},{2,10},{6,14},... | collective-permute-start | bytes 196616 | tf_op jit(solution)/shard_map/ppermute | solution.py:19
  11.5 14.3 %collective-permute-start = (bf16[2,1,64,256]{3,2,1,0:T(8,128)(2,1)S(1)}, bf16[2,1,64,256]{3,2,1,0:T(8,128)(2,1)S(1)}, u32[]{:S(2)}, u32[]{:S(2)}) collective-permute-start(bf16[2,1,64,256]{3,2,1,0:T(8,128)(2,1)S(1)} %get-tuple-element.17.refs_0_), channel_id=1, source_target_pairs={{0,4},{4,0},{8,12},{12,8},{1,5},{5,1},{9,13},{13,9},{2,6},{6,2},{1... | collective-permute-start | bytes 196616 | tf_op jit(solution)/shard_map/ppermute | solution.py:19
  13.1 1.2 %copy-start = (bf16[2,512,512]{2,1,0:T(8,128)(2,1)S(1)}, bf16[2,512,512]{2,1,0:T(8,128)(2,1)}, u32[]{:S(2)}) copy-start(bf16[2,512,512]{2,1,0:T(8,128)(2,1)} %ainv_ref.1) | copy-start | bytes 3145732
  14.3 1.2 %copy-start.1 = (bf16[2,4,256,256]{3,2,1,0:T(8,128)(2,1)S(1)}, bf16[2,4,256,256]{3,2,1,0:T(8,128)(2,1)}, u32[]{:S(2)}) copy-start(bf16[2,4,256,256]{3,2,1,0:T(8,128)(2,1)} %u_ref.1) | copy-start | bytes 3145732
  16.3 19.3 %collective-permute-start.9 = (bf16[2,1,256,256]{3,2,1,0:T(8,128)(2,1)S(1)}, bf16[2,1,256,256]{3,2,1,0:T(8,128)(2,1)S(1)}, u32[]{:S(2)}, u32[]{:S(2)}) collective-permute-start(bf16[2,1,256,256]{3,2,1,0:T(8,128)(2,1)S(1)} %get-tuple-element.22), channel_id=1, source_target_pairs={{0,1},{1,0},{2,3},{3,2},{4,5},{5,4},{6,7},{7,6},{8,9},{9,8},{10,11... | collective-permute-start | bytes 786440 | tf_op jit(solution)/shard_map/ppermute | solution.py:19
  23.9 4.3 %collective-permute-start.2 = (bf16[2,1,64,256]{3,2,1,0:T(8,128)(2,1)S(1)}, bf16[2,1,64,256]{3,2,1,0:T(8,128)(2,1)S(1)}, u32[]{:S(2)}, u32[]{:S(2)}) collective-permute-start(bf16[2,1,64,256]{3,2,1,0:T(8,128)(2,1)S(1)} %collective-permute-done.1.refs_2_), channel_id=1, source_target_pairs={{0,4},{4,0},{8,12},{12,8},{1,5},{5,1},{9,13},{13,9},{2,6},{6,2},{1... | collective-permute-start | bytes 196616 | tf_op jit(solution)/shard_map/ppermute | solution.py:19
  24.5 11.1 %collective-permute-start.10 = (bf16[2,1,256,256]{3,2,1,0:T(8,128)(2,1)S(1)}, bf16[2,1,256,256]{3,2,1,0:T(8,128)(2,1)S(1)}, u32[]{:S(2)}, u32[]{:S(2)}) collective-permute-start(bf16[2,1,256,256]{3,2,1,0:T(8,128)(2,1)S(1)} %get-tuple-element.23), channel_id=1, source_target_pairs={{0,2},{1,3},{2,0},{3,1},{4,6},{5,7},{6,4},{7,5},{8,10},{9,11},{10,... | collective-permute-start | bytes 786440 | tf_op jit(solution)/shard_map/ppermute | solution.py:19
  25.8 11.1 %collective-permute-start.11 = (bf16[2,1,256,256]{3,2,1,0:T(8,128)(2,1)S(1)}, bf16[2,1,256,256]{3,2,1,0:T(8,128)(2,1)S(1)}, u32[]{:S(2)}, u32[]{:S(2)}) collective-permute-start(bf16[2,1,256,256]{3,2,1,0:T(8,128)(2,1)S(1)} %get-tuple-element.24), channel_id=1, source_target_pairs={{0,3},{1,2},{2,1},{3,0},{4,7},{5,6},{6,5},{7,4},{8,11},{9,10},{10,... | collective-permute-start | bytes 786440 | tf_op jit(solution)/shard_map/ppermute | solution.py:19
  28.1 7.5 %collective-permute-start.6 = (bf16[3,2,1,64,256]{4,3,2,1,0:T(8,128)(2,1)S(1)}, bf16[3,2,1,64,256]{4,3,2,1,0:T(8,128)(2,1)S(1)}, u32[]{:S(2)}, u32[]{:S(2)}) collective-permute-start(bf16[3,2,1,64,256]{4,3,2,1,0:T(8,128)(2,1)S(1)} %pad_maximum_fusion.refs_4_), channel_id=1, source_target_pairs={{0,4},{4,0},{8,12},{12,8},{1,5},{5,1},{9,13},{13,9},{2,6},{6,2},{1... | collective-permute-start | bytes 589832 | tf_op jit(solution)/shard_map/ppermute | solution.py:19
  28.8 8.9 %collective-permute-start.8 = (bf16[3,2,1,64,256]{4,3,2,1,0:T(8,128)(2,1)S(1)}, bf16[3,2,1,64,256]{4,3,2,1,0:T(8,128)(2,1)S(1)}, u32[]{:S(2)}, u32[]{:S(2)}) collective-permute-start(bf16[3,2,1,64,256]{4,3,2,1,0:T(8,128)(2,1)S(1)} %collective-permute-done.7.refs_6_), channel_id=1, source_target_pairs={{0,4},{4,0},{8,12},{12,8},{1,5},{5,1},{9,13},{13,9},{2,6},{6,2},{1... | collective-permute-start | bytes 589832 | tf_op jit(solution)/shard_map/ppermute | solution.py:19
  37.7 14.1 %copy-start.2 = (f32[2,1,256,256]{3,2,1,0:T(8,128)S(1)}, f32[2,1,256,256]{3,2,1,0:T(8,128)}, u32[]{:S(2)}) copy-start(f32[2,1,256,256]{3,2,1,0:T(8,128)} %k_ref.1) | copy-start | bytes 1572868
  41.2 4.8 %collective-permute-start.12 = (bf16[2,1,64,256]{3,2,1,0:T(8,128)(2,1)S(1)}, bf16[2,1,64,256]{3,2,1,0:T(8,128)(2,1)S(1)}, u32[]{:S(2)}, u32[]{:S(2)}) collective-permute-start(bf16[2,1,64,256]{3,2,1,0:T(8,128)(2,1)S(1)} %get-tuple-element.27), channel_id=1, source_target_pairs={{0,4},{4,0},{8,12},{12,8},{1,5},{5,1},{9,13},{13,9},{2,6},{6,2},{1... | collective-permute-start | bytes 196616 | tf_op jit(solution)/shard_map/ppermute | solution.py:19
  42.5 5.6 %collective-permute-start.13 = (bf16[2,1,64,256]{3,2,1,0:T(8,128)(2,1)S(1)}, bf16[2,1,64,256]{3,2,1,0:T(8,128)(2,1)S(1)}, u32[]{:S(2)}, u32[]{:S(2)}) collective-permute-start(bf16[2,1,64,256]{3,2,1,0:T(8,128)(2,1)S(1)} %get-tuple-element.28), channel_id=1, source_target_pairs={{0,8},{4,12},{8,0},{12,4},{1,9},{5,13},{9,1},{13,5},{2,10},{6,14},... | collective-permute-start | bytes 196616 | tf_op jit(solution)/shard_map/ppermute | solution.py:19
  45.6 6.2 %collective-permute-start.14 = (bf16[2,1,64,256]{3,2,1,0:T(8,128)(2,1)S(1)}, bf16[2,1,64,256]{3,2,1,0:T(8,128)(2,1)S(1)}, u32[]{:S(2)}, u32[]{:S(2)}) collective-permute-start(bf16[2,1,64,256]{3,2,1,0:T(8,128)(2,1)S(1)} %get-tuple-element.29), channel_id=1, source_target_pairs={{0,12},{4,8},{8,4},{12,0},{1,13},{5,9},{9,5},{13,1},{2,14},{6,10},... | collective-permute-start | bytes 196616 | tf_op jit(solution)/shard_map/ppermute | solution.py:19
  51.8 6.7 %collective-permute-start.17 = (bf16[2,1,64,256]{3,2,1,0:T(8,128)(2,1)S(1)}, bf16[2,1,64,256]{3,2,1,0:T(8,128)(2,1)S(1)}, u32[]{:S(2)}, u32[]{:S(2)}) collective-permute-start(bf16[2,1,64,256]{3,2,1,0:T(8,128)(2,1)S(1)} %finish_band.1.refs_0_), channel_id=1, source_target_pairs={{0,12},{4,8},{8,4},{12,0},{1,13},{5,9},{9,5},{13,1},{2,14},{6,10},... | collective-permute-start | bytes 196616 | tf_op jit(solution)/shard_map/ppermute | solution.py:19
  54.0 6.4 %collective-permute-start.16 = (bf16[2,1,64,256]{3,2,1,0:T(8,128)(2,1)S(1)}, bf16[2,1,64,256]{3,2,1,0:T(8,128)(2,1)S(1)}, u32[]{:S(2)}, u32[]{:S(2)}) collective-permute-start(bf16[2,1,64,256]{3,2,1,0:T(8,128)(2,1)S(1)} %finish_band.1.refs_0_), channel_id=1, source_target_pairs={{0,8},{4,12},{8,0},{12,4},{1,9},{5,13},{9,1},{13,5},{2,10},{6,14},... | collective-permute-start | bytes 196616 | tf_op jit(solution)/shard_map/ppermute | solution.py:19
  54.4 6.1 %collective-permute-start.15 = (bf16[2,1,64,256]{3,2,1,0:T(8,128)(2,1)S(1)}, bf16[2,1,64,256]{3,2,1,0:T(8,128)(2,1)S(1)}, u32[]{:S(2)}, u32[]{:S(2)}) collective-permute-start(bf16[2,1,64,256]{3,2,1,0:T(8,128)(2,1)S(1)} %finish_band.1.refs_0_), channel_id=1, source_target_pairs={{0,4},{4,0},{8,12},{12,8},{1,5},{5,1},{9,13},{13,9},{2,6},{6,2},{1... | collective-permute-start | bytes 196616 | tf_op jit(solution)/shard_map/ppermute | solution.py:19

commit v3 on v2

--- a/solution.py
+++ b/solution.py
@@ -87,15 +87,14 @@
         return jnp.int32(index), live > 0, group, found
 
 
-def pick_ainv(ainv, u_inv, structure, own_k, rows):
+def pick_ainv(ainv, structure, own_k, width, rows):
     n_cols = lax.axis_size("pcol")
-    width = u_inv.shape[-1]
     slots = rows.group_slots
 
-    def kernel(struct_ref, ainv_ref, u_ref, *refs):
-        outs, u_out, sems, u_sem = refs[:n_cols], refs[n_cols], refs[n_cols + 1], refs[n_cols + 2]
+    def kernel(struct_ref, ainv_ref, *refs):
+        outs, sems = refs[:n_cols], refs[n_cols]
         col, row = lax.axis_index("pcol"), lax.axis_index("prow")
-        copies = [pltpu.make_async_copy(u_ref.at[:, pl.ds(col * own_k, own_k)], u_out, u_sem)]
+        copies = []
         for d in range(n_cols):
             for kk in range(own_k):
                 node = (col ^ d) * own_k + kk
@@ -114,20 +113,15 @@
         run_copies(copies)
 
     shape = jax.ShapeDtypeStruct((2, own_k, rows.count * width, slots * width), ainv.dtype)
-    outs = [shape] * n_cols + [jax.ShapeDtypeStruct((2, own_k, width, width), u_inv.dtype)]
-    out = pl.pallas_call(
+    return pl.pallas_call(
         kernel,
         name="pick_ainv",
-        in_specs=[SMEM, ANY, ANY],
-        out_specs=[VMEM] * (n_cols + 1),
-        out_shape=outs,
-        compiler_params=limits(*outs),
-        scratch_shapes=[
-            pltpu.SemaphoreType.DMA((n_cols, own_k, rows.count, slots)),
-            pltpu.SemaphoreType.DMA,
-        ],
-    )(structure, ainv, u_inv)
-    return out[:n_cols], out[n_cols]
+        in_specs=[SMEM, ANY],
+        out_specs=[VMEM] * n_cols,
+        out_shape=[shape] * n_cols,
+        scratch_shapes=[pltpu.SemaphoreType.DMA((n_cols, own_k, rows.count, slots))],
+        compiler_params=limits(*[shape] * n_cols),
+    )(structure, ainv)
 
 
 def dot(left, right):
@@ -138,82 +132,119 @@
     return lax.dot_general(left, right, (((0,), (0,)), ((), ())), preferred_element_type=F32)
 
 
-def solve(structure, own, rest, ainv, u_own, rows):
-    n_rows, n_cols = lax.axis_size("prow"), lax.axis_size("pcol")
-    _, own_k, part, width = own[0].shape[-4:]
-    few = len(own) == n_rows
-    slots = rows.group_slots
+def scale(struct_ref, u_ref, ref, dxs, member, out, at_dx):
+    n_cols = lax.axis_size("pcol")
+    col = lax.axis_index("pcol")
+    _, _, own_k, part, width = ref.shape
+    slots = struct_ref.shape[1] // n_cols
     sub = min(part, width)
+    first = member * part
+    for kk in range(own_k):
+        node = col * own_k + kk
+        u_real, u_imag = u_ref[0, node], u_ref[1, node]
+        real = ref[:, 0, kk].reshape(len(dxs) * part, width)
+        imag = ref[:, 1, kk].reshape(len(dxs) * part, width)
+        s_real = dot(real, u_real) - dot(imag, u_imag)
+        s_imag = dot(real, u_imag) + dot(imag, u_real)
+        for n, dx in enumerate(dxs):
+            for o in range(0, part, sub):
+                live = struct_ref[node, (col ^ dx) * slots + (first + o) // width] >= 0
+                at = pl.ds(pl.multiple_of(first + o, sub), sub)
+                for plane, value in ((0, s_real), (1, s_imag)):
+                    piece = value[n * part + o : n * part + o + sub]
+                    out[plane, kk, dx - at_dx, at, :] = jnp.where(live, piece, 0.0).astype(BF16)
+
+
+def scale_all(struct_ref, u_ref, refs, offsets, dxs, out, at_dx):
+    row = lax.axis_index("prow")
+    if offsets is None:
+
+        @pl.loop(0, lax.axis_size("prow"))
+        def _(member):
+            scale(struct_ref, u_ref, refs[0].at[member], dxs, member, out, at_dx)
+
+    else:
+        for ref, dz in zip(refs, offsets, strict=True):
+            scale(struct_ref, u_ref, ref, dxs, row ^ dz, out, at_dx)
+
+
+def add_products(acc, ainv_ref, scaled, kk, here, at_dx):
+    a_real, a_imag = ainv_ref[0, kk, here, :], ainv_ref[1, kk, here, :]
+    s_real, s_imag = scaled[0, kk, at_dx], scaled[1, kk, at_dx]
+    real, imag = acc
+    real += dot(a_real, s_real) - dot(a_imag, s_imag)
+    imag += dot(a_real, s_imag) + dot(a_imag, s_real)
+    return real, imag
+
+
+def solve_early(structure, u_inv, groups, near, ainv, rows):
+    n_cols = lax.axis_size("pcol")
+    own_k, _, width = groups[0][0][0].shape[-3:]
+    arrays = [a for refs, _, _ in groups for a in refs]
+    length = rows.group_slots * width
+
+    def kernel(struct_ref, u_ref, *refs):
+        group_refs, refs = refs[: len(arrays)], refs[len(arrays) :]
+        ainv_refs, (scaled, acc_ref) = refs[: len(near)], refs[len(near) :]
+        for values, offsets, dxs in groups:
+            scale_all(struct_ref, u_ref, group_refs[: len(values)], offsets, dxs, scaled, 0)
+            group_refs = group_refs[len(values) :]
+        for kk in range(own_k):
+            for i in range(rows.count):
+                here = slice(i * width, (i + 1) * width)
+                acc = jnp.zeros((width, width), F32), jnp.zeros((width, width), F32)
+                for ref, dx in zip(ainv_refs, near, strict=True):
+                    acc = add_products(acc, ref, scaled, kk, here, dx)
+                acc_ref[0, kk, here, :], acc_ref[1, kk, here, :] = acc
+
+    outs = [
+        jax.ShapeDtypeStruct((2, own_k, n_cols, length, width), BF16),
+        jax.ShapeDtypeStruct((2, own_k, rows.count * width, width), F32),
+    ]
+    inputs = [u_inv, *arrays, *[ainv[dx] for dx in near]]
+    return pl.pallas_call(
+        kernel,
+        name="solve_early",
+        in_specs=[SMEM] + [VMEM] * len(inputs),
+        out_specs=[VMEM] * 2,
+        out_shape=outs,
+        compiler_params=limits(*outs, *inputs),
+    )(structure, *inputs)
+
+
+def solve_late(structure, u_inv, last, scaled, acc, far, ainv, rows):
+    n_rows = lax.axis_size("prow")
+    _, own_k, _, width = acc.shape
+    values, offsets, dxs = last
+    few = offsets is not None
     band = width // n_rows
 
-    def kernel(struct_ref, u_ref, *refs):
-        own_refs, refs = refs[: len(own)], refs[len(own) :]
-        rest_refs, refs = refs[: len(rest)], refs[len(rest) :]
-        ainv_refs, refs = refs[:n_cols], refs[n_cols:]
+    def kernel(struct_ref, u_ref, scaled_ref, acc_ref, *refs):
+        last_refs, refs = refs[: len(values)], refs[len(values) :]
+        ainv_refs, refs = refs[: len(far)], refs[len(far) :]
         sel_ref, *q_refs, scaled, quad = refs
         col, row = lax.axis_index("pcol"), lax.axis_index("prow")
-        if rows.by_slot:
-            sel_ref[...] = jnp.zeros_like(sel_ref)
+        scaled[...] = scaled_ref[:, :, far[0] :]
+        scale_all(struct_ref, u_ref, last_refs, offsets, dxs, scaled, far[0])
         for kk in range(own_k):
             node = col * own_k + kk
-            u_real, u_imag = u_ref[0, kk], u_ref[1, kk]
-
-            def scale(own_ref, rest_ref, member, node=node, kk=kk, u_real=u_real, u_imag=u_imag):
-                first = member * part
-                for real, imag, dxs in (
-                    (own_ref[0, kk], own_ref[1, kk], (0,)),
-                    (
-                        rest_ref[:, 0, kk].reshape((n_cols - 1) * part, width),
-                        rest_ref[:, 1, kk].reshape((n_cols - 1) * part, width),
-                        tuple(range(1, n_cols)),
-                    ),
-                ):
-                    s_real = dot(real, u_real) - dot(imag, u_imag)
-                    s_imag = dot(real, u_imag) + dot(imag, u_real)
-                    for n, dx in enumerate(dxs):
-                        for o in range(0, part, sub):
-                            slot = (first + o) // width
-                            live = struct_ref[node, (col ^ dx) * slots + slot] >= 0
-                            at = pl.ds(pl.multiple_of(first + o, sub), sub)
-                            for plane, value in ((0, s_real), (1, s_imag)):
-                                piece = value[n * part + o : n * part + o + sub]
-                                scaled[plane, kk, dx, at, :] = jnp.where(live, piece, 0.0).astype(BF16)
-
-            if few:
-                for dz in range(n_rows):
-                    scale(own_refs[dz], rest_refs[dz], row ^ dz)
-            else:
-
-                @pl.loop(0, n_rows)
-                def _(i, scale=scale):
-                    scale(own_refs[0].at[i], rest_refs[0].at[i], i)
-
             q_real = jnp.zeros((width, width), F32)
             q_imag = jnp.zeros((width, width), F32)
             for i in range(rows.count):
-                block, live, group, slot = rows.entry(struct_ref, node, row, i)
+                _, live, group, slot = rows.entry(struct_ref, node, row, i)
                 here = slice(i * width, (i + 1) * width)
-                acc_real = jnp.zeros((width, width), F32)
-                acc_imag = jnp.zeros((width, width), F32)
-                for dx in range(n_cols):
-                    a_real, a_imag = ainv_refs[dx][0, kk, here, :], ainv_refs[dx][1, kk, here, :]
-                    s_real, s_imag = scaled[0, kk, dx], scaled[1, kk, dx]
-                    acc_real += dot(a_real, s_real) - dot(a_imag, s_imag)
-                    acc_imag += dot(a_real, s_imag) + dot(a_imag, s_real)
-                sel_real = jnp.where(live, -acc_real, 0.0)
-                sel_imag = jnp.where(live, -acc_imag, 0.0)
-
-                def put(block=block, sel_real=sel_real, sel_imag=sel_imag, kk=kk):
-                    at = pl.ds(pl.multiple_of(block * width, width), width)
-                    sel_ref[0, at, kk * width : (kk + 1) * width] = sel_real
-                    sel_ref[1, at, kk * width : (kk + 1) * width] = sel_imag
-
-                if rows.by_slot:
-                    pl.when(live)(put)
-                else:
-                    put()
+                acc = acc_ref[0, kk, here, :], acc_ref[1, kk, here, :]
+                for ref, dx in zip(ainv_refs, far, strict=True):
+                    acc = add_products(acc, ref, scaled, kk, here, dx - far[0])
+                sel_real = jnp.where(live, -acc[0], 0.0)
+                sel_imag = jnp.where(live, -acc[1], 0.0)
+                sel_ref[0, kk, here, :], sel_ref[1, kk, here, :] = sel_real, sel_imag
                 at = pl.ds(pl.multiple_of(slot * width, width), width)
-                left_real, left_imag = scaled[0, kk, group ^ col, at, :], scaled[1, kk, group ^ col, at, :]
+                dx = group ^ col
+                is_far = dx >= far[0]
+                fdx = jnp.where(is_far, dx - far[0], 0)
+                left_real = jnp.where(is_far, scaled[0, kk, fdx, at, :], scaled_ref[0, kk, dx, at, :])
+                left_imag = jnp.where(is_far, scaled[1, kk, fdx, at, :], scaled_ref[1, kk, dx, at, :])
                 hi_real, hi_imag = sel_real.astype(BF16), sel_imag.astype(BF16)
                 lo_real = (sel_real - hi_real.astype(F32)).astype(BF16)
                 lo_imag = (sel_imag - hi_imag.astype(F32)).astype(BF16)
@@ -224,33 +255,64 @@
                 q_real += by_real[:, :width] - by_imag[:, width:]
                 q_imag += by_real[:, width:] + by_imag[:, :width]
             quad[0], quad[1] = q_real, q_imag
-            if few:
-                for dz in range(n_rows):
-                    at = pl.ds(pl.multiple_of((row ^ dz) * band, band), band)
-                    for plane in range(2):
+            for plane in range(2):
+                if few:
+                    for dz in range(n_rows):
+                        at = pl.ds(pl.multiple_of((row ^ dz) * band, band), band)
                         q_refs[dz][plane, kk] = quad[plane, at, :].astype(q_refs[dz].dtype)
-            else:
-                for plane in range(2):
+                else:
                     q_refs[0][plane, kk] = quad[plane].astype(BF16)
 
-    sel = jax.ShapeDtypeStruct((2, rows.row_blocks * width, own_k * width), F32)
     chunk = (2, own_k, band, width)
     if few:
         terms = [jax.ShapeDtypeStruct(chunk, F32)] + [jax.ShapeDtypeStruct(chunk, BF16)] * (n_rows - 1)
     else:
         terms = [jax.ShapeDtypeStruct((2, own_k, width, width), BF16)]
-    scaled = jax.ShapeDtypeStruct((2, own_k, n_cols, slots * width, width), BF16)
+    length = scaled.shape[3]
+    late = jax.ShapeDtypeStruct((2, own_k, len(far), length, width), BF16)
     quad = jax.ShapeDtypeStruct((2, width, width), F32)
+    inputs = [u_inv, scaled, acc, *values, *[ainv[dx] for dx in far]]
     out = pl.pallas_call(
         kernel,
-        name="solve",
-        in_specs=[SMEM] + [VMEM] * (1 + len(own) + len(rest) + n_cols),
+        name="solve_late",
+        in_specs=[SMEM] + [VMEM] * len(inputs),
         out_specs=[VMEM] * (1 + len(terms)),
-        out_shape=[sel] + terms,
-        scratch_shapes=[pltpu.VMEM(scaled.shape, scaled.dtype), pltpu.VMEM(quad.shape, quad.dtype)],
-        compiler_params=limits(sel, *terms, scaled, quad, u_own, *own, *rest, *ainv),
-    )(structure, u_own, *own, *rest, *ainv)
+        out_shape=[acc] + terms,
+        scratch_shapes=[pltpu.VMEM(late.shape, late.dtype), pltpu.VMEM(quad.shape, quad.dtype)],
+        compiler_params=limits(*terms, late, quad, acc, *inputs),
+    )(structure, *inputs)
     return out[0], out[1:]
+
+
+def place(structure, sel, rows):
+    _, own_k, _, width = sel.shape
+
+    def kernel(struct_ref, sel_ref, out_ref):
+        col, row = lax.axis_index("pcol"), lax.axis_index("prow")
+        if rows.by_slot:
+            out_ref[...] = jnp.zeros_like(out_ref)
+        for kk in range(own_k):
+            for i in range(rows.count):
+                block, live, _, _ = rows.entry(struct_ref, col * own_k + kk, row, i)
+
+                def put(block=block, kk=kk, i=i):
+                    at = pl.ds(pl.multiple_of(block * width, width), width)
+                    out_ref[:, at, kk * width : (kk + 1) * width] = sel_ref[:, kk, i * width : (i + 1) * width, :]
+
+                if rows.by_slot:
+                    pl.when(live)(put)
+                else:
+                    put()
+
+    out = jax.ShapeDtypeStruct((2, rows.row_blocks * width, own_k * width), F32)
+    return pl.pallas_call(
+        kernel,
+        name="place",
+        in_specs=[SMEM, VMEM],
+        out_specs=VMEM,
+        out_shape=out,
+        compiler_params=limits(out, sel),
+    )(structure, sel)
 
 
 def finish_band(k_inv, terms):
@@ -296,13 +358,13 @@
 def gather_rows(x):
     n = lax.axis_size("prow")
     if n > FEW:
-        return [lax.all_gather(x, "prow")]
+        return [lax.all_gather(x, "prow")], None
     held = {0: x}
     d = n // 2
     while d:
         held.update({at ^ d: swap(value, "prow", d) for at, value in list(held.items())})
         d //= 2
-    return [held[d] for d in range(n)]
+    return [held[d] for d in range(n)], list(range(n))
 
 
 def local(ainv_anc, panel, u_inv, k_inv, structure):
@@ -311,12 +373,23 @@
     n_rows, n_cols = lax.axis_size("prow"), lax.axis_size("pcol")
     rows = Rows(ainv_anc.shape[1] // width, ainv_anc.shape[2] // width, structure.shape[1] // n_cols)
     parts = pick_panel(panel, own_k)
-    own = gather_rows(parts[0])
-    got = [swap(parts[d], "pcol", d) for d in range(1, n_cols)]
-    rest = gather_rows(jnp.stack(got))
-    blocks, u_own = pick_ainv(ainv_anc, u_inv, structure, own_k, rows)
+    parts = [parts[0]] + [swap(parts[d], "pcol", d) for d in range(1, n_cols)]
+    near, far = list(range(n_cols // 2)), list(range(n_cols // 2, n_cols))
+    groups = []
+    for dxs in [[d] for d in near] + [far]:
+        values = jnp.stack([parts[d] for d in dxs])
+        groups.append((*gather_rows(values), dxs))
+    blocks = pick_ainv(ainv_anc, structure, own_k, width, rows)
     ainv = [blocks[0]] + [swap(blocks[d], "pcol", d) for d in range(1, n_cols)]
-    sel_inv, terms = solve(structure, own, rest, ainv, u_own, rows)
+    values, offsets, dxs = groups.pop()
+    if offsets is None:
+        last = (values, None, dxs)
+    else:
+        groups.append((values[:-1], offsets[:-1], dxs))
+        last = (values[-1:], offsets[-1:], dxs)
+    scaled, acc = solve_early(structure, u_inv, groups, near, ainv, rows)
+    sel, terms = solve_late(structure, u_inv, last, scaled, acc, far, ainv, rows)
+    sel_inv = place(structure, sel, rows)
     if n_rows > FEW:
         total = lax.psum_scatter(terms[0], "prow", scatter_dimension=2, tiled=True)
         mine = finish_band(k_inv, [total])

time: 61.5 us -> 57.9 us (0.941)
  waiting for transfers between devices: 30.8 us -> 21.6 us
  starting transfers between devices: 21.1 us -> 24.9 us
  Pallas kernels: 5.3 us -> 7.46 us
    ppermute x18 -> x21, waiting for transfers between devices: 30.8 us -> 21.6 us  [swap(): return lax.ppermute(x, axis, [(i, i ^ d) for i in range(n)])]
    ppermute x18 -> x21, starting transfers between devices: 21.1 us -> 24.9 us  [swap(): return lax.ppermute(x, axis, [(i, i ^ d) for i in range(n)])]
    pallas_call x2 -> x4, Pallas kernels: 4.23 us -> 6.39 us  [the longest x1 2.11 us: solve_early(): pl.pallas_call(kernel, name='solve_early', in_specs=[SMEM] + [VMEM] * len...]
    unnamed x10 -> x12, local copies, waits for them, and re-layouts: 3.4 us -> 2.95 us
  transfers between devices with their start and end apart: 18 -> 21, of which waited for: 11 -> 7; matrix products, arithmetic and copies ran while one was open for 0% -> 0% of each run, Pallas kernels for 1% -> 8%
where the time goes in v3:
time: 57.9 us; the launch traced here: 57.7 us
  starting transfers between devices  24.9 us (43%)
  waiting for transfers between devices  21.6 us (37%)
  Pallas kernels  7.46 us (13%)
  local copies, waits for them, and re-layouts  2.95 us (5%)
  between operations  0.78 us (1%)
    ppermute x21, starting transfers between devices, swap(): return lax.ppermute(x, axis, [(i, i ^ d) for i in range(n)])  24.9 us
    ppermute x21, waiting for transfers between devices, swap(): return lax.ppermute(x, axis, [(i, i ^ d) for i in range(n)])  21.6 us
    unnamed x12, local copies, waits for them, and re-layouts  2.95 us
    pallas_call x1, Pallas kernels, solve_early(): pl.pallas_call(kernel, name='solve_early', in_specs=[SMEM] + [VMEM] * len...  2.11 us
    pallas_call x1, Pallas kernels, solve_late(): pl.pallas_call(kernel, name='solve_late', in_specs=[SMEM] + [VMEM] * len(...  1.92 us
    pallas_call x1, Pallas kernels, place(): pl.pallas_call(kernel, name='place', in_specs=[SMEM, VMEM], out_specs=VME...  1.64 us
  transfers between devices with their start and end apart: 21, of which 7 were waited for; matrix products, arithmetic and copies ran while one was open for 0% of the time, Pallas kernels for 8%

profile of v3, /device:TPU:0, one launch (start us, length us, event | category | flops | bytes accessed | tf_op | source)
XLA Modules:
  0.0 57.7 jit_solution(4002103306514985783)
XLA Ops:
  0.6 1.0 %copy-done.3 = bf16[2,4,64,256]{3,2,1,0:T(8,128)(2,1)S(1)} copy-done((bf16[2,4,64,256]{3,2,1,0:T(8,128)(2,1)S(1)}, bf16[2,4,64,256]{3,2,1,0:T(8,128)(2,1)}, u32[]{:S(2)}) %copy-start.3) | copy-done | bytes 262168
  1.7 0.2 pick_panel.1
  1.9 3.0 %collective-permute-start.7 = (bf16[2,1,64,256]{3,2,0,1:T(8,128)(2,1)S(1)}, bf16[2,1,64,256]{3,2,0,1:T(8,128)(2,1)S(1)}, u32[]{:S(2)}, u32[]{:S(2)}) collective-permute-start(bf16[2,1,64,256]{3,2,0,1:T(8,128)(2,1)S(1)} %bitcast.15), channel_id=1, source_target_pairs={{0,2},{1,3},{2,0},{3,1},{4,6},{5,7},{6,4},{7,5},{8,10},{9,11},{10,... | collective-permute-start | bytes 196616 | tf_op jit(solution)/shard_map/ppermute | solution.py:19
  4.9 0.0 collective-permute-start.3
  4.9 0.2 collective-permute-start.8
  5.1 3.0 %collective-permute-start.1 = (bf16[1,2,1,64,256]{4,3,2,1,0:T(8,128)(2,1)S(1)}, bf16[1,2,1,64,256]{4,3,2,1,0:T(8,128)(2,1)S(1)}, u32[]{:S(2)}, u32[]{:S(2)}) collective-permute-start(bf16[1,2,1,64,256]{4,3,2,1,0:T(8,128)(2,1)S(1)} %bitcast.7), channel_id=1, source_target_pairs={{0,8},{4,12},{8,0},{12,4},{1,9},{5,13},{9,1},{13,5},{2,10},{6,14},... | collective-permute-start | bytes 196616 | tf_op jit(solution)/shard_map/ppermute | solution.py:19
  8.1 1.6 %collective-permute-start = (bf16[1,2,1,64,256]{4,3,2,1,0:T(8,128)(2,1)S(1)}, bf16[1,2,1,64,256]{4,3,2,1,0:T(8,128)(2,1)S(1)}, u32[]{:S(2)}, u32[]{:S(2)}) collective-permute-start(bf16[1,2,1,64,256]{4,3,2,1,0:T(8,128)(2,1)S(1)} %bitcast.8), channel_id=1, source_target_pairs={{0,4},{4,0},{8,12},{12,8},{1,5},{5,1},{9,13},{13,9},{2,6},{6,2},{1... | collective-permute-start | bytes 196616 | tf_op jit(solution)/shard_map/ppermute | solution.py:19
  9.7 1.2 %copy-done.1 = bf16[2,512,512]{2,1,0:T(8,128)(2,1)S(1)} copy-done((bf16[2,512,512]{2,1,0:T(8,128)(2,1)S(1)}, bf16[2,512,512]{2,1,0:T(8,128)(2,1)}, u32[]{:S(2)}) %copy-start.1) | copy-done | bytes 1048600
  11.0 0.7 %copy-done.4 = s32[4,4]{1,0:T(4,128)S(1)} copy-done((s32[4,4]{1,0:T(4,128)S(1)}, s32[4,4]{1,0:T(4,128)}, u32[]{:S(2)}) %copy-start.4) | copy-done | bytes 88
  11.6 0.7 %pick_ainv.1 = (bf16[2,1,256,256]{3,2,1,0:T(8,128)(2,1)S(1)}, bf16[2,1,256,256]{3,2,1,0:T(8,128)(2,1)S(1)}, bf16[2,1,256,256]{3,2,1,0:T(8,128)(2,1)S(1)}, bf16[2,1,256,256]{3,2,1,0:T(8,128)(2,1)S(1)}) custom-call(s32[4,4]{1,0:T(4,128)S(1)} %copy-done.4, bf16[2,512,512]{2,1,0:T(8,128)(2,1)S(1)} %copy-done.1), custom_call_target="tpu_custom_call" | custom-call | tf_op jit(solution)/shard_map/pick_ainv/pallas_call | solution.py:116
  12.4 0.0 collective-permute-done.7
  12.4 0.1 collective-permute-start.11
  12.5 0.0 collective-permute-done.3
  12.5 0.4 collective-permute-start.5
  12.9 0.0 collective-permute-done.8
  12.9 0.2 collective-permute-start.4
  13.1 0.0 collective-permute-done.1.refs_2_
  13.1 1.8 %collective-permute-start.2 = (bf16[1,2,1,64,256]{4,3,2,1,0:T(8,128)(2,1)S(1)}, bf16[1,2,1,64,256]{4,3,2,1,0:T(8,128)(2,1)S(1)}, u32[]{:S(2)}, u32[]{:S(2)}) collective-permute-start(bf16[1,2,1,64,256]{4,3,2,1,0:T(8,128)(2,1)S(1)} %collective-permute-done.1.refs_2_), channel_id=1, source_target_pairs={{0,4},{4,0},{8,12},{12,8},{1,5},{5,1},{9,13},{13,9},{2,6},{6,2},{1... | collective-permute-start | bytes 196616 | tf_op jit(solution)/shard_map/ppermute | solution.py:19
  14.9 0.0 collective-permute-done.refs_1_
  14.9 0.0 copy-start.5
  14.9 1.6 %collective-permute-start.13 = (bf16[2,1,256,256]{3,2,1,0:T(8,128)(2,1)S(1)}, bf16[2,1,256,256]{3,2,1,0:T(8,128)(2,1)S(1)}, u32[]{:S(2)}, u32[]{:S(2)}) collective-permute-start(bf16[2,1,256,256]{3,2,1,0:T(8,128)(2,1)S(1)} %get-tuple-element.25), channel_id=1, source_target_pairs={{0,2},{1,3},{2,0},{3,1},{4,6},{5,7},{6,4},{7,5},{8,10},{9,11},{10,... | collective-permute-start | bytes 786440 | tf_op jit(solution)/shard_map/ppermute | solution.py:19
  16.5 2.7 %collective-permute-done.5.refs_6_ = bf16[1,2,1,64,256]{4,3,2,1,0:T(8,128)(2,1)S(1)} collective-permute-done((bf16[1,2,1,64,256]{4,3,2,1,0:T(8,128)(2,1)S(1)}, bf16[1,2,1,64,256]{4,3,2,1,0:T(8,128)(2,1)S(1)}, u32[]{:S(2)}, u32[]{:S(2)}) %collective-permute-start.5) | collective-permute-done | bytes 65568 | tf_op jit(solution)/shard_map/ppermute | solution.py:19
  19.2 1.1 %collective-permute-start.14 = (bf16[2,1,256,256]{3,2,1,0:T(8,128)(2,1)S(1)}, bf16[2,1,256,256]{3,2,1,0:T(8,128)(2,1)S(1)}, u32[]{:S(2)}, u32[]{:S(2)}) collective-permute-start(bf16[2,1,256,256]{3,2,1,0:T(8,128)(2,1)S(1)} %get-tuple-element.26), channel_id=1, source_target_pairs={{0,3},{1,2},{2,1},{3,0},{4,7},{5,6},{6,5},{7,4},{8,11},{9,10},{10,... | collective-permute-start | bytes 786440 | tf_op jit(solution)/shard_map/ppermute | solution.py:19
  20.4 0.8 %collective-permute-start.10 = (bf16[2,2,1,64,256]{4,3,2,1,0:T(8,128)(2,1)S(1)}, bf16[2,2,1,64,256]{4,3,2,1,0:T(8,128)(2,1)S(1)}, u32[]{:S(2)}, u32[]{:S(2)}) collective-permute-start(bf16[2,2,1,64,256]{4,3,2,1,0:T(8,128)(2,1)S(1)} %pad_maximum_fusion.refs_8_), channel_id=1, source_target_pairs={{0,8},{4,12},{8,0},{12,4},{1,9},{5,13},{9,1},{13,5},{2,10},{6,14},... | collective-permute-start | bytes 393224 | tf_op jit(solution)/shard_map/ppermute | solution.py:19
  21.1 0.6 %collective-permute-start.9 = (bf16[2,2,1,64,256]{4,3,2,1,0:T(8,128)(2,1)S(1)}, bf16[2,2,1,64,256]{4,3,2,1,0:T(8,128)(2,1)S(1)}, u32[]{:S(2)}, u32[]{:S(2)}) collective-permute-start(bf16[2,2,1,64,256]{4,3,2,1,0:T(8,128)(2,1)S(1)} %pad_maximum_fusion.refs_8_), channel_id=1, source_target_pairs={{0,4},{4,0},{8,12},{12,8},{1,5},{5,1},{9,13},{13,9},{2,6},{6,2},{1... | collective-permute-start | bytes 393224 | tf_op jit(solution)/shard_map/ppermute | solution.py:19
  21.8 6.9 %collective-permute-done.10.refs_10_ = bf16[2,2,1,64,256]{4,3,2,1,0:T(8,128)(2,1)S(1)} collective-permute-done((bf16[2,2,1,64,256]{4,3,2,1,0:T(8,128)(2,1)S(1)}, bf16[2,2,1,64,256]{4,3,2,1,0:T(8,128)(2,1)S(1)}, u32[]{:S(2)}, u32[]{:S(2)}) %collective-permute-start.10) | collective-permute-done | bytes 131104 | tf_op jit(solution)/shard_map/ppermute | solution.py:19
  28.7 0.0 collective-permute-start.12
  28.7 0.5 collective-permute-done.9.refs_9_
  29.1 1.6 %collective-permute-start.6 = (bf16[1,2,1,64,256]{4,3,2,1,0:T(8,128)(2,1)S(1)}, bf16[1,2,1,64,256]{4,3,2,1,0:T(8,128)(2,1)S(1)}, u32[]{:S(2)}, u32[]{:S(2)}) collective-permute-start(bf16[1,2,1,64,256]{4,3,2,1,0:T(8,128)(2,1)S(1)} %collective-permute-done.5.refs_6_), channel_id=1, source_target_pairs={{0,4},{4,0},{8,12},{12,8},{1,5},{5,1},{9,13},{13,9},{2,6},{6,2},{1... | collective-permute-start | bytes 196616 | tf_op jit(solution)/shard_map/ppermute | solution.py:19
  30.7 4.8 %collective-permute-done.6.refs_7_ = bf16[1,2,1,64,256]{4,3,2,1,0:T(8,128)(2,1)S(1)} collective-permute-done((bf16[1,2,1,64,256]{4,3,2,1,0:T(8,128)(2,1)S(1)}, bf16[1,2,1,64,256]{4,3,2,1,0:T(8,128)(2,1)S(1)}, u32[]{:S(2)}, u32[]{:S(2)}) %collective-permute-start.6) | collective-permute-done | bytes 65568 | tf_op jit(solution)/shard_map/ppermute | solution.py:19
  35.5 0.0 collective-permute-done.11.refs_12_
  35.5 2.1 %solve_early.1 = (bf16[2,1,4,256,256]{4,3,2,1,0:T(8,128)(2,1)S(1)}, f32[2,1,256,256]{3,2,1,0:T(8,128)S(1)}) custom-call(s32[4,4]{1,0:T(4,128)S(1)} %copy-done.5, bf16[2,4,256,256]{3,2,1,0:T(8,128)(2,1)S(1)} %copy-done, bf16[1,2,1,64,256]{4,3,2,1,0:T(8,128)(2,1)S(1)} %bitcast.9, bf16[1,2,1,64,256]{4,3,2,1,0:T(8,128)(2,1)S(1)} %collective-permute-done.refs_1_, ...), custom_call_target="tpu_custom_call" | custom-call | tf_op jit(solution)/shard_map/solve_early/pallas_call | solution.py:205
  37.6 0.0 collective-permute-done.14.refs_2_
  37.6 0.0 collective-permute-done.12.refs_0_
  37.6 0.0 copy-start.2
  37.7 1.9 %solve_late.1 = (f32[2,1,256,256]{3,2,1,0:T(8,128)S(1)}, f32[2,1,64,256]{3,2,1,0:T(8,128)S(1)}, bf16[2,1,64,256]{3,2,1,0:T(8,128)(2,1)S(1)}, bf16[2,1,64,256]{3,...) custom-call(s32[4,4]{1,0:T(4,128)S(1)} %copy-done.5, bf16[2,4,256,256]{3,2,1,0:T(8,128)(2,1)S(1)} %copy-done, ...), custom_call_target="tpu_custom_call" | custom-call | tf_op jit(solution)/shard_map/solve_late/pallas_call | solution.py:275
  39.6 0.3 collective-permute-start.15
  39.9 0.6 %collective-permute-start.16 = (bf16[2,1,64,256]{3,2,1,0:T(8,128)(2,1)S(1)}, bf16[2,1,64,256]{3,2,1,0:T(8,128)(2,1)S(1)}, u32[]{:S(2)}, u32[]{:S(2)}) collective-permute-start(bf16[2,1,64,256]{3,2,1,0:T(8,128)(2,1)S(1)} %get-tuple-element.30), channel_id=1, source_target_pairs={{0,8},{4,12},{8,0},{12,4},{1,9},{5,13},{9,1},{13,5},{2,10},{6,14},... | collective-permute-start | bytes 196616 | tf_op jit(solution)/shard_map/ppermute | solution.py:19
  40.5 3.5 %collective-permute-start.17 = (bf16[2,1,64,256]{3,2,1,0:T(8,128)(2,1)S(1)}, bf16[2,1,64,256]{3,2,1,0:T(8,128)(2,1)S(1)}, u32[]{:S(2)}, u32[]{:S(2)}) collective-permute-start(bf16[2,1,64,256]{3,2,1,0:T(8,128)(2,1)S(1)} %get-tuple-element.31), channel_id=1, source_target_pairs={{0,12},{4,8},{8,4},{12,0},{1,13},{5,9},{9,5},{13,1},{2,14},{6,10},... | collective-permute-start | bytes 196616 | tf_op jit(solution)/shard_map/ppermute | solution.py:19
  44.0 3.5 %collective-permute-done.16.refs_2_ = bf16[2,1,64,256]{3,2,1,0:T(8,128)(2,1)S(1)} collective-permute-done((bf16[2,1,64,256]{3,2,1,0:T(8,128)(2,1)S(1)}, bf16[2,1,64,256]{3,2,1,0:T(8,128)(2,1)S(1)}, u32[]{:S(2)}, u32[]{:S(2)}) %collective-permute-start.16) | collective-permute-done | bytes 65568 | tf_op jit(solution)/shard_map/ppermute | solution.py:19
  47.5 0.0 collective-permute-done.17.refs_3_
  47.6 1.3 %collective-permute-start.18 = (bf16[2,1,64,256]{3,2,1,0:T(8,128)(2,1)S(1)}, bf16[2,1,64,256]{3,2,1,0:T(8,128)(2,1)S(1)}, u32[]{:S(2)}, u32[]{:S(2)}) collective-permute-start(bf16[2,1,64,256]{3,2,1,0:T(8,128)(2,1)S(1)} %finish_band.1.refs_0_), channel_id=1, source_target_pairs={{0,4},{4,0},{8,12},{12,8},{1,5},{5,1},{9,13},{13,9},{2,6},{6,2},{1... | collective-permute-start | bytes 196616 | tf_op jit(solution)/shard_map/ppermute | solution.py:19
  48.9 1.9 %collective-permute-start.19 = (bf16[2,1,64,256]{3,2,1,0:T(8,128)(2,1)S(1)}, bf16[2,1,64,256]{3,2,1,0:T(8,128)(2,1)S(1)}, u32[]{:S(2)}, u32[]{:S(2)}) collective-permute-start(bf16[2,1,64,256]{3,2,1,0:T(8,128)(2,1)S(1)} %finish_band.1.refs_0_), channel_id=1, source_target_pairs={{0,8},{4,12},{8,0},{12,4},{1,9},{5,13},{9,1},{13,5},{2,10},{6,14},... | collective-permute-start | bytes 196616 | tf_op jit(solution)/shard_map/ppermute | solution.py:19
  50.8 1.2 %collective-permute-start.20 = (bf16[2,1,64,256]{3,2,1,0:T(8,128)(2,1)S(1)}, bf16[2,1,64,256]{3,2,1,0:T(8,128)(2,1)S(1)}, u32[]{:S(2)}, u32[]{:S(2)}) collective-permute-start(bf16[2,1,64,256]{3,2,1,0:T(8,128)(2,1)S(1)} %finish_band.1.refs_0_), channel_id=1, source_target_pairs={{0,12},{4,8},{8,4},{12,0},{1,13},{5,9},{9,5},{13,1},{2,14},{6,10},... | collective-permute-start | bytes 196616 | tf_op jit(solution)/shard_map/ppermute | solution.py:19
  52.0 1.6 %place.1 = f32[2,512,256]{2,1,0:T(8,128)} custom-call(s32[4,4]{1,0:T(4,128)S(1)} %copy-done.5, f32[2,1,256,256]{3,2,1,0:T(8,128)S(1)} %get-tuple-element.27.sel_ref), custom_call_target="tpu_custom_call" | custom-call | tf_op jit(solution)/shard_map/place/pallas_call | solution.py:308
  53.6 1.3 %collective-permute-done.19.refs_2_ = bf16[2,1,64,256]{3,2,1,0:T(8,128)(2,1)S(1)} collective-permute-done((bf16[2,1,64,256]{3,2,1,0:T(8,128)(2,1)S(1)}, bf16[2,1,64,256]{3,2,1,0:T(8,128)(2,1)S(1)}, u32[]{:S(2)}, u32[]{:S(2)}) %collective-permute-start.19) | collective-permute-done | bytes 65568 | tf_op jit(solution)/shard_map/ppermute | solution.py:19
  54.9 1.9 %collective-permute-done.20.refs_3_ = bf16[2,1,64,256]{3,2,1,0:T(8,128)(2,1)S(1)} collective-permute-done((bf16[2,1,64,256]{3,2,1,0:T(8,128)(2,1)S(1)}, bf16[2,1,64,256]{3,2,1,0:T(8,128)(2,1)S(1)}, u32[]{:S(2)}, u32[]{:S(2)}) %collective-permute-start.20) | collective-permute-done | bytes 65568 | tf_op jit(solution)/shard_map/ppermute | solution.py:19
  56.8 0.8 %join_bands.1 = f32[2,1,256,256]{3,2,1,0:T(8,128)} custom-call(bf16[2,1,64,256]{3,2,1,0:T(8,128)(2,1)S(1)} %finish_band.1.refs_0_, bf16[2,1,64,256]{3,2,1,0:T(8,128)(2,1)S(1)} %collective-permute-done.18.refs_1_, bf16[2,1,64,256]{3,2,1,0:T(8,128)(2,1)S(1)} %collective-permute-done.19.refs_2_, bf16[2,1,64,256]{3,2,1,0:T(8,128)(2,1)S(1)} %collective-permute-done.20.refs_3_), custom_call_target="tpu_custom_call" | custom-call | tf_op jit(solution)/shard_map/join_bands/pallas_call | solution.py:348
  (14 shorter events, 0.1 us)
Async XLA Ops:
  0.6 34.9 %copy-start = (bf16[2,4,256,256]{3,2,1,0:T(8,128)(2,1)S(1)}, bf16[2,4,256,256]{3,2,1,0:T(8,128)(2,1)}, u32[]{:S(2)}) copy-start(bf16[2,4,256,256]{3,2,1,0:T(8,128)(2,1)} %u_ref.3) | copy-start | bytes 3145732
  0.6 1.0 %copy-start.3 = (bf16[2,4,64,256]{3,2,1,0:T(8,128)(2,1)S(1)}, bf16[2,4,64,256]{3,2,1,0:T(8,128)(2,1)}, u32[]{:S(2)}) copy-start(bf16[2,4,64,256]{3,2,1,0:T(8,128)(2,1)} %panel_ref.1) | copy-start | bytes 786436
  1.9 10.5 %collective-permute-start.7 = (bf16[2,1,64,256]{3,2,0,1:T(8,128)(2,1)S(1)}, bf16[2,1,64,256]{3,2,0,1:T(8,128)(2,1)S(1)}, u32[]{:S(2)}, u32[]{:S(2)}) collective-permute-start(bf16[2,1,64,256]{3,2,0,1:T(8,128)(2,1)S(1)} %bitcast.15), channel_id=1, source_target_pairs={{0,2},{1,3},{2,0},{3,1},{4,6},{5,7},{6,4},{7,5},{8,10},{9,11},{10,... | collective-permute-start | bytes 196616 | tf_op jit(solution)/shard_map/ppermute | solution.py:19
  4.9 7.5 %collective-permute-start.3 = (bf16[2,1,64,256]{3,2,0,1:T(8,128)(2,1)S(1)}, bf16[2,1,64,256]{3,2,0,1:T(8,128)(2,1)S(1)}, u32[]{:S(2)}, u32[]{:S(2)}) collective-permute-start(bf16[2,1,64,256]{3,2,0,1:T(8,128)(2,1)S(1)} %bitcast.14), channel_id=1, source_target_pairs={{0,1},{1,0},{2,3},{3,2},{4,5},{5,4},{6,7},{7,6},{8,9},{9,8},{10,11... | collective-permute-start | bytes 196616 | tf_op jit(solution)/shard_map/ppermute | solution.py:19
  4.9 8.0 %collective-permute-start.8 = (bf16[2,1,64,256]{3,2,0,1:T(8,128)(2,1)S(1)}, bf16[2,1,64,256]{3,2,0,1:T(8,128)(2,1)S(1)}, u32[]{:S(2)}, u32[]{:S(2)}) collective-permute-start(bf16[2,1,64,256]{3,2,0,1:T(8,128)(2,1)S(1)} %bitcast.13), channel_id=1, source_target_pairs={{0,3},{1,2},{2,1},{3,0},{4,7},{5,6},{6,5},{7,4},{8,11},{9,10},{10,... | collective-permute-start | bytes 196616 | tf_op jit(solution)/shard_map/ppermute | solution.py:19
  5.1 8.0 %collective-permute-start.1 = (bf16[1,2,1,64,256]{4,3,2,1,0:T(8,128)(2,1)S(1)}, bf16[1,2,1,64,256]{4,3,2,1,0:T(8,128)(2,1)S(1)}, u32[]{:S(2)}, u32[]{:S(2)}) collective-permute-start(bf16[1,2,1,64,256]{4,3,2,1,0:T(8,128)(2,1)S(1)} %bitcast.7), channel_id=1, source_target_pairs={{0,8},{4,12},{8,0},{12,4},{1,9},{5,13},{9,1},{13,5},{2,10},{6,14},... | collective-permute-start | bytes 196616 | tf_op jit(solution)/shard_map/ppermute | solution.py:19
  8.1 6.8 %collective-permute-start = (bf16[1,2,1,64,256]{4,3,2,1,0:T(8,128)(2,1)S(1)}, bf16[1,2,1,64,256]{4,3,2,1,0:T(8,128)(2,1)S(1)}, u32[]{:S(2)}, u32[]{:S(2)}) collective-permute-start(bf16[1,2,1,64,256]{4,3,2,1,0:T(8,128)(2,1)S(1)} %bitcast.8), channel_id=1, source_target_pairs={{0,4},{4,0},{8,12},{12,8},{1,5},{5,1},{9,13},{13,9},{2,6},{6,2},{1... | collective-permute-start | bytes 196616 | tf_op jit(solution)/shard_map/ppermute | solution.py:19
  9.7 1.2 %copy-start.1 = (bf16[2,512,512]{2,1,0:T(8,128)(2,1)S(1)}, bf16[2,512,512]{2,1,0:T(8,128)(2,1)}, u32[]{:S(2)}) copy-start(bf16[2,512,512]{2,1,0:T(8,128)(2,1)} %ainv_ref.1) | copy-start | bytes 3145732
  11.0 0.7 %copy-start.4 = (s32[4,4]{1,0:T(4,128)S(1)}, s32[4,4]{1,0:T(4,128)}, u32[]{:S(2)}) copy-start(s32[4,4]{1,0:T(4,128)} %struct_ref.7) | copy-start | bytes 196
  12.4 23.1 %collective-permute-start.11 = (bf16[2,1,256,256]{3,2,1,0:T(8,128)(2,1)S(1)}, bf16[2,1,256,256]{3,2,1,0:T(8,128)(2,1)S(1)}, u32[]{:S(2)}, u32[]{:S(2)}) collective-permute-start(bf16[2,1,256,256]{3,2,1,0:T(8,128)(2,1)S(1)} %get-tuple-element.22), channel_id=1, source_target_pairs={{0,1},{1,0},{2,3},{3,2},{4,5},{5,4},{6,7},{7,6},{8,9},{9,8},{10,11... | collective-permute-start | bytes 786440 | tf_op jit(solution)/shard_map/ppermute | solution.py:19
  12.5 6.8 %collective-permute-start.5 = (bf16[1,2,1,64,256]{4,3,2,1,0:T(8,128)(2,1)S(1)}, bf16[1,2,1,64,256]{4,3,2,1,0:T(8,128)(2,1)S(1)}, u32[]{:S(2)}, u32[]{:S(2)}) collective-permute-start(bf16[1,2,1,64,256]{4,3,2,1,0:T(8,128)(2,1)S(1)} %bitcast.10), channel_id=1, source_target_pairs={{0,8},{4,12},{8,0},{12,4},{1,9},{5,13},{9,1},{13,5},{2,10},{6,14},... | collective-permute-start | bytes 196616 | tf_op jit(solution)/shard_map/ppermute | solution.py:19
  12.9 8.2 %collective-permute-start.4 = (bf16[1,2,1,64,256]{4,3,2,1,0:T(8,128)(2,1)S(1)}, bf16[1,2,1,64,256]{4,3,2,1,0:T(8,128)(2,1)S(1)}, u32[]{:S(2)}, u32[]{:S(2)}) collective-permute-start(bf16[1,2,1,64,256]{4,3,2,1,0:T(8,128)(2,1)S(1)} %bitcast.11), channel_id=1, source_target_pairs={{0,4},{4,0},{8,12},{12,8},{1,5},{5,1},{9,13},{13,9},{2,6},{6,2},{1... | collective-permute-start | bytes 196616 | tf_op jit(solution)/shard_map/ppermute | solution.py:19
  13.1 7.3 %collective-permute-start.2 = (bf16[1,2,1,64,256]{4,3,2,1,0:T(8,128)(2,1)S(1)}, bf16[1,2,1,64,256]{4,3,2,1,0:T(8,128)(2,1)S(1)}, u32[]{:S(2)}, u32[]{:S(2)}) collective-permute-start(bf16[1,2,1,64,256]{4,3,2,1,0:T(8,128)(2,1)S(1)} %collective-permute-done.1.refs_2_), channel_id=1, source_target_pairs={{0,4},{4,0},{8,12},{12,8},{1,5},{5,1},{9,13},{13,9},{2,6},{6,2},{1... | collective-permute-start | bytes 196616 | tf_op jit(solution)/shard_map/ppermute | solution.py:19
  14.9 20.6 %copy-start.5 = (s32[4,4]{1,0:T(4,128)S(1)}, s32[4,4]{1,0:T(4,128)}, u32[]{:S(2)}) copy-start(s32[4,4]{1,0:T(4,128)} %struct_ref.7) | copy-start | bytes 196
  14.9 22.7 %collective-permute-start.13 = (bf16[2,1,256,256]{3,2,1,0:T(8,128)(2,1)S(1)}, bf16[2,1,256,256]{3,2,1,0:T(8,128)(2,1)S(1)}, u32[]{:S(2)}, u32[]{:S(2)}) collective-permute-start(bf16[2,1,256,256]{3,2,1,0:T(8,128)(2,1)S(1)} %get-tuple-element.25), channel_id=1, source_target_pairs={{0,2},{1,3},{2,0},{3,1},{4,6},{5,7},{6,4},{7,5},{8,10},{9,11},{10,... | collective-permute-start | bytes 786440 | tf_op jit(solution)/shard_map/ppermute | solution.py:19
  19.2 18.4 %collective-permute-start.14 = (bf16[2,1,256,256]{3,2,1,0:T(8,128)(2,1)S(1)}, bf16[2,1,256,256]{3,2,1,0:T(8,128)(2,1)S(1)}, u32[]{:S(2)}, u32[]{:S(2)}) collective-permute-start(bf16[2,1,256,256]{3,2,1,0:T(8,128)(2,1)S(1)} %get-tuple-element.26), channel_id=1, source_target_pairs={{0,3},{1,2},{2,1},{3,0},{4,7},{5,6},{6,5},{7,4},{8,11},{9,10},{10,... | collective-permute-start | bytes 786440 | tf_op jit(solution)/shard_map/ppermute | solution.py:19
  20.4 8.3 %collective-permute-start.10 = (bf16[2,2,1,64,256]{4,3,2,1,0:T(8,128)(2,1)S(1)}, bf16[2,2,1,64,256]{4,3,2,1,0:T(8,128)(2,1)S(1)}, u32[]{:S(2)}, u32[]{:S(2)}) collective-permute-start(bf16[2,2,1,64,256]{4,3,2,1,0:T(8,128)(2,1)S(1)} %pad_maximum_fusion.refs_8_), channel_id=1, source_target_pairs={{0,8},{4,12},{8,0},{12,4},{1,9},{5,13},{9,1},{13,5},{2,10},{6,14},... | collective-permute-start | bytes 393224 | tf_op jit(solution)/shard_map/ppermute | solution.py:19
  21.1 8.0 %collective-permute-start.9 = (bf16[2,2,1,64,256]{4,3,2,1,0:T(8,128)(2,1)S(1)}, bf16[2,2,1,64,256]{4,3,2,1,0:T(8,128)(2,1)S(1)}, u32[]{:S(2)}, u32[]{:S(2)}) collective-permute-start(bf16[2,2,1,64,256]{4,3,2,1,0:T(8,128)(2,1)S(1)} %pad_maximum_fusion.refs_8_), channel_id=1, source_target_pairs={{0,4},{4,0},{8,12},{12,8},{1,5},{5,1},{9,13},{13,9},{2,6},{6,2},{1... | collective-permute-start | bytes 393224 | tf_op jit(solution)/shard_map/ppermute | solution.py:19
  28.7 9.0 %collective-permute-start.12 = (bf16[2,2,1,64,256]{4,3,2,1,0:T(8,128)(2,1)S(1)}, bf16[2,2,1,64,256]{4,3,2,1,0:T(8,128)(2,1)S(1)}, u32[]{:S(2)}, u32[]{:S(2)}) collective-permute-start(bf16[2,2,1,64,256]{4,3,2,1,0:T(8,128)(2,1)S(1)} %collective-permute-done.10.refs_10_), channel_id=1, source_target_pairs={{0,4},{4,0},{8,12},{12,8},{1,5},{5,1},{9,13},{13,9},{2,6},{6,2},{1... | collective-permute-start | bytes 393224 | tf_op jit(solution)/shard_map/ppermute | solution.py:19
  29.1 6.3 %collective-permute-start.6 = (bf16[1,2,1,64,256]{4,3,2,1,0:T(8,128)(2,1)S(1)}, bf16[1,2,1,64,256]{4,3,2,1,0:T(8,128)(2,1)S(1)}, u32[]{:S(2)}, u32[]{:S(2)}) collective-permute-start(bf16[1,2,1,64,256]{4,3,2,1,0:T(8,128)(2,1)S(1)} %collective-permute-done.5.refs_6_), channel_id=1, source_target_pairs={{0,4},{4,0},{8,12},{12,8},{1,5},{5,1},{9,13},{13,9},{2,6},{6,2},{1... | collective-permute-start | bytes 196616 | tf_op jit(solution)/shard_map/ppermute | solution.py:19
  37.6 9.9 %copy-start.2 = (f32[2,1,256,256]{3,2,1,0:T(8,128)S(1)}, f32[2,1,256,256]{3,2,1,0:T(8,128)}, u32[]{:S(2)}) copy-start(f32[2,1,256,256]{3,2,1,0:T(8,128)} %k_ref.1) | copy-start | bytes 1572868
  39.6 4.5 %collective-permute-start.15 = (bf16[2,1,64,256]{3,2,1,0:T(8,128)(2,1)S(1)}, bf16[2,1,64,256]{3,2,1,0:T(8,128)(2,1)S(1)}, u32[]{:S(2)}, u32[]{:S(2)}) collective-permute-start(bf16[2,1,64,256]{3,2,1,0:T(8,128)(2,1)S(1)} %get-tuple-element.29), channel_id=1, source_target_pairs={{0,4},{4,0},{8,12},{12,8},{1,5},{5,1},{9,13},{13,9},{2,6},{6,2},{1... | collective-permute-start | bytes 196616 | tf_op jit(solution)/shard_map/ppermute | solution.py:19
  39.9 7.6 %collective-permute-start.16 = (bf16[2,1,64,256]{3,2,1,0:T(8,128)(2,1)S(1)}, bf16[2,1,64,256]{3,2,1,0:T(8,128)(2,1)S(1)}, u32[]{:S(2)}, u32[]{:S(2)}) collective-permute-start(bf16[2,1,64,256]{3,2,1,0:T(8,128)(2,1)S(1)} %get-tuple-element.30), channel_id=1, source_target_pairs={{0,8},{4,12},{8,0},{12,4},{1,9},{5,13},{9,1},{13,5},{2,10},{6,14},... | collective-permute-start | bytes 196616 | tf_op jit(solution)/shard_map/ppermute | solution.py:19
  40.5 7.0 %collective-permute-start.17 = (bf16[2,1,64,256]{3,2,1,0:T(8,128)(2,1)S(1)}, bf16[2,1,64,256]{3,2,1,0:T(8,128)(2,1)S(1)}, u32[]{:S(2)}, u32[]{:S(2)}) collective-permute-start(bf16[2,1,64,256]{3,2,1,0:T(8,128)(2,1)S(1)} %get-tuple-element.31), channel_id=1, source_target_pairs={{0,12},{4,8},{8,4},{12,0},{1,13},{5,9},{9,5},{13,1},{2,14},{6,10},... | collective-permute-start | bytes 196616 | tf_op jit(solution)/shard_map/ppermute | solution.py:19
  47.6 6.1 %collective-permute-start.18 = (bf16[2,1,64,256]{3,2,1,0:T(8,128)(2,1)S(1)}, bf16[2,1,64,256]{3,2,1,0:T(8,128)(2,1)S(1)}, u32[]{:S(2)}, u32[]{:S(2)}) collective-permute-start(bf16[2,1,64,256]{3,2,1,0:T(8,128)(2,1)S(1)} %finish_band.1.refs_0_), channel_id=1, source_target_pairs={{0,4},{4,0},{8,12},{12,8},{1,5},{5,1},{9,13},{13,9},{2,6},{6,2},{1... | collective-permute-start | bytes 196616 | tf_op jit(solution)/shard_map/ppermute | solution.py:19
  48.9 6.0 %collective-permute-start.19 = (bf16[2,1,64,256]{3,2,1,0:T(8,128)(2,1)S(1)}, bf16[2,1,64,256]{3,2,1,0:T(8,128)(2,1)S(1)}, u32[]{:S(2)}, u32[]{:S(2)}) collective-permute-start(bf16[2,1,64,256]{3,2,1,0:T(8,128)(2,1)S(1)} %finish_band.1.refs_0_), channel_id=1, source_target_pairs={{0,8},{4,12},{8,0},{12,4},{1,9},{5,13},{9,1},{13,5},{2,10},{6,14},... | collective-permute-start | bytes 196616 | tf_op jit(solution)/shard_map/ppermute | solution.py:19
  50.8 6.1 %collective-permute-start.20 = (bf16[2,1,64,256]{3,2,1,0:T(8,128)(2,1)S(1)}, bf16[2,1,64,256]{3,2,1,0:T(8,128)(2,1)S(1)}, u32[]{:S(2)}, u32[]{:S(2)}) collective-permute-start(bf16[2,1,64,256]{3,2,1,0:T(8,128)(2,1)S(1)} %finish_band.1.refs_0_), channel_id=1, source_target_pairs={{0,12},{4,8},{8,4},{12,0},{1,13},{5,9},{9,5},{13,1},{2,14},{6,10},... | collective-permute-start | bytes 196616 | tf_op jit(solution)/shard_map/ppermute | solution.py:19

commit v4 on v3

v4 whole, which is shorter than its diff:
```python
import jax
import jax.numpy as jnp
from jax import lax
from jax.experimental import pallas as pl
from jax.experimental.pallas import tpu as pltpu
from jax.sharding import PartitionSpec as P

BF16 = jnp.bfloat16
F32 = jnp.float32
NEAR = 1
FEW = 8
HBM = pl.BlockSpec(memory_space=pltpu.HBM)
VMEM = pl.BlockSpec(memory_space=pltpu.VMEM)
SMEM = pl.BlockSpec(memory_space=pltpu.SMEM)


def swap(x, axis, d):
    n = lax.axis_size(axis)
    return lax.ppermute(x, axis, [(i, i ^ d) for i in range(n)])


def nbytes(*arrays):
    return sum(a.size * a.dtype.itemsize for a in arrays)


def limits(*arrays):
    return pltpu.CompilerParams(vmem_limit_bytes=nbytes(*arrays) + (4 << 20))


class Rows:
    def __init__(self, row_blocks, group_blocks, group_slots):
        self.row_blocks, self.group_blocks, self.group_slots = row_blocks, group_blocks, group_slots
        nested = row_blocks % group_blocks == 0 or group_blocks % row_blocks == 0
        slots = max(row_blocks // group_blocks, 1) * group_slots
        self.by_slot = nested and slots < row_blocks
        self.count = slots if self.by_slot else row_blocks

    def slot_of(self, row, index):
        slot = (row * self.row_blocks // self.group_blocks) * self.group_slots + index
        return slot // self.group_slots, slot % self.group_slots

    def entry(self, struct_ref, node, row, index):
        base = row * self.row_blocks
        if self.by_slot:
            slot = (base // self.group_blocks) * self.group_slots + index
            block = struct_ref[node, slot] - base
            live = jnp.logical_and(block >= 0, block < self.row_blocks)
            return jnp.where(live, block, 0), live, slot // self.group_slots, slot % self.group_slots
        target = base + index
        group = target // self.group_blocks
        found, live = jnp.int32(0), jnp.int32(0)
        for s in range(self.group_slots):
            hit = struct_ref[node, group * self.group_slots + s] == target
            found = jnp.where(hit, s, found)
            live = jnp.where(hit, 1, live)
        return jnp.int32(index), live > 0, group, found


def run_copies(copies):
    for copy in copies:
        copy.start()
    for copy in copies:
        copy.wait()


def pick_panel(panel, own_k):
    n_cols = lax.axis_size("pcol")

    def kernel(panel_ref, *refs):
        outs, sems = refs[:-1], refs[-1]
        col = lax.axis_index("pcol")
        sources = [panel_ref.at[:, pl.ds((col ^ d) * own_k, own_k)] for d in range(n_cols)]
        run_copies([pltpu.make_async_copy(sources[d], outs[d], sems.at[d]) for d in range(n_cols)])

    planes, _, part, width = panel.shape
    outs = [jax.ShapeDtypeStruct((planes, own_k, part, width), panel.dtype)] * n_cols
    return pl.pallas_call(
        kernel,
        name="pick_panel",
        in_specs=[HBM],
        out_specs=[VMEM] * n_cols,
        out_shape=outs,
        scratch_shapes=[pltpu.SemaphoreType.DMA((n_cols,))],
        compiler_params=limits(*outs),
    )(pltpu.with_memory_space_constraint(panel, pltpu.HBM))


def pick_ainv(ainv, structure, own_k, width, rows, ds):
    slots = rows.group_slots

    def kernel(struct_ref, ainv_ref, *refs):
        outs, sems = refs[: len(ds)], refs[len(ds)]
        col, row = lax.axis_index("pcol"), lax.axis_index("prow")
        copies = []
        for n, d in enumerate(ds):
            for kk in range(own_k):
                node = (col ^ d) * own_k + kk
                for i in range(rows.count):
                    block, _, _, _ = rows.entry(struct_ref, node, row, i)
                    for s in range(slots):
                        j = struct_ref[node, col * slots + s] - col * rows.group_blocks
                        j = jnp.maximum(j, 0)
                        copies.append(
                            pltpu.make_async_copy(
                                ainv_ref.at[:, pl.ds(block * width, width), pl.ds(j * width, width)],
                                outs[n].at[:, kk, pl.ds(i * width, width), pl.ds(s * width, width)],
                                sems.at[n, kk, i, s],
                            )
                        )
        run_copies(copies)

    outs = [jax.ShapeDtypeStruct((2, own_k, rows.count * width, slots * width), ainv.dtype)] * len(ds)
    return pl.pallas_call(
        kernel,
        name="pick_ainv",
        in_specs=[SMEM, HBM],
        out_specs=[VMEM] * len(ds),
        out_shape=outs,
        scratch_shapes=[pltpu.SemaphoreType.DMA((len(ds), own_k, rows.count, slots))],
        compiler_params=limits(*outs),
    )(structure, pltpu.with_memory_space_constraint(ainv, pltpu.HBM))


def dot(left, right):
    return jnp.dot(left, right, preferred_element_type=F32)


def tdot(left, right):
    return lax.dot_general(left, right, (((0,), (0,)), ((), ())), preferred_element_type=F32)


def scale(is_live, u_ref, ref, dxs, member, out):
    col = lax.axis_index("pcol")
    _, _, own_k, part, width = ref.shape
    sub = min(part, width)
    first = member * part
    for kk in range(own_k):
        u_real, u_imag = u_ref[0, col * own_k + kk], u_ref[1, col * own_k + kk]
        real = ref[:, 0, kk].reshape(len(dxs) * part, width)
        imag = ref[:, 1, kk].reshape(len(dxs) * part, width)
        s_real = dot(real, u_real) - dot(imag, u_imag)
        s_imag = dot(real, u_imag) + dot(imag, u_real)
        for n, dx in enumerate(dxs):
            for o in range(0, part, sub):
                live = is_live(kk, dx, (first + o) // width)
                at = pl.ds(pl.multiple_of(first + o, sub), sub)
                for plane, value in ((0, s_real), (1, s_imag)):
                    piece = value[n * part + o : n * part + o + sub]
                    out(plane, kk, dx)[at, :] = jnp.where(live, piece, 0.0).astype(BF16)


def scale_all(is_live, u_ref, refs, offsets, dxs, out):
    row = lax.axis_index("prow")
    if offsets is None:

        @pl.loop(0, lax.axis_size("prow"))
        def _(member):
            scale(is_live, u_ref, refs[0].at[member], dxs, member, out)

    else:
        for ref, dz in zip(refs, offsets, strict=True):
            scale(is_live, u_ref, ref, dxs, row ^ dz, out)


def take(refs, groups):
    dealt = []
    for values, offsets, dxs in groups:
        dealt.append((refs[: len(values)], offsets, dxs))
        refs = refs[len(values) :]
    return dealt, refs


def add_products(acc, ainv_ref, s_real, s_imag, kk, here):
    a_real, a_imag = ainv_ref[0, kk, here, :], ainv_ref[1, kk, here, :]
    real, imag = acc
    real += dot(a_real, s_real) - dot(a_imag, s_imag)
    imag += dot(a_real, s_imag) + dot(a_imag, s_real)
    return real, imag


def solve_early(structure, u_inv, groups, near, ainv, rows):
    n_cols = lax.axis_size("pcol")
    own_k, _, width = groups[0][0][0].shape[-3:]
    slots = rows.group_slots

    def kernel(struct_ref, u_ref, *refs):
        col, row = lax.axis_index("pcol"), lax.axis_index("prow")
        dealt, refs = take(refs, groups)
        ainv_refs, (scaled, acc_ref, slot_mask, row_mask) = refs[: len(near)], refs[len(near) :]
        for kk in range(own_k):
            node = col * own_k + kk
            for dx in range(n_cols):
                for s in range(slots):
                    live = struct_ref[node, (col ^ dx) * slots + s] >= 0
                    slot_mask[kk, dx, s] = jnp.full((8, width), jnp.where(live, 1.0, 0.0), F32)
            for i in range(rows.count):
                _, live, _, _ = rows.entry(struct_ref, node, row, i)
                row_mask[kk, i] = jnp.full((8, width), jnp.where(live, 1.0, 0.0), F32)

        def is_live(kk, dx, slot):
            return struct_ref[col * own_k + kk, (col ^ dx) * slots + slot] >= 0

        for values, offsets, dxs in dealt:
            scale_all(is_live, u_ref, values, offsets, dxs, lambda plane, kk, dx: scaled.at[plane, kk, dx])
        for kk in range(own_k):
            for i in range(rows.count):
                here = slice(i * width, (i + 1) * width)
                acc = jnp.zeros((width, width), F32), jnp.zeros((width, width), F32)
                for ref, dx in zip(ainv_refs, near, strict=True):
                    acc = add_products(acc, ref, scaled[0, kk, dx], scaled[1, kk, dx], kk, here)
                acc_ref[0, kk, here, :], acc_ref[1, kk, here, :] = acc

    outs = [
        jax.ShapeDtypeStruct((2, own_k, n_cols, slots * width, width), BF16),
        jax.ShapeDtypeStruct((2, own_k, rows.count * width, width), F32),
        jax.ShapeDtypeStruct((own_k, n_cols, slots, 8, width), F32),
        jax.ShapeDtypeStruct((own_k, rows.count, 8, width), F32),
    ]
    inputs = [u_inv, *[a for values, _, _ in groups for a in values], *[ainv[dx] for dx in near]]
    return pl.pallas_call(
        kernel,
        name="solve_early",
        in_specs=[SMEM] + [VMEM] * len(inputs),
        out_specs=[VMEM] * len(outs),
        out_shape=outs,
        compiler_params=limits(*outs, *inputs),
    )(structure, *inputs)


def solve_late(structure, u_inv, groups, early, far, ainv, rows):
    n_rows = lax.axis_size("prow")
    scaled, acc, _, _ = early
    _, own_k, _, width = acc.shape
    few = groups[-1][1] is not None
    band = width // n_rows
    struct = [] if rows.by_slot else [structure]

    def kernel(*refs):
        struct_refs, refs = refs[: len(struct)], refs[len(struct) :]
        (u_ref, scaled_ref, acc_ref, slot_mask, row_mask), refs = refs[:5], refs[5:]
        dealt, refs = take(refs, groups)
        ainv_refs, refs = refs[: len(far)], refs[len(far) :]
        sel_ref, *q_refs, scaled, quad = refs
        col, row = lax.axis_index("pcol"), lax.axis_index("prow")

        def is_live(kk, dx, slot):
            return slot_mask[kk, dx, slot, 0:1, :] > 0.0

        scaled[...] = scaled_ref[...]
        for values, offsets, dxs in dealt:
            scale_all(is_live, u_ref, values, offsets, dxs, lambda plane, kk, dx: scaled.at[plane, kk, dx])
        for kk in range(own_k):
            q_real = jnp.zeros((width, width), F32)
            q_imag = jnp.zeros((width, width), F32)
            for i in range(rows.count):
                if rows.by_slot:
                    group, slot = rows.slot_of(row, i)
                else:
                    _, _, group, slot = rows.entry(struct_refs[0], col * own_k + kk, row, i)
                live = row_mask[kk, i, 0:1, :] > 0.0
                here = slice(i * width, (i + 1) * width)
                acc = acc_ref[0, kk, here, :], acc_ref[1, kk, here, :]
                for ref, dx in zip(ainv_refs, far, strict=True):
                    acc = add_products(acc, ref, scaled[0, kk, dx], scaled[1, kk, dx], kk, here)
                sel_real = jnp.where(live, -acc[0], 0.0)
                sel_imag = jnp.where(live, -acc[1], 0.0)
                sel_ref[0, kk, here, :], sel_ref[1, kk, here, :] = sel_real, sel_imag
                at = pl.ds(pl.multiple_of(slot * width, width), width)
                left_real, left_imag = scaled[0, kk, group ^ col, at, :], scaled[1, kk, group ^ col, at, :]
                hi_real, hi_imag = sel_real.astype(BF16), sel_imag.astype(BF16)
                lo_real = (sel_real - hi_real.astype(F32)).astype(BF16)
                lo_imag = (sel_imag - hi_imag.astype(F32)).astype(BF16)
                right = jnp.concatenate([hi_real, hi_imag, lo_real, lo_imag], axis=1)
                by_real, by_imag = tdot(left_real, right), tdot(left_imag, right)
                by_real = by_real[:, : 2 * width] + by_real[:, 2 * width :]
                by_imag = by_imag[:, : 2 * width] + by_imag[:, 2 * width :]
                q_real += by_real[:, :width] - by_imag[:, width:]
                q_imag += by_real[:, width:] + by_imag[:, :width]
            quad[0], quad[1] = q_real, q_imag
            for plane in range(2):
                if few:
                    for dz in range(n_rows):
                        at = pl.ds(pl.multiple_of((row ^ dz) * band, band), band)
                        q_refs[dz][plane, kk] = quad[plane, at, :].astype(q_refs[dz].dtype)
                else:
                    q_refs[0][plane, kk] = quad[plane].astype(BF16)

    chunk = (2, own_k, band, width)
    if few:
        terms = [jax.ShapeDtypeStruct(chunk, F32)] + [jax.ShapeDtypeStruct(chunk, BF16)] * (n_rows - 1)
    else:
        terms = [jax.ShapeDtypeStruct((2, own_k, width, width), BF16)]
    quad = jax.ShapeDtypeStruct((2, width, width), F32)
    inputs = [u_inv, *early, *[a for values, _, _ in groups for a in values], *[ainv[dx] for dx in far]]
    out = pl.pallas_call(
        kernel,
        name="solve_late",
        in_specs=[SMEM] * len(struct) + [VMEM] * len(inputs),
        out_specs=[VMEM] * (1 + len(terms)),
        out_shape=[acc] + terms,
        scratch_shapes=[pltpu.VMEM(scaled.shape, scaled.dtype), pltpu.VMEM(quad.shape, quad.dtype)],
        compiler_params=limits(*terms, scaled, quad, acc, *inputs),
    )(*struct, *inputs)
    return out[0], out[1:]


def place(structure, sel, rows):
    _, own_k, _, width = sel.shape

    def kernel(struct_ref, sel_ref, out_ref):
        col, row = lax.axis_index("pcol"), lax.axis_index("prow")
        if rows.by_slot:
            out_ref[...] = jnp.zeros_like(out_ref)
        for kk in range(own_k):
            for i in range(rows.count):
                block, live, _, _ = rows.entry(struct_ref, col * own_k + kk, row, i)

                def put(block=block, kk=kk, i=i):
                    at = pl.ds(pl.multiple_of(block * width, width), width)
                    out_ref[:, at, kk * width : (kk + 1) * width] = sel_ref[:, kk, i * width : (i + 1) * width, :]

                if rows.by_slot:
                    pl.when(live)(put)
                else:
                    put()

    out = jax.ShapeDtypeStruct((2, rows.row_blocks * width, own_k * width), F32)
    return pl.pallas_call(
        kernel,
        name="place",
        in_specs=[SMEM, VMEM],
        out_specs=VMEM,
        out_shape=out,
        compiler_params=limits(out, sel),
    )(structure, sel)


def finish_band(k_inv, terms):
    def kernel(k_ref, *refs):
        *term_refs, out_ref = refs
        row = lax.axis_index("prow")
        band = out_ref.shape[2]
        total = term_refs[0][...].astype(F32)
        for ref in term_refs[1:]:
            total += ref[...].astype(F32)
        at = pl.ds(pl.multiple_of(row * band, band), band)
        out_ref[...] = (k_ref[:, :, at, :] - total).astype(BF16)

    return pl.pallas_call(
        kernel,
        name="finish_band",
        in_specs=[VMEM] * (1 + len(terms)),
        out_specs=VMEM,
        out_shape=jax.ShapeDtypeStruct(terms[0].shape, BF16),
        compiler_params=limits(k_inv, *terms),
    )(k_inv, *terms)


def join_bands(bands, shape):
    def kernel(*refs):
        *band_refs, out_ref = refs
        row = lax.axis_index("prow")
        band = band_refs[0].shape[2]
        for d, ref in enumerate(band_refs):
            at = pl.ds(pl.multiple_of((row ^ d) * band, band), band)
            out_ref[:, :, at, :] = ref[...].astype(F32)

    return pl.pallas_call(
        kernel,
        name="join_bands",
        in_specs=[VMEM] * len(bands),
        out_specs=VMEM,
        out_shape=jax.ShapeDtypeStruct(shape, F32),
        compiler_params=limits(jax.ShapeDtypeStruct(shape, F32), *bands),
    )(*bands)


def gather_rows(x, direct):
    n = lax.axis_size("prow")
    if n > FEW:
        return [lax.all_gather(x, "prow")], None
    if direct:
        return [x] + [swap(x, "prow", d) for d in range(1, n)], list(range(n))
    held = {0: x}
    d = n // 2
    while d:
        held.update({at ^ d: swap(value, "prow", d) for at, value in list(held.items())})
        d //= 2
    return [held[d] for d in range(n)], list(range(n))


def groups_of(n_cols):
    half = n_cols // 2
    return [[d] for d in range(half)] + [list(range(half, n_cols))]


def local(ainv_anc, panel, u_inv, k_inv, structure):
    width = u_inv.shape[-1]
    own_k = k_inv.shape[1]
    n_rows, n_cols = lax.axis_size("prow"), lax.axis_size("pcol")
    rows = Rows(ainv_anc.shape[1] // width, ainv_anc.shape[2] // width, structure.shape[1] // n_cols)
    parts = pick_panel(panel, own_k)
    parts = [parts[0]] + [swap(parts[d], "pcol", d) for d in range(1, n_cols)]
    near, far = list(range(NEAR)), list(range(NEAR, n_cols))
    near_a, far_a = list(range(n_cols // 2)), list(range(n_cols // 2, n_cols))
    groups = []
    for dxs in groups_of(n_cols):
        values = jnp.stack([parts[d] for d in dxs])
        groups.append((*gather_rows(values, False), dxs))
    blocks = dict(zip(far_a, pick_ainv(ainv_anc, structure, own_k, width, rows, far_a), strict=True))
    blocks.update(zip(near_a, pick_ainv(ainv_anc, structure, own_k, width, rows, near_a), strict=True))
    ainv = [blocks[0]] + [swap(blocks[d], "pcol", d) for d in range(1, n_cols)]
    early, late = [], []
    for values, offsets, dxs in groups:
        whole = set(dxs) <= set(near)
        if whole or offsets is None:
            (early if whole else late).append((values, offsets, dxs))
        else:
            early.append((values[:-1], offsets[:-1], dxs))
            late.append((values[-1:], offsets[-1:], dxs))
    found = solve_early(structure, u_inv, early, near, ainv, rows)
    sel, terms = solve_late(structure, u_inv, late, found, far, ainv, rows)
    sel_inv = place(structure, sel, rows)
    if n_rows > FEW:
        total = lax.psum_scatter(terms[0], "prow", scatter_dimension=2, tiled=True)
        mine = finish_band(k_inv, [total])
        return sel_inv, lax.all_gather(mine, "prow", axis=2, tiled=True).astype(F32)
    terms = [terms[0]] + [swap(terms[d], "prow", d) for d in range(1, n_rows)]
    mine = finish_band(k_inv, terms)
    bands, _ = gather_rows(mine, True)
    return sel_inv, join_bands(bands, k_inv.shape)


def solution(mesh):
    placed = (
        P(None, ("pole", "prow"), "pcol"),
        P(None, "pole", ("pcol", "prow"), None),
        P(None, "pole", None, None),
        P(None, ("pole", "pcol"), None, None),
        P(),
    )
    return jax.shard_map(
        local,
        mesh=mesh,
        in_specs=placed,
        out_specs=(P(None, ("pole", "prow"), "pcol"), P(None, ("pole", "pcol"), None, None)),
        check_vma=False,
    )
```

time: 57.9 us -> 57.1 us (0.986)
  local copies, waits for them, and re-layouts: 2.95 us -> 0.01 us
  Pallas kernels: 7.46 us -> 10.3 us
    unnamed x12 -> x6, local copies, waits for them, and re-layouts: 2.95 us -> 0.01 us
    pallas_call x2 -> x3, Pallas kernels: 2.64 us -> 4.91 us  [the longest x2 3.3 us: pick_ainv(): pl.pallas_call(kernel, name='pick_ainv', in_specs=[SMEM, HBM], out_specs=...]
    pallas_call x1, Pallas kernels: 0.19 us -> 0.98 us  [pick_panel(): pl.pallas_call(kernel, name='pick_panel', in_specs=[HBM], out_specs=[VMEM...]
  transfers between devices with their start and end apart: 21 -> 21, of which waited for: 7 -> 9; matrix products, arithmetic and copies ran while one was open for 0% -> 0% of each run, Pallas kernels for 8% -> 12%
where the time goes in v4:
time: 57.1 us; the launch traced here: 56.9 us
  starting transfers between devices  24.7 us (43%)
  waiting for transfers between devices  21.2 us (37%)
  Pallas kernels  10.3 us (18%)
  between operations  0.75 us (1%)
    ppermute x21, starting transfers between devices, swap(): return lax.ppermute(x, axis, [(i, i ^ d) for i in range(n)])  24.7 us
    ppermute x21, waiting for transfers between devices, swap(): return lax.ppermute(x, axis, [(i, i ^ d) for i in range(n)])  21.2 us
    pallas_call x2, Pallas kernels, pick_ainv(): pl.pallas_call(kernel, name='pick_ainv', in_specs=[SMEM, HBM], out_specs=...  3.3 us
    pallas_call x1, Pallas kernels, solve_early(): pl.pallas_call(kernel, name='solve_early', in_specs=[SMEM] + [VMEM] * len...  1.88 us
    pallas_call x1, Pallas kernels, place(): pl.pallas_call(kernel, name='place', in_specs=[SMEM, VMEM], out_specs=VME...  1.64 us
    pallas_call x1, Pallas kernels, solve_late(): pl.pallas_call(kernel, name='solve_late', in_specs=[SMEM] * len(struct) +...  1.6 us
  transfers between devices with their start and end apart: 21, of which 9 were waited for; matrix products, arithmetic and copies ran while one was open for 0% of the time, Pallas kernels for 12%

profile of v4, /device:TPU:0, one launch (start us, length us, event | category | flops | bytes accessed | tf_op | source)
XLA Modules:
  0.0 56.9 jit_solution(6452009275081216635)
XLA Ops:
  0.6 1.0 %pick_panel.1 = (bf16[2,1,64,256]{3,2,1,0:T(8,128)(2,1)S(1)}, bf16[2,1,64,256]{3,2,1,0:T(8,128)(2,1)S(1)}, bf16[2,1,64,256]{3,2,1,0:T(8,128)(2,1)S(1)}, bf16[2,1,64,256]{3,2,1,0:T(8,128)(2,1)S(1)}) custom-call(bf16[2,4,64,256]{3,2,1,0:T(8,128)(2,1)} %panel_ref.1), custom_call_target="tpu_custom_call" | custom-call | tf_op jit(solution)/shard_map/pick_panel/pallas_call | solution.py:77
  1.6 3.0 %collective-permute-start.6 = (bf16[2,1,64,256]{3,2,0,1:T(8,128)(2,1)S(1)}, bf16[2,1,64,256]{3,2,0,1:T(8,128)(2,1)S(1)}, u32[]{:S(2)}, u32[]{:S(2)}) collective-permute-start(bf16[2,1,64,256]{3,2,0,1:T(8,128)(2,1)S(1)} %bitcast.15), channel_id=1, source_target_pairs={{0,2},{1,3},{2,0},{3,1},{4,6},{5,7},{6,4},{7,5},{8,10},{9,11},{10,... | collective-permute-start | bytes 196616 | tf_op jit(solution)/shard_map/ppermute | solution.py:19
  4.6 0.0 collective-permute-start.3
  4.7 0.2 collective-permute-start.7
  4.8 3.0 %collective-permute-start.1 = (bf16[1,2,1,64,256]{4,3,2,1,0:T(8,128)(2,1)S(1)}, bf16[1,2,1,64,256]{4,3,2,1,0:T(8,128)(2,1)S(1)}, u32[]{:S(2)}, u32[]{:S(2)}) collective-permute-start(bf16[1,2,1,64,256]{4,3,2,1,0:T(8,128)(2,1)S(1)} %bitcast.7), channel_id=1, source_target_pairs={{0,8},{4,12},{8,0},{12,4},{1,9},{5,13},{9,1},{13,5},{2,10},{6,14},... | collective-permute-start | bytes 196616 | tf_op jit(solution)/shard_map/ppermute | solution.py:19
  7.9 1.6 %collective-permute-start = (bf16[1,2,1,64,256]{4,3,2,1,0:T(8,128)(2,1)S(1)}, bf16[1,2,1,64,256]{4,3,2,1,0:T(8,128)(2,1)S(1)}, u32[]{:S(2)}, u32[]{:S(2)}) collective-permute-start(bf16[1,2,1,64,256]{4,3,2,1,0:T(8,128)(2,1)S(1)} %bitcast.8), channel_id=1, source_target_pairs={{0,4},{4,0},{8,12},{12,8},{1,5},{5,1},{9,13},{13,9},{2,6},{6,2},{1... | collective-permute-start | bytes 196616 | tf_op jit(solution)/shard_map/ppermute | solution.py:19
  9.5 1.7 %pick_ainv.2 = (bf16[2,1,256,256]{3,2,1,0:T(8,128)(2,1)S(1)}, bf16[2,1,256,256]{3,2,1,0:T(8,128)(2,1)S(1)}) custom-call(s32[4,4]{1,0:T(4,128)S(1)} %copy-done.2, bf16[2,512,512]{2,1,0:T(8,128)(2,1)} %ainv_ref.3), custom_call_target="tpu_custom_call" | custom-call | tf_op jit(solution)/shard_map/pick_ainv/pallas_call | solution.py:113
  11.1 1.7 %pick_ainv.3 = (bf16[2,1,256,256]{3,2,1,0:T(8,128)(2,1)S(1)}, bf16[2,1,256,256]{3,2,1,0:T(8,128)(2,1)S(1)}) custom-call(s32[4,4]{1,0:T(4,128)S(1)} %copy-done.2, bf16[2,512,512]{2,1,0:T(8,128)(2,1)} %ainv_ref.3), custom_call_target="tpu_custom_call" | custom-call | tf_op jit(solution)/shard_map/pick_ainv/pallas_call | solution.py:113
  12.8 0.0 collective-permute-done.6
  12.8 0.1 collective-permute-start.12
  12.9 0.0 collective-permute-done.3
  12.9 0.4 collective-permute-start.5
  13.3 0.0 collective-permute-done.7
  13.3 0.2 collective-permute-start.4
  13.5 0.0 collective-permute-done.1.refs_2_
  13.5 1.8 %collective-permute-start.2 = (bf16[1,2,1,64,256]{4,3,2,1,0:T(8,128)(2,1)S(1)}, bf16[1,2,1,64,256]{4,3,2,1,0:T(8,128)(2,1)S(1)}, u32[]{:S(2)}, u32[]{:S(2)}) collective-permute-start(bf16[1,2,1,64,256]{4,3,2,1,0:T(8,128)(2,1)S(1)} %collective-permute-done.1.refs_2_), channel_id=1, source_target_pairs={{0,4},{4,0},{8,12},{12,8},{1,5},{5,1},{9,13},{13,9},{2,6},{6,2},{1... | collective-permute-start | bytes 196616 | tf_op jit(solution)/shard_map/ppermute | solution.py:19
  15.3 0.0 collective-permute-done.refs_1_
  15.4 1.6 %collective-permute-start.13 = (bf16[2,1,256,256]{3,2,1,0:T(8,128)(2,1)S(1)}, bf16[2,1,256,256]{3,2,1,0:T(8,128)(2,1)S(1)}, u32[]{:S(2)}, u32[]{:S(2)}) collective-permute-start(bf16[2,1,256,256]{3,2,1,0:T(8,128)(2,1)S(1)} %get-tuple-element.29), channel_id=1, source_target_pairs={{0,2},{1,3},{2,0},{3,1},{4,6},{5,7},{6,4},{7,5},{8,10},{9,11},{10,... | collective-permute-start | bytes 786440 | tf_op jit(solution)/shard_map/ppermute | solution.py:19
  16.9 3.4 %collective-permute-done.2.refs_3_ = bf16[1,2,1,64,256]{4,3,2,1,0:T(8,128)(2,1)S(1)} collective-permute-done((bf16[1,2,1,64,256]{4,3,2,1,0:T(8,128)(2,1)S(1)}, bf16[1,2,1,64,256]{4,3,2,1,0:T(8,128)(2,1)S(1)}, u32[]{:S(2)}, u32[]{:S(2)}) %collective-permute-start.2) | collective-permute-done | bytes 65568 | tf_op jit(solution)/shard_map/ppermute | solution.py:19
  20.3 0.0 collective-permute-start.14
  20.3 0.0 collective-permute-done.5.refs_6_
  20.3 1.8 %collective-permute-start.9 = (bf16[2,2,1,64,256]{4,3,2,1,0:T(8,128)(2,1)S(1)}, bf16[2,2,1,64,256]{4,3,2,1,0:T(8,128)(2,1)S(1)}, u32[]{:S(2)}, u32[]{:S(2)}) collective-permute-start(bf16[2,2,1,64,256]{4,3,2,1,0:T(8,128)(2,1)S(1)} %pad_maximum_fusion.refs_7_), channel_id=1, source_target_pairs={{0,8},{4,12},{8,0},{12,4},{1,9},{5,13},{9,1},{13,5},{2,10},{6,14},... | collective-permute-start | bytes 393224 | tf_op jit(solution)/shard_map/ppermute | solution.py:19
  22.0 0.0 collective-permute-done.4.refs_5_
  22.0 0.7 %collective-permute-start.8 = (bf16[2,2,1,64,256]{4,3,2,1,0:T(8,128)(2,1)S(1)}, bf16[2,2,1,64,256]{4,3,2,1,0:T(8,128)(2,1)S(1)}, u32[]{:S(2)}, u32[]{:S(2)}) collective-permute-start(bf16[2,2,1,64,256]{4,3,2,1,0:T(8,128)(2,1)S(1)} %pad_maximum_fusion.refs_7_), channel_id=1, source_target_pairs={{0,4},{4,0},{8,12},{12,8},{1,5},{5,1},{9,13},{13,9},{2,6},{6,2},{1... | collective-permute-start | bytes 393224 | tf_op jit(solution)/shard_map/ppermute | solution.py:19
  22.8 7.3 %collective-permute-done.9.refs_9_ = bf16[2,2,1,64,256]{4,3,2,1,0:T(8,128)(2,1)S(1)} collective-permute-done((bf16[2,2,1,64,256]{4,3,2,1,0:T(8,128)(2,1)S(1)}, bf16[2,2,1,64,256]{4,3,2,1,0:T(8,128)(2,1)S(1)}, u32[]{:S(2)}, u32[]{:S(2)}) %collective-permute-start.9) | collective-permute-done | bytes 131104 | tf_op jit(solution)/shard_map/ppermute | solution.py:19
  30.0 0.0 collective-permute-start.11
  30.0 0.6 %collective-permute-done.8.refs_8_ = bf16[2,2,1,64,256]{4,3,2,1,0:T(8,128)(2,1)S(1)} collective-permute-done((bf16[2,2,1,64,256]{4,3,2,1,0:T(8,128)(2,1)S(1)}, bf16[2,2,1,64,256]{4,3,2,1,0:T(8,128)(2,1)S(1)}, u32[]{:S(2)}, u32[]{:S(2)}) %collective-permute-start.8) | collective-permute-done | bytes 131104 | tf_op jit(solution)/shard_map/ppermute | solution.py:19
  30.7 1.4 %collective-permute-start.10 = (bf16[1,2,1,64,256]{4,3,2,1,0:T(8,128)(2,1)S(1)}, bf16[1,2,1,64,256]{4,3,2,1,0:T(8,128)(2,1)S(1)}, u32[]{:S(2)}, u32[]{:S(2)}) collective-permute-start(bf16[1,2,1,64,256]{4,3,2,1,0:T(8,128)(2,1)S(1)} %collective-permute-done.5.refs_6_), channel_id=1, source_target_pairs={{0,4},{4,0},{8,12},{12,8},{1,5},{5,1},{9,13},{13,9},{2,6},{6,2},{1... | collective-permute-start | bytes 196616 | tf_op jit(solution)/shard_map/ppermute | solution.py:19
  32.1 1.9 %solve_early.1 = (bf16[2,1,4,256,256]{4,3,2,1,0:T(8,128)(2,1)S(1)}, f32[2,1,256,256]{3,2,1,0:T(8,128)S(1)}, f32[1,4,1,8,256]{4,3,2,1,0:T(8,128)S(1)}, f32[1,1,8,256]{3,2,1,0:T(8,128)S(1)}) custom-call(s32[4,4]{1,0:T(4,128)S(1)} %copy-done.2, bf16[2,4,256,256]{3,2,1,0:T(8,128)(2,1)S(1)} %copy-done, bf16[1,2,1,64,256]{4,3,2,1,0:T(8,128)(2,1)S(1)} %bitcast.9, ...), custom_call_target="tpu_custom_call" | custom-call | tf_op jit(solution)/shard_map/solve_early/pallas_call | solution.py:220
  33.9 3.1 %collective-permute-done.10.refs_5_ = bf16[1,2,1,64,256]{4,3,2,1,0:T(8,128)(2,1)S(1)} collective-permute-done((bf16[1,2,1,64,256]{4,3,2,1,0:T(8,128)(2,1)S(1)}, bf16[1,2,1,64,256]{4,3,2,1,0:T(8,128)(2,1)S(1)}, u32[]{:S(2)}, u32[]{:S(2)}) %collective-permute-start.10) | collective-permute-done | bytes 65568 | tf_op jit(solution)/shard_map/ppermute | solution.py:19
  37.1 0.0 collective-permute-done.12.refs_7_
  37.1 0.0 collective-permute-done.13.refs_8_
  37.1 0.0 collective-permute-done.11.refs_6_
  37.1 0.0 copy-start.1
  37.1 1.6 %solve_late.1 = (f32[2,1,256,256]{3,2,1,0:T(8,128)S(1)}, f32[2,1,64,256]{3,2,1,0:T(8,128)S(1)}, bf16[2,1,64,256]{3,2,1,0:T(8,128)(2,1)S(1)}, bf16[2,1,64,256]{3,...) custom-call(bf16[2,4,256,256]{3,2,1,0:T(8,128)(2,1)S(1)} %copy-done, ...), custom_call_target="tpu_custom_call" | custom-call | tf_op jit(solution)/shard_map/solve_late/pallas_call | solution.py:295
  38.7 0.3 collective-permute-start.15
  39.1 2.3 %collective-permute-start.16 = (bf16[2,1,64,256]{3,2,1,0:T(8,128)(2,1)S(1)}, bf16[2,1,64,256]{3,2,1,0:T(8,128)(2,1)S(1)}, u32[]{:S(2)}, u32[]{:S(2)}) collective-permute-start(bf16[2,1,64,256]{3,2,1,0:T(8,128)(2,1)S(1)} %get-tuple-element.34), channel_id=1, source_target_pairs={{0,8},{4,12},{8,0},{12,4},{1,9},{5,13},{9,1},{13,5},{2,10},{6,14},... | collective-permute-start | bytes 196616 | tf_op jit(solution)/shard_map/ppermute | solution.py:19
  41.4 1.8 %collective-permute-start.17 = (bf16[2,1,64,256]{3,2,1,0:T(8,128)(2,1)S(1)}, bf16[2,1,64,256]{3,2,1,0:T(8,128)(2,1)S(1)}, u32[]{:S(2)}, u32[]{:S(2)}) collective-permute-start(bf16[2,1,64,256]{3,2,1,0:T(8,128)(2,1)S(1)} %get-tuple-element.35), channel_id=1, source_target_pairs={{0,12},{4,8},{8,4},{12,0},{1,13},{5,9},{9,5},{13,1},{2,14},{6,10},... | collective-permute-start | bytes 196616 | tf_op jit(solution)/shard_map/ppermute | solution.py:19
  43.2 0.2 collective-permute-done.15.refs_1_
  43.4 2.8 %collective-permute-done.16.refs_2_ = bf16[2,1,64,256]{3,2,1,0:T(8,128)(2,1)S(1)} collective-permute-done((bf16[2,1,64,256]{3,2,1,0:T(8,128)(2,1)S(1)}, bf16[2,1,64,256]{3,2,1,0:T(8,128)(2,1)S(1)}, u32[]{:S(2)}, u32[]{:S(2)}) %collective-permute-start.16) | collective-permute-done | bytes 65568 | tf_op jit(solution)/shard_map/ppermute | solution.py:19
  46.2 1.4 %collective-permute-done.17.refs_3_ = bf16[2,1,64,256]{3,2,1,0:T(8,128)(2,1)S(1)} collective-permute-done((bf16[2,1,64,256]{3,2,1,0:T(8,128)(2,1)S(1)}, bf16[2,1,64,256]{3,2,1,0:T(8,128)(2,1)S(1)}, u32[]{:S(2)}, u32[]{:S(2)}) %collective-permute-start.17) | collective-permute-done | bytes 65568 | tf_op jit(solution)/shard_map/ppermute | solution.py:19
  47.6 0.7 %collective-permute-start.18 = (bf16[2,1,64,256]{3,2,1,0:T(8,128)(2,1)S(1)}, bf16[2,1,64,256]{3,2,1,0:T(8,128)(2,1)S(1)}, u32[]{:S(2)}, u32[]{:S(2)}) collective-permute-start(bf16[2,1,64,256]{3,2,1,0:T(8,128)(2,1)S(1)} %finish_band.1.refs_0_), channel_id=1, source_target_pairs={{0,4},{4,0},{8,12},{12,8},{1,5},{5,1},{9,13},{13,9},{2,6},{6,2},{1... | collective-permute-start | bytes 196616 | tf_op jit(solution)/shard_map/ppermute | solution.py:19
  48.3 1.8 %collective-permute-start.19 = (bf16[2,1,64,256]{3,2,1,0:T(8,128)(2,1)S(1)}, bf16[2,1,64,256]{3,2,1,0:T(8,128)(2,1)S(1)}, u32[]{:S(2)}, u32[]{:S(2)}) collective-permute-start(bf16[2,1,64,256]{3,2,1,0:T(8,128)(2,1)S(1)} %finish_band.1.refs_0_), channel_id=1, source_target_pairs={{0,8},{4,12},{8,0},{12,4},{1,9},{5,13},{9,1},{13,5},{2,10},{6,14},... | collective-permute-start | bytes 196616 | tf_op jit(solution)/shard_map/ppermute | solution.py:19
  50.0 2.0 %collective-permute-start.20 = (bf16[2,1,64,256]{3,2,1,0:T(8,128)(2,1)S(1)}, bf16[2,1,64,256]{3,2,1,0:T(8,128)(2,1)S(1)}, u32[]{:S(2)}, u32[]{:S(2)}) collective-permute-start(bf16[2,1,64,256]{3,2,1,0:T(8,128)(2,1)S(1)} %finish_band.1.refs_0_), channel_id=1, source_target_pairs={{0,12},{4,8},{8,4},{12,0},{1,13},{5,9},{9,5},{13,1},{2,14},{6,10},... | collective-permute-start | bytes 196616 | tf_op jit(solution)/shard_map/ppermute | solution.py:19
  52.0 1.6 %place.1 = f32[2,512,256]{2,1,0:T(8,128)} custom-call(s32[4,4]{1,0:T(4,128)S(1)} %copy-done.2, f32[2,1,256,256]{3,2,1,0:T(8,128)S(1)} %get-tuple-element.31.sel_ref), custom_call_target="tpu_custom_call" | custom-call | tf_op jit(solution)/shard_map/place/pallas_call | solution.py:328
  53.7 0.7 %collective-permute-done.19.refs_2_ = bf16[2,1,64,256]{3,2,1,0:T(8,128)(2,1)S(1)} collective-permute-done((bf16[2,1,64,256]{3,2,1,0:T(8,128)(2,1)S(1)}, bf16[2,1,64,256]{3,2,1,0:T(8,128)(2,1)S(1)}, u32[]{:S(2)}, u32[]{:S(2)}) %collective-permute-start.19) | collective-permute-done | bytes 65568 | tf_op jit(solution)/shard_map/ppermute | solution.py:19
  54.4 1.7 %collective-permute-done.20.refs_3_ = bf16[2,1,64,256]{3,2,1,0:T(8,128)(2,1)S(1)} collective-permute-done((bf16[2,1,64,256]{3,2,1,0:T(8,128)(2,1)S(1)}, bf16[2,1,64,256]{3,2,1,0:T(8,128)(2,1)S(1)}, u32[]{:S(2)}, u32[]{:S(2)}) %collective-permute-start.20) | collective-permute-done | bytes 65568 | tf_op jit(solution)/shard_map/ppermute | solution.py:19
  56.1 0.8 %join_bands.1 = f32[2,1,256,256]{3,2,1,0:T(8,128)} custom-call(bf16[2,1,64,256]{3,2,1,0:T(8,128)(2,1)S(1)} %finish_band.1.refs_0_, bf16[2,1,64,256]{3,2,1,0:T(8,128)(2,1)S(1)} %collective-permute-done.18.refs_1_, bf16[2,1,64,256]{3,2,1,0:T(8,128)(2,1)S(1)} %collective-permute-done.19.refs_2_, bf16[2,1,64,256]{3,2,1,0:T(8,128)(2,1)S(1)} %collective-permute-done.20.refs_3_), custom_call_target="tpu_custom_call" | custom-call | tf_op jit(solution)/shard_map/join_bands/pallas_call | solution.py:368
  (9 shorter events, 0.1 us)
Async XLA Ops:
  1.6 11.2 %collective-permute-start.6 = (bf16[2,1,64,256]{3,2,0,1:T(8,128)(2,1)S(1)}, bf16[2,1,64,256]{3,2,0,1:T(8,128)(2,1)S(1)}, u32[]{:S(2)}, u32[]{:S(2)}) collective-permute-start(bf16[2,1,64,256]{3,2,0,1:T(8,128)(2,1)S(1)} %bitcast.15), channel_id=1, source_target_pairs={{0,2},{1,3},{2,0},{3,1},{4,6},{5,7},{6,4},{7,5},{8,10},{9,11},{10,... | collective-permute-start | bytes 196616 | tf_op jit(solution)/shard_map/ppermute | solution.py:19
  4.6 8.2 %collective-permute-start.3 = (bf16[2,1,64,256]{3,2,0,1:T(8,128)(2,1)S(1)}, bf16[2,1,64,256]{3,2,0,1:T(8,128)(2,1)S(1)}, u32[]{:S(2)}, u32[]{:S(2)}) collective-permute-start(bf16[2,1,64,256]{3,2,0,1:T(8,128)(2,1)S(1)} %bitcast.14), channel_id=1, source_target_pairs={{0,1},{1,0},{2,3},{3,2},{4,5},{5,4},{6,7},{7,6},{8,9},{9,8},{10,11... | collective-permute-start | bytes 196616 | tf_op jit(solution)/shard_map/ppermute | solution.py:19
  4.7 4.8 %copy-start.2 = (s32[4,4]{1,0:T(4,128)S(1)}, s32[4,4]{1,0:T(4,128)}, u32[]{:S(2)}) copy-start(s32[4,4]{1,0:T(4,128)} %struct_ref.7) | copy-start | bytes 196
  4.7 8.6 %collective-permute-start.7 = (bf16[2,1,64,256]{3,2,0,1:T(8,128)(2,1)S(1)}, bf16[2,1,64,256]{3,2,0,1:T(8,128)(2,1)S(1)}, u32[]{:S(2)}, u32[]{:S(2)}) collective-permute-start(bf16[2,1,64,256]{3,2,0,1:T(8,128)(2,1)S(1)} %bitcast.13), channel_id=1, source_target_pairs={{0,3},{1,2},{2,1},{3,0},{4,7},{5,6},{6,5},{7,4},{8,11},{9,10},{10,... | collective-permute-start | bytes 196616 | tf_op jit(solution)/shard_map/ppermute | solution.py:19
  4.8 27.2 %copy-start = (bf16[2,4,256,256]{3,2,1,0:T(8,128)(2,1)S(1)}, bf16[2,4,256,256]{3,2,1,0:T(8,128)(2,1)}, u32[]{:S(2)}) copy-start(bf16[2,4,256,256]{3,2,1,0:T(8,128)(2,1)} %refs_0_.1) | copy-start | bytes 3145732
  4.8 8.7 %collective-permute-start.1 = (bf16[1,2,1,64,256]{4,3,2,1,0:T(8,128)(2,1)S(1)}, bf16[1,2,1,64,256]{4,3,2,1,0:T(8,128)(2,1)S(1)}, u32[]{:S(2)}, u32[]{:S(2)}) collective-permute-start(bf16[1,2,1,64,256]{4,3,2,1,0:T(8,128)(2,1)S(1)} %bitcast.7), channel_id=1, source_target_pairs={{0,8},{4,12},{8,0},{12,4},{1,9},{5,13},{9,1},{13,5},{2,10},{6,14},... | collective-permute-start | bytes 196616 | tf_op jit(solution)/shard_map/ppermute | solution.py:19
  7.9 7.5 %collective-permute-start = (bf16[1,2,1,64,256]{4,3,2,1,0:T(8,128)(2,1)S(1)}, bf16[1,2,1,64,256]{4,3,2,1,0:T(8,128)(2,1)S(1)}, u32[]{:S(2)}, u32[]{:S(2)}) collective-permute-start(bf16[1,2,1,64,256]{4,3,2,1,0:T(8,128)(2,1)S(1)} %bitcast.8), channel_id=1, source_target_pairs={{0,4},{4,0},{8,12},{12,8},{1,5},{5,1},{9,13},{13,9},{2,6},{6,2},{1... | collective-permute-start | bytes 196616 | tf_op jit(solution)/shard_map/ppermute | solution.py:19
  12.8 24.3 %collective-permute-start.12 = (bf16[2,1,256,256]{3,2,1,0:T(8,128)(2,1)S(1)}, bf16[2,1,256,256]{3,2,1,0:T(8,128)(2,1)S(1)}, u32[]{:S(2)}, u32[]{:S(2)}) collective-permute-start(bf16[2,1,256,256]{3,2,1,0:T(8,128)(2,1)S(1)} %get-tuple-element.28), channel_id=1, source_target_pairs={{0,1},{1,0},{2,3},{3,2},{4,5},{5,4},{6,7},{7,6},{8,9},{9,8},{10,11... | collective-permute-start | bytes 786440 | tf_op jit(solution)/shard_map/ppermute | solution.py:19
  12.9 7.4 %collective-permute-start.5 = (bf16[1,2,1,64,256]{4,3,2,1,0:T(8,128)(2,1)S(1)}, bf16[1,2,1,64,256]{4,3,2,1,0:T(8,128)(2,1)S(1)}, u32[]{:S(2)}, u32[]{:S(2)}) collective-permute-start(bf16[1,2,1,64,256]{4,3,2,1,0:T(8,128)(2,1)S(1)} %bitcast.10), channel_id=1, source_target_pairs={{0,8},{4,12},{8,0},{12,4},{1,9},{5,13},{9,1},{13,5},{2,10},{6,14},... | collective-permute-start | bytes 196616 | tf_op jit(solution)/shard_map/ppermute | solution.py:19
  13.3 8.7 %collective-permute-start.4 = (bf16[1,2,1,64,256]{4,3,2,1,0:T(8,128)(2,1)S(1)}, bf16[1,2,1,64,256]{4,3,2,1,0:T(8,128)(2,1)S(1)}, u32[]{:S(2)}, u32[]{:S(2)}) collective-permute-start(bf16[1,2,1,64,256]{4,3,2,1,0:T(8,128)(2,1)S(1)} %bitcast.11), channel_id=1, source_target_pairs={{0,4},{4,0},{8,12},{12,8},{1,5},{5,1},{9,13},{13,9},{2,6},{6,2},{1... | collective-permute-start | bytes 196616 | tf_op jit(solution)/shard_map/ppermute | solution.py:19
  13.5 6.8 %collective-permute-start.2 = (bf16[1,2,1,64,256]{4,3,2,1,0:T(8,128)(2,1)S(1)}, bf16[1,2,1,64,256]{4,3,2,1,0:T(8,128)(2,1)S(1)}, u32[]{:S(2)}, u32[]{:S(2)}) collective-permute-start(bf16[1,2,1,64,256]{4,3,2,1,0:T(8,128)(2,1)S(1)} %collective-permute-done.1.refs_2_), channel_id=1, source_target_pairs={{0,4},{4,0},{8,12},{12,8},{1,5},{5,1},{9,13},{13,9},{2,6},{6,2},{1... | collective-permute-start | bytes 196616 | tf_op jit(solution)/shard_map/ppermute | solution.py:19
  15.4 21.7 %collective-permute-start.13 = (bf16[2,1,256,256]{3,2,1,0:T(8,128)(2,1)S(1)}, bf16[2,1,256,256]{3,2,1,0:T(8,128)(2,1)S(1)}, u32[]{:S(2)}, u32[]{:S(2)}) collective-permute-start(bf16[2,1,256,256]{3,2,1,0:T(8,128)(2,1)S(1)} %get-tuple-element.29), channel_id=1, source_target_pairs={{0,2},{1,3},{2,0},{3,1},{4,6},{5,7},{6,4},{7,5},{8,10},{9,11},{10,... | collective-permute-start | bytes 786440 | tf_op jit(solution)/shard_map/ppermute | solution.py:19
  20.3 16.8 %collective-permute-start.14 = (bf16[2,1,256,256]{3,2,1,0:T(8,128)(2,1)S(1)}, bf16[2,1,256,256]{3,2,1,0:T(8,128)(2,1)S(1)}, u32[]{:S(2)}, u32[]{:S(2)}) collective-permute-start(bf16[2,1,256,256]{3,2,1,0:T(8,128)(2,1)S(1)} %get-tuple-element.30), channel_id=1, source_target_pairs={{0,3},{1,2},{2,1},{3,0},{4,7},{5,6},{6,5},{7,4},{8,11},{9,10},{10,... | collective-permute-start | bytes 786440 | tf_op jit(solution)/shard_map/ppermute | solution.py:19
  20.3 9.8 %collective-permute-start.9 = (bf16[2,2,1,64,256]{4,3,2,1,0:T(8,128)(2,1)S(1)}, bf16[2,2,1,64,256]{4,3,2,1,0:T(8,128)(2,1)S(1)}, u32[]{:S(2)}, u32[]{:S(2)}) collective-permute-start(bf16[2,2,1,64,256]{4,3,2,1,0:T(8,128)(2,1)S(1)} %pad_maximum_fusion.refs_7_), channel_id=1, source_target_pairs={{0,8},{4,12},{8,0},{12,4},{1,9},{5,13},{9,1},{13,5},{2,10},{6,14},... | collective-permute-start | bytes 393224 | tf_op jit(solution)/shard_map/ppermute | solution.py:19
  22.0 8.6 %collective-permute-start.8 = (bf16[2,2,1,64,256]{4,3,2,1,0:T(8,128)(2,1)S(1)}, bf16[2,2,1,64,256]{4,3,2,1,0:T(8,128)(2,1)S(1)}, u32[]{:S(2)}, u32[]{:S(2)}) collective-permute-start(bf16[2,2,1,64,256]{4,3,2,1,0:T(8,128)(2,1)S(1)} %pad_maximum_fusion.refs_7_), channel_id=1, source_target_pairs={{0,4},{4,0},{8,12},{12,8},{1,5},{5,1},{9,13},{13,9},{2,6},{6,2},{1... | collective-permute-start | bytes 393224 | tf_op jit(solution)/shard_map/ppermute | solution.py:19
  30.0 7.1 %collective-permute-start.11 = (bf16[2,2,1,64,256]{4,3,2,1,0:T(8,128)(2,1)S(1)}, bf16[2,2,1,64,256]{4,3,2,1,0:T(8,128)(2,1)S(1)}, u32[]{:S(2)}, u32[]{:S(2)}) collective-permute-start(bf16[2,2,1,64,256]{4,3,2,1,0:T(8,128)(2,1)S(1)} %collective-permute-done.9.refs_9_), channel_id=1, source_target_pairs={{0,4},{4,0},{8,12},{12,8},{1,5},{5,1},{9,13},{13,9},{2,6},{6,2},{1... | collective-permute-start | bytes 393224 | tf_op jit(solution)/shard_map/ppermute | solution.py:19
  30.7 6.4 %collective-permute-start.10 = (bf16[1,2,1,64,256]{4,3,2,1,0:T(8,128)(2,1)S(1)}, bf16[1,2,1,64,256]{4,3,2,1,0:T(8,128)(2,1)S(1)}, u32[]{:S(2)}, u32[]{:S(2)}) collective-permute-start(bf16[1,2,1,64,256]{4,3,2,1,0:T(8,128)(2,1)S(1)} %collective-permute-done.5.refs_6_), channel_id=1, source_target_pairs={{0,4},{4,0},{8,12},{12,8},{1,5},{5,1},{9,13},{13,9},{2,6},{6,2},{1... | collective-permute-start | bytes 196616 | tf_op jit(solution)/shard_map/ppermute | solution.py:19
  37.1 10.4 %copy-start.1 = (f32[2,1,256,256]{3,2,1,0:T(8,128)S(1)}, f32[2,1,256,256]{3,2,1,0:T(8,128)}, u32[]{:S(2)}) copy-start(f32[2,1,256,256]{3,2,1,0:T(8,128)} %k_ref.1) | copy-start | bytes 1572868
  38.7 4.6 %collective-permute-start.15 = (bf16[2,1,64,256]{3,2,1,0:T(8,128)(2,1)S(1)}, bf16[2,1,64,256]{3,2,1,0:T(8,128)(2,1)S(1)}, u32[]{:S(2)}, u32[]{:S(2)}) collective-permute-start(bf16[2,1,64,256]{3,2,1,0:T(8,128)(2,1)S(1)} %get-tuple-element.33), channel_id=1, source_target_pairs={{0,4},{4,0},{8,12},{12,8},{1,5},{5,1},{9,13},{13,9},{2,6},{6,2},{1... | collective-permute-start | bytes 196616 | tf_op jit(solution)/shard_map/ppermute | solution.py:19
  39.1 7.1 %collective-permute-start.16 = (bf16[2,1,64,256]{3,2,1,0:T(8,128)(2,1)S(1)}, bf16[2,1,64,256]{3,2,1,0:T(8,128)(2,1)S(1)}, u32[]{:S(2)}, u32[]{:S(2)}) collective-permute-start(bf16[2,1,64,256]{3,2,1,0:T(8,128)(2,1)S(1)} %get-tuple-element.34), channel_id=1, source_target_pairs={{0,8},{4,12},{8,0},{12,4},{1,9},{5,13},{9,1},{13,5},{2,10},{6,14},... | collective-permute-start | bytes 196616 | tf_op jit(solution)/shard_map/ppermute | solution.py:19
  41.4 6.2 %collective-permute-start.17 = (bf16[2,1,64,256]{3,2,1,0:T(8,128)(2,1)S(1)}, bf16[2,1,64,256]{3,2,1,0:T(8,128)(2,1)S(1)}, u32[]{:S(2)}, u32[]{:S(2)}) collective-permute-start(bf16[2,1,64,256]{3,2,1,0:T(8,128)(2,1)S(1)} %get-tuple-element.35), channel_id=1, source_target_pairs={{0,12},{4,8},{8,4},{12,0},{1,13},{5,9},{9,5},{13,1},{2,14},{6,10},... | collective-permute-start | bytes 196616 | tf_op jit(solution)/shard_map/ppermute | solution.py:19
  47.6 6.1 %collective-permute-start.18 = (bf16[2,1,64,256]{3,2,1,0:T(8,128)(2,1)S(1)}, bf16[2,1,64,256]{3,2,1,0:T(8,128)(2,1)S(1)}, u32[]{:S(2)}, u32[]{:S(2)}) collective-permute-start(bf16[2,1,64,256]{3,2,1,0:T(8,128)(2,1)S(1)} %finish_band.1.refs_0_), channel_id=1, source_target_pairs={{0,4},{4,0},{8,12},{12,8},{1,5},{5,1},{9,13},{13,9},{2,6},{6,2},{1... | collective-permute-start | bytes 196616 | tf_op jit(solution)/shard_map/ppermute | solution.py:19
  48.3 6.2 %collective-permute-start.19 = (bf16[2,1,64,256]{3,2,1,0:T(8,128)(2,1)S(1)}, bf16[2,1,64,256]{3,2,1,0:T(8,128)(2,1)S(1)}, u32[]{:S(2)}, u32[]{:S(2)}) collective-permute-start(bf16[2,1,64,256]{3,2,1,0:T(8,128)(2,1)S(1)} %finish_band.1.refs_0_), channel_id=1, source_target_pairs={{0,8},{4,12},{8,0},{12,4},{1,9},{5,13},{9,1},{13,5},{2,10},{6,14},... | collective-permute-start | bytes 196616 | tf_op jit(solution)/shard_map/ppermute | solution.py:19
  50.0 6.1 %collective-permute-start.20 = (bf16[2,1,64,256]{3,2,1,0:T(8,128)(2,1)S(1)}, bf16[2,1,64,256]{3,2,1,0:T(8,128)(2,1)S(1)}, u32[]{:S(2)}, u32[]{:S(2)}) collective-permute-start(bf16[2,1,64,256]{3,2,1,0:T(8,128)(2,1)S(1)} %finish_band.1.refs_0_), channel_id=1, source_target_pairs={{0,12},{4,8},{8,4},{12,0},{1,13},{5,9},{9,5},{13,1},{2,14},{6,10},... | collective-permute-start | bytes 196616 | tf_op jit(solution)/shard_map/ppermute | solution.py:19
